TPU v7x, 32 devices: a whole 2x2x4 slice. The times are simulated.
32 devices in a mesh: zg: 4 (over x, core), xy: 8 (over z, y).
Axes of the slice: x: 2, y: 2, z: 4, core: 2. Of those that a mesh axis runs over, the one named last changes fastest.
Arguments:
- dipole_field: bfloat16 [2, 3, 16, 512, 256], P(None, None, 'zg', 'xy'), may hold values from -6 to 6
- material: int32 [16, 512, 2], P('zg', 'xy'), may hold values from 0 to 3
- alpha_table: float32 [4, 2, 3, 3], replicated, may hold values from -3 to 3
- green_spectrum: bfloat16 [2, 6, 32, 1024, 512], P(None, None, 'xy', None, 'zg'), may hold values from -6 to 6
- green_scale: float32 [6, 32], P(None, 'xy'), may hold values from 0.5 to 2
Outputs:
- scattered_field: bfloat16 [2, 3, 16, 512, 256], P(None, None, 'zg', 'xy')
All inputs are finite; a program needn't handle non-finite values.
Results may differ from a plain program's by a relative error of at most 0.019.
Values may be sent and summed in bfloat16 or wider, within the bound.
No kernel may reach another device: no remote copies, remote signals or barrier semaphores. Data moves between devices by JAX's collectives and lax.ppermute only.
A program may use at most 128 MiB of HBM per device.

v0:
```python
import functools
import math

import jax
import jax.numpy as jnp
import numpy as np
from jax import lax
from jax.experimental import pallas as pl
from jax.experimental.pallas import tpu as pltpu
from jax.sharding import PartitionSpec as P

pairing = ((0, 3, 4), (3, 1, 5), (4, 5, 2))

VMEM = pltpu.VMEM
f32 = jnp.float32
bf16 = jnp.bfloat16


def phase(rows, cols, length):
    return (np.outer(rows, cols) % length).astype(np.float64) * (2.0 * math.pi / length)


def table_y(rows_y, length_y, groups):
    ny, nk = rows_y // groups, length_y // groups
    out = np.zeros((groups, groups, 2 * ny, 2 * nk), np.float32)
    for a in range(groups):
        for b in range(groups):
            angle = phase(np.arange(ny) + b * ny, np.arange(nk) + a * nk, length_y)
            cosine, sine = np.cos(angle), -np.sin(angle)
            out[a, b, :ny, :nk] = cosine
            out[a, b, ny:, :nk] = -sine
            out[a, b, :ny, nk:] = sine
            out[a, b, ny:, nk:] = cosine
    return jnp.asarray(out, bf16)


def tables_x(rows_x, length_x):
    half, many = length_x // 2, rows_x // 2
    forward = np.zeros((2, 2 * half, many), np.float32)
    inverse = np.zeros((2, 2 * many, half), np.float32)
    for p in range(2):
        angle = phase(np.arange(half), 2 * np.arange(many) + p, length_x)
        forward[p, :half], forward[p, half:] = np.cos(angle), -np.sin(angle)
        inverse[p, :many], inverse[p, many:] = np.cos(angle).T, np.sin(angle).T
    return jnp.asarray(forward, bf16), jnp.asarray(inverse, bf16)


def parity_order(rows):
    out = np.zeros((rows, rows), np.float32)
    for p in range(2):
        for m in range(rows // 2):
            out[p * (rows // 2) + m, 2 * m + p] = 1.0
    return jnp.asarray(out, bf16)


def swapped(value):
    return pltpu.roll(value, value.shape[-1] // 2, 1)


def times(value, angle, low):
    turn = round(angle / (math.pi / 2.0), 9) % 4
    if turn == 0:
        return value
    if turn == 2:
        return -value
    other = swapped(value)
    if turn in (1, 3):
        s = 1.0 if turn == 1 else -1.0
        return other * jnp.where(low, -s, s)
    c, s = math.cos(angle), math.sin(angle)
    return value * c + other * jnp.where(low, -s, s)


def transform_list(values, sign, low):
    n = len(values)
    if n == 1:
        return values
    even = transform_list(values[0::2], sign, low)
    odd = transform_list(values[1::2], sign, low)
    odd = [times(v, sign * 2.0 * math.pi * k / n, low) for k, v in enumerate(odd)]
    return [e + o for e, o in zip(even, odd)] + [e - o for e, o in zip(even, odd)]


def moments_kernel(where_ref, alpha_ref, field_ref, material_ref, order_ref, *rest, groups, counts):
    outs, scratch = rest[:groups], rest[groups]
    me = where_ref[0]
    _, _, planes, rows, many = field_ref.shape
    blocks = material_ref.shape[2]
    cols = many // blocks
    part = many // groups
    low = lax.broadcasted_iota(jnp.int32, (rows, 2 * part), 1) < part
    for z in range(planes):
        for b in range(blocks):
            mat = jnp.broadcast_to(material_ref[z, :, b : b + 1], (rows, cols))
            masks = [mat == n for n in range(1, counts)]

            def pick(c, i, j):
                value = jnp.full((rows, cols), alpha_ref[((0 * 2 + c) * 3 + i) * 3 + j], f32)
                for n in range(1, counts):
                    value = jnp.where(masks[n - 1], alpha_ref[((n * 2 + c) * 3 + i) * 3 + j], value)
                return value

            reals = [field_ref[0, j, z, :, b * cols : (b + 1) * cols].astype(f32) for j in range(3)]
            imags = [field_ref[1, j, z, :, b * cols : (b + 1) * cols].astype(f32) for j in range(3)]
            for i in range(3):
                re = im = None
                for j in range(3):
                    ar, ai = pick(0, i, j), pick(1, i, j)
                    r = ar * reals[j] - ai * imags[j]
                    m = ar * imags[j] + ai * reals[j]
                    re, im = (r, m) if re is None else (re + r, im + m)
                first = jnp.where(low, re, swapped(im)).astype(bf16)
                second = jnp.where(low, swapped(re), im).astype(bf16)
                for h, v in enumerate((first, second)):
                    v = jnp.dot(order_ref[...], v, preferred_element_type=f32).astype(bf16)
                    scratch[2 * b + h, z, i] = v
    for s in range(groups):
        outs[s][...] = scratch[me ^ s]


def forward_z_kernel(where_ref, *rest, groups, members, held):
    pieces = rest[:groups]
    outs = rest[groups : groups + members * held]
    source, target = rest[groups + members * held :]
    me, at = where_ref[0], where_ref[1]
    planes, comps, rows, lanes = pieces[0].shape
    total = planes * groups
    for s in range(groups):
        source[me ^ s] = pieces[s][...]
    tile = min(16, rows)
    steps = rows // tile
    low = lax.broadcasted_iota(jnp.int32, (tile, lanes), 1) < lanes // 2

    def step(n, carry):
        j = n // steps
        at_row = pl.multiple_of((n % steps) * tile, tile)
        values = [
            source[z // planes, z % planes, j, pl.ds(at_row, tile), :].astype(f32) for z in range(total)
        ]
        even = transform_list(values, -1.0, low)
        for k, v in enumerate(even):
            target[2 * k, j, pl.ds(at_row, tile), :] = v.astype(bf16)
        turned = [times(v, -2.0 * math.pi * z / (2 * total), low) for z, v in enumerate(values)]
        for k, v in enumerate(transform_list(turned, -1.0, low)):
            target[2 * k + 1, j, pl.ds(at_row, tile), :] = v.astype(bf16)
        return carry

    lax.fori_loop(0, comps * steps, step, 0)
    for r in range(held):
        for s in range(members):
            outs[r * members + s][...] = target[(at ^ s) * held + r]


def inverse_z_kernel(where_ref, *rest, groups, members, held):
    pieces = rest[: members * held]
    outs = rest[members * held : members * held + groups]
    source, target = rest[members * held + groups :]
    me, at = where_ref[0], where_ref[1]
    comps, rows, lanes = pieces[0].shape
    total = members * held // 2
    planes = total // groups
    for r in range(held):
        for s in range(members):
            source[(at ^ s) * held + r] = pieces[r * members + s][...]
    tile = min(16, rows)
    steps = rows // tile
    low = lax.broadcasted_iota(jnp.int32, (tile, lanes), 1) < lanes // 2

    def step(n, carry):
        j = n // steps
        at_row = pl.multiple_of((n % steps) * tile, tile)
        values = [source[k, j, pl.ds(at_row, tile), :].astype(f32) for k in range(2 * total)]
        even = transform_list(values[0::2], 1.0, low)
        odd = transform_list(values[1::2], 1.0, low)
        for z in range(total):
            v = even[z] + times(odd[z], 2.0 * math.pi * z / (2 * total), low)
            target[z // planes, z % planes, j, pl.ds(at_row, tile), :] = v.astype(bf16)
        return carry

    lax.fori_loop(0, comps * steps, step, 0)
    for s in range(groups):
        outs[s][...] = target[me ^ s]


def middle_kernel(
    where_ref, scale_ref, tabley_hbm, forward_hbm, inverse_hbm, green_hbm, *rest, plane, groups, members
):
    pieces = rest[:groups]
    outs = rest[groups : 2 * groups]
    tabley, forward, inverse, green, spread, wide, product, sems = rest[2 * groups :]
    me, at = where_ref[0], where_ref[1]
    _, comps, rows, lanes = pieces[0].shape
    half = rows // 2
    copies = [
        pltpu.make_async_copy(tabley_hbm.at[me, me ^ t], tabley.at[pl.ds(t * lanes, lanes)], sems.at[t])
        for t in range(groups)
    ]
    copies.append(pltpu.make_async_copy(forward_hbm, forward, sems.at[groups]))
    copies.append(pltpu.make_async_copy(green_hbm.at[:, :, plane], green, sems.at[groups + 1]))
    copies.append(pltpu.make_async_copy(inverse_hbm, inverse, sems.at[groups + 2]))
    for c in copies:
        c.start()
    for c in copies[:groups]:
        c.wait()
    wave = tabley.shape[1] // 2
    for s in range(members):
        block = jnp.concatenate(
            [pieces[t][s].reshape(comps * rows, lanes) for t in range(groups)], axis=1
        )
        result = jnp.dot(block, tabley[...], preferred_element_type=f32).astype(bf16)
        start = pl.multiple_of((at ^ s) * half, half)
        for j in range(comps):
            for p in range(2):
                spread[j, p, pl.ds(start, half), :] = result[j * rows + p * half : j * rows + (p + 1) * half]
    copies[groups].wait()
    for j in range(comps):
        for p in range(2):
            wide[j, p] = jnp.dot(forward[p], spread[j, p], preferred_element_type=f32)
    copies[groups + 1].wait()
    many = wide.shape[2] // 2
    tile = 16

    def step(n, carry):
        top = pl.multiple_of(n * tile, tile)
        spectra = []
        for j in range(comps):
            re, im = [], []
            for p in range(2):
                c = wide[j, p, pl.ds(top, tile), :]
                s = wide[j, p, pl.ds(many + top, tile), :]
                re.append(c[:, :wave] - s[:, wave:])
                im.append(s[:, :wave] + c[:, wave:])
            spectra.append(((re[0] + re[1], im[0] + im[1]), (re[0] - re[1], im[0] - im[1])))
        totals = []
        for h in range(2):
            weights = [
                tuple(
                    green[c, e, pl.ds(h * many + top, tile), :].astype(f32) * scale_ref[e, plane]
                    for c in range(2)
                )
                for e in range(2 * comps)
            ]
            out = []
            for i in range(comps):
                re = im = None
                for j in range(comps):
                    gr, gi = weights[pairing[i][j]]
                    xr, xi = spectra[j][h]
                    r, m = gr * xr - gi * xi, gr * xi + gi * xr
                    re, im = (r, m) if re is None else (re + r, im + m)
                out.append((re, im))
            totals.append(out)
        for i in range(comps):
            for p in range(2):
                for c in range(2):
                    a, b = totals[0][i][c], totals[1][i][c]
                    product[i, p, pl.ds(top, tile), c * wave : (c + 1) * wave] = (
                        a + b if p == 0 else a - b
                    ).astype(bf16)
        return carry

    lax.fori_loop(0, many // tile, step, 0)
    copies[groups + 2].wait()
    count = inverse.shape[1] // 2
    for i in range(comps):
        for p in range(2):
            both = jnp.dot(inverse[p], product[i, p], preferred_element_type=f32)
            c, s = both[:count], both[count:]
            re = c[:, :wave] - s[:, wave:]
            im = s[:, :wave] + c[:, wave:]
            back = jnp.concatenate([re.astype(bf16), im.astype(bf16)], axis=1)
            share = lax.dot_general(
                back, tabley[...], (((1,), (1,)), ((), ())), preferred_element_type=f32
            ).astype(bf16)
            for b in range(members):
                for t in range(groups):
                    outs[t][at ^ b, i, p * half : (p + 1) * half, :] = share[
                        b * half : (b + 1) * half, t * lanes : (t + 1) * lanes
                    ]


def join_kernel(*refs):
    ins, out = refs[:-1], refs[-1]
    for s, piece in enumerate(ins):
        out[s] = piece[...]


def add_kernel(a, b, out):
    out[...] = (a[...].astype(f32) + b[...].astype(f32)).astype(bf16)


def finish_kernel(a, b, c, *outs):
    for s, out in enumerate(outs):
        out[...] = (a[s].astype(f32) + b[s].astype(f32) + c[s].astype(f32)).astype(bf16)


def result_kernel(where_ref, field_ref, order_ref, *rest, groups, factor):
    pieces, out, scratch = rest[:groups], rest[groups], rest[groups + 1]
    me = where_ref[0]
    _, _, planes, rows, many = field_ref.shape
    part = many // groups
    lanes = 2 * part
    for s in range(groups):
        scratch[me ^ s] = pieces[s][...]
    low = lax.broadcasted_iota(jnp.int32, (rows, lanes), 1) < part
    for z in range(planes):
        for i in range(3):
            for b in range(groups // 2):
                first, second = [
                    lax.dot_general(
                        order_ref[...], scratch[2 * b + h, z, i], (((0,), (0,)), ((), ())),
                        preferred_element_type=f32,
                    )
                    for h in range(2)
                ]
                re = jnp.where(low, first, swapped(second))
                im = jnp.where(low, swapped(first), second)
                for c, v in enumerate((re, im)):
                    field = field_ref[c, i, z, :, b * lanes : (b + 1) * lanes].astype(f32)
                    out[c, i, z, :, b * lanes : (b + 1) * lanes] = (field - v * factor).astype(bf16)


def smem():
    return pl.BlockSpec(memory_space=pltpu.SMEM)


def vmem():
    return pl.BlockSpec(memory_space=pltpu.VMEM)


def hbm():
    return pl.BlockSpec(memory_space=pl.ANY)


def call(kernel, specs, shapes, scratch, flops, args, name):
    many = isinstance(shapes, list)
    return pl.pallas_call(
        kernel,
        in_specs=specs,
        out_specs=[vmem() for _ in shapes] if many else vmem(),
        out_shape=shapes,
        scratch_shapes=scratch,
        compiler_params=pltpu.CompilerParams(vmem_limit_bytes=56 * 1024 * 1024),
        cost_estimate=pl.CostEstimate(flops=int(flops), transcendentals=0, bytes_accessed=1 << 20),
        name=name,
    )(*args)


def on_device(dipole_field, material, alpha_table, green_spectrum, green_scale):
    groups, members = lax.axis_size("zg"), lax.axis_size("xy")
    _, comps, planes, rows, rows_y = dipole_field.shape
    length_y = 2 * rows_y
    rows_x = rows * members
    length_x = 2 * rows_x
    total_z = planes * groups
    length_z = 2 * total_z
    held = length_z // members
    part = rows_y // groups
    lanes = 2 * part
    wave = length_y // groups
    counts = alpha_table.shape[0]
    where = jnp.stack([lax.axis_index("zg"), lax.axis_index("xy")]).astype(jnp.int32)
    tabley = table_y(rows_y, length_y, groups)
    forward, inverse = tables_x(rows_x, length_x)
    order = parity_order(rows)

    def send(value, axis, size, distance):
        return lax.ppermute(value, axis, [(i, i ^ distance) for i in range(size)])

    def exchange(parts, axis):
        return [parts[0]] + [send(parts[s], axis, len(parts), s) for s in range(1, len(parts))]

    def shape(*dims):
        return jax.ShapeDtypeStruct(dims, bf16)

    cycle = 1e6

    parts = call(
        functools.partial(moments_kernel, groups=groups, counts=counts),
        [smem(), smem(), vmem(), vmem(), vmem()],
        [shape(planes, comps, rows, lanes)] * groups,
        [VMEM((groups, planes, comps, rows, lanes), bf16)],
        5e9,
        (where, alpha_table.reshape(-1), dipole_field, material, order),
        "moments",
    )
    parts = exchange(parts, "zg")
    pieces = call(
        functools.partial(forward_z_kernel, groups=groups, members=members, held=held),
        [smem()] + [vmem()] * groups,
        [shape(comps, rows, lanes)] * (members * held),
        [VMEM((groups, planes, comps, rows, lanes), bf16), VMEM((length_z, comps, rows, lanes), bf16)],
        4e9,
        (where, *parts),
        "forward_z",
    )
    full = shape(members, comps, rows, lanes)
    returned = []
    for r in range(held):
        mine = exchange(pieces[r * members : (r + 1) * members], "xy")
        gathered = [call(join_kernel, [vmem()] * members, full, [], 1e9, mine, "join")]
        have = {0: gathered[0]}
        bit = groups // 2
        while bit:
            for t in sorted(have):
                have[t ^ bit] = send(have[t], "zg", groups, bit)
            bit //= 2
        shares = call(
            functools.partial(middle_kernel, plane=r, groups=groups, members=members),
            [smem(), smem(), hbm(), hbm(), hbm(), hbm()] + [vmem()] * groups,
            [full] * groups,
            [
                VMEM((groups * lanes, 2 * wave), bf16),
                VMEM(forward.shape, bf16),
                VMEM(inverse.shape, bf16),
                VMEM((2, 2 * comps, length_x, wave), bf16),
                VMEM((comps, 2, rows_x // 2, 2 * wave), bf16),
                VMEM((comps, 2, length_x, 2 * wave), f32),
                VMEM((comps, 2, length_x // 2, 2 * wave), bf16),
                pltpu.SemaphoreType.DMA((groups + 3,)),
            ],
            8e9,
            (where, green_scale, tabley, forward, inverse, green_spectrum, *[have[t] for t in range(groups)]),
            "middle",
        )
        held_shares = dict(enumerate(shares))
        bit = 1
        while bit < groups // 2:
            moved = {t: send(held_shares[t ^ bit], "zg", groups, bit) for t in held_shares if not t & bit}
            later = {}
            for t in moved:
                if t:
                    later[t] = call(add_kernel, [vmem()] * 2, full, [], 1e9, (held_shares[t], moved[t]), "add")
                else:
                    own = (held_shares[t], moved[t])
            held_shares = later
            bit *= 2
        last = send(held_shares[bit], "zg", groups, bit)
        split = call(
            finish_kernel, [vmem()] * 3, [shape(comps, rows, lanes)] * members, [], 1e9, (*own, last), "finish"
        )
        returned += exchange(split, "xy")
    parts = call(
        functools.partial(inverse_z_kernel, groups=groups, members=members, held=held),
        [smem()] + [vmem()] * (members * held),
        [shape(planes, comps, rows, lanes)] * groups,
        [VMEM((length_z, comps, rows, lanes), bf16), VMEM((groups, planes, comps, rows, lanes), bf16)],
        4e9,
        (where, *returned),
        "inverse_z",
    )
    parts = exchange(parts, "zg")
    return call(
        functools.partial(result_kernel, groups=groups, factor=1.0 / float(length_x * length_y * length_z)),
        [smem(), vmem(), vmem()] + [vmem()] * groups,
        shape(*dipole_field.shape),
        [VMEM((groups, planes, comps, rows, lanes), bf16)],
        3e9,
        (where, dipole_field, order, *parts),
        "result",
    )


def solution(mesh):
    return jax.shard_map(
        on_device,
        mesh=mesh,
        in_specs=(
            P(None, None, "zg", "xy", None),
            P("zg", "xy", None),
            P(),
            P(None, None, "xy", None, "zg"),
            P(None, "xy"),
        ),
        out_specs=P(None, None, "zg", "xy", None),
        check_vma=False,
    )
```

profile of v0, /device:TPU:0, one launch (start us, length us, event | category | flops | bytes accessed | tf_op | source)
XLA Modules:
  0.0 262.2 jit_solution(6473469374198638743)
XLA Ops:
  3.5 3.9 %moments.1 = (bf16[4,3,64,128]{3,2,1,0:T(8,128)(2,1)}, bf16[4,3,64,128]{3,2,1,0:T(8,128)(2,1)}, bf16[4,3,64,128]{3,2,1,0:T(8,128)(2,1)}, bf16[4,3,64,128]{3,2,1,0:T(8,128)(2,1)}) custom-call(s32[2]{0:T(128)} %pad_add_fusion.where_ref, f32[72]{0:T(128)} %reshape.3.alpha_ref, bf16[2,3,4,64,256]{4,3,2,1,0:T(8,128)(2,1)} %field_ref.3, ...), custom_call_target="tpu_custom_call" | custom-call | flops 5000000000 | bytes 1048576 | tf_op jit(solution)/shard_map/moments/pallas_call | solution.py:337
  10.5 5.9 %collective-permute-done.1.rest_2_ = bf16[4,3,64,128]{3,2,1,0:T(8,128)(2,1)S(1)} collective-permute-done((bf16[4,3,64,128]{3,2,1,0:T(8,128)(2,1)}, bf16[4,3,64,128]{3,2,1,0:T(8,128)(2,1)S(1)}, u32[]{:S(2)}, u32[]{:S(2)}) %collective-permute-start.1) | collective-permute-done | bytes 196640 | tf_op jit(solution)/shard_map/ppermute | solution.py:368
  16.4 3.7 %collective-permute-done.2.rest_3_ = bf16[4,3,64,128]{3,2,1,0:T(8,128)(2,1)S(1)} collective-permute-done((bf16[4,3,64,128]{3,2,1,0:T(8,128)(2,1)}, bf16[4,3,64,128]{3,2,1,0:T(8,128)(2,1)S(1)}, u32[]{:S(2)}, u32[]{:S(2)}) %collective-permute-start.2) | collective-permute-done | bytes 196640 | tf_op jit(solution)/shard_map/ppermute | solution.py:368
  20.8 6.3 %forward_z.1 = (bf16[3,64,128]{2,1,0:T(8,128)(2,1)}, bf16[3,64,128]{2,1,0:T(8,128)(2,1)}, bf16[3,64,128]{2,1,0:T(8,128)(2,1)}, bf16[3,64,128]{2,1,0:T(8,128)(2,1...) custom-call(s32[2]{0:T(128)} %pad_add_fusion.where_ref, ...), custom_call_target="tpu_custom_call" | custom-call | flops 4000000000 | bytes 1048576 | tf_op jit(solution)/shard_map/forward_z/pallas_call | solution.py:337
  34.6 3.6 %collective-permute-start.68 = (bf16[3,64,128]{2,1,0:T(8,128)(2,1)}, bf16[3,64,128]{2,1,0:T(8,128)(2,1)S(1)}, u32[]{:S(2)}, u32[]{:S(2)}) collective-permute-start(bf16[3,64,128]{2,1,0:T(8,128)(2,1)} %get-tuple-element.163), channel_id=1, source_target_pairs={{0,6},{1,7},{2,4},{3,5},{4,2},{5,3},{6,0},{7,1},{8,14},{9,15},{10,... | collective-permute-start | bytes 147464 | tf_op jit(solution)/shard_map/ppermute | solution.py:368
  41.3 3.9 %collective-permute-done.69.refs_7_ = bf16[3,64,128]{2,1,0:T(8,128)(2,1)S(1)} collective-permute-done((bf16[3,64,128]{2,1,0:T(8,128)(2,1)}, bf16[3,64,128]{2,1,0:T(8,128)(2,1)S(1)}, u32[]{:S(2)}, u32[]{:S(2)}) %collective-permute-start.69) | collective-permute-done | bytes 49184 | tf_op jit(solution)/shard_map/ppermute | solution.py:368
  49.6 3.0 %collective-permute-start.45 = (bf16[3,64,128]{2,1,0:T(8,128)(2,1)}, bf16[3,64,128]{2,1,0:T(8,128)(2,1)S(1)}, u32[]{:S(2)}, u32[]{:S(2)}) collective-permute-start(bf16[3,64,128]{2,1,0:T(8,128)(2,1)} %get-tuple-element.140), channel_id=1, source_target_pairs={{0,3},{1,2},{2,1},{3,0},{4,7},{5,6},{6,5},{7,4},{8,11},{9,10},{10,... | collective-permute-start | bytes 147464 | tf_op jit(solution)/shard_map/ppermute | solution.py:368
  56.1 4.1 %collective-permute-start.49 = (bf16[3,64,128]{2,1,0:T(8,128)(2,1)}, bf16[3,64,128]{2,1,0:T(8,128)(2,1)S(1)}, u32[]{:S(2)}, u32[]{:S(2)}) collective-permute-start(bf16[3,64,128]{2,1,0:T(8,128)(2,1)} %get-tuple-element.144), channel_id=1, source_target_pairs={{0,7},{1,6},{2,5},{3,4},{4,3},{5,2},{6,1},{7,0},{8,15},{9,14},{10,... | collective-permute-start | bytes 147464 | tf_op jit(solution)/shard_map/ppermute | solution.py:368
  73.1 3.0 %collective-permute-start.24 = (bf16[3,64,128]{2,1,0:T(8,128)(2,1)}, bf16[3,64,128]{2,1,0:T(8,128)(2,1)S(1)}, u32[]{:S(2)}, u32[]{:S(2)}) collective-permute-start(bf16[3,64,128]{2,1,0:T(8,128)(2,1)} %get-tuple-element.119), channel_id=1, source_target_pairs={{0,2},{1,3},{2,0},{3,1},{4,6},{5,7},{6,4},{7,5},{8,10},{9,11},{10,... | collective-permute-start | bytes 147464 | tf_op jit(solution)/shard_map/ppermute | solution.py:368
  83.7 4.1 %collective-permute-start.28 = (bf16[3,64,128]{2,1,0:T(8,128)(2,1)}, bf16[3,64,128]{2,1,0:T(8,128)(2,1)S(1)}, u32[]{:S(2)}, u32[]{:S(2)}) collective-permute-start(bf16[3,64,128]{2,1,0:T(8,128)(2,1)} %get-tuple-element.123), channel_id=1, source_target_pairs={{0,6},{1,7},{2,4},{3,5},{4,2},{5,3},{6,0},{7,1},{8,14},{9,15},{10,... | collective-permute-start | bytes 147464 | tf_op jit(solution)/shard_map/ppermute | solution.py:368
  90.6 3.3 %collective-permute-start.8 = (bf16[3,64,128]{2,1,0:T(8,128)(2,1)}, bf16[3,64,128]{2,1,0:T(8,128)(2,1)S(1)}, u32[]{:S(2)}, u32[]{:S(2)}) collective-permute-start(bf16[3,64,128]{2,1,0:T(8,128)(2,1)} %get-tuple-element.103), channel_id=1, source_target_pairs={{0,6},{1,7},{2,4},{3,5},{4,2},{5,3},{6,0},{7,1},{8,14},{9,15},{10,... | collective-permute-start | bytes 147464 | tf_op jit(solution)/shard_map/ppermute | solution.py:368
  98.8 3.7 %collective-permute-done.9.refs_7_ = bf16[3,64,128]{2,1,0:T(8,128)(2,1)S(1)} collective-permute-done((bf16[3,64,128]{2,1,0:T(8,128)(2,1)}, bf16[3,64,128]{2,1,0:T(8,128)(2,1)S(1)}, u32[]{:S(2)}, u32[]{:S(2)}) %collective-permute-start.9) | collective-permute-done | bytes 49184 | tf_op jit(solution)/shard_map/ppermute | solution.py:368
  107.2 10.2 %middle.7 = (bf16[8,3,64,128]{3,2,1,0:T(8,128)(2,1)}, bf16[8,3,64,128]{3,2,1,0:T(8,128)(2,1)}, bf16[8,3,64,128]{3,2,1,0:T(8,128)(2,1)}, bf16[8,3,64,128]{3,2,1,0:T(8,128)(2,1)}) custom-call(s32[2]{0:T(128)} %pad_add_fusion.where_ref, f32[6,4]{1,0:T(8,128)} %copy.18.scale_ref, bf16[4,4,128,256]{3,2,1,0:T(8,128)(2,1)} %constant.16.clone.tabley_hbm, ...), custom_call_target="tpu_custom_call" | custom-call | flops 8000000000 | bytes 1048576 | tf_op jit(solution)/shard_map/middle/pallas_call | solution.py:337
  119.8 10.5 %middle.6 = (bf16[8,3,64,128]{3,2,1,0:T(8,128)(2,1)}, bf16[8,3,64,128]{3,2,1,0:T(8,128)(2,1)}, bf16[8,3,64,128]{3,2,1,0:T(8,128)(2,1)}, bf16[8,3,64,128]{3,2,1,0:T(8,128)(2,1)}) custom-call(s32[2]{0:T(128)} %pad_add_fusion.where_ref, f32[6,4]{1,0:T(8,128)} %copy.18.scale_ref, bf16[4,4,128,256]{3,2,1,0:T(8,128)(2,1)} %constant.16.clone.tabley_hbm, ...), custom_call_target="tpu_custom_call" | custom-call | flops 8000000000 | bytes 1048576 | tf_op jit(solution)/shard_map/middle/pallas_call | solution.py:337
  131.6 10.3 %middle.5 = (bf16[8,3,64,128]{3,2,1,0:T(8,128)(2,1)}, bf16[8,3,64,128]{3,2,1,0:T(8,128)(2,1)}, bf16[8,3,64,128]{3,2,1,0:T(8,128)(2,1)}, bf16[8,3,64,128]{3,2,1,0:T(8,128)(2,1)}) custom-call(s32[2]{0:T(128)} %pad_add_fusion.where_ref, f32[6,4]{1,0:T(8,128)} %copy.18.scale_ref, bf16[4,4,128,256]{3,2,1,0:T(8,128)(2,1)} %constant.16.clone.tabley_hbm, ...), custom_call_target="tpu_custom_call" | custom-call | flops 8000000000 | bytes 1048576 | tf_op jit(solution)/shard_map/middle/pallas_call | solution.py:337
  142.8 10.5 %middle.4 = (bf16[8,3,64,128]{3,2,1,0:T(8,128)(2,1)}, bf16[8,3,64,128]{3,2,1,0:T(8,128)(2,1)}, bf16[8,3,64,128]{3,2,1,0:T(8,128)(2,1)}, bf16[8,3,64,128]{3,2,1,0:T(8,128)(2,1)}) custom-call(s32[2]{0:T(128)} %pad_add_fusion.where_ref, f32[6,4]{1,0:T(8,128)} %copy.18.scale_ref, bf16[4,4,128,256]{3,2,1,0:T(8,128)(2,1)} %constant.16.clone.tabley_hbm, ...), custom_call_target="tpu_custom_call" | custom-call | flops 8000000000 | bytes 1048576 | tf_op jit(solution)/shard_map/middle/pallas_call | solution.py:337
  173.1 3.7 %collective-permute-done.55.c = bf16[8,3,64,128]{3,2,1,0:T(8,128)(2,1)S(1)} collective-permute-done((bf16[8,3,64,128]{3,2,1,0:T(8,128)(2,1)}, bf16[8,3,64,128]{3,2,1,0:T(8,128)(2,1)S(1)}, u32[]{:S(2)}, u32[]{:S(2)}) %collective-permute-start.55) | collective-permute-done | bytes 393248 | tf_op jit(solution)/shard_map/ppermute | solution.py:368
  179.5 5.7 %collective-permute-done.35.c = bf16[8,3,64,128]{3,2,1,0:T(8,128)(2,1)S(1)} collective-permute-done((bf16[8,3,64,128]{3,2,1,0:T(8,128)(2,1)}, bf16[8,3,64,128]{3,2,1,0:T(8,128)(2,1)S(1)}, u32[]{:S(2)}, u32[]{:S(2)}) %collective-permute-start.35) | collective-permute-done | bytes 393248 | tf_op jit(solution)/shard_map/ppermute | solution.py:368
  185.1 7.9 %collective-permute-done.15.c = bf16[8,3,64,128]{3,2,1,0:T(8,128)(2,1)S(1)} collective-permute-done((bf16[8,3,64,128]{3,2,1,0:T(8,128)(2,1)}, bf16[8,3,64,128]{3,2,1,0:T(8,128)(2,1)S(1)}, u32[]{:S(2)}, u32[]{:S(2)}) %collective-permute-start.15) | collective-permute-done | bytes 393248 | tf_op jit(solution)/shard_map/ppermute | solution.py:368
  201.1 3.4 %collective-permute-start.59 = (bf16[3,64,128]{2,1,0:T(8,128)(2,1)}, bf16[3,64,128]{2,1,0:T(8,128)(2,1)S(1)}, u32[]{:S(2)}, u32[]{:S(2)}) collective-permute-start(bf16[3,64,128]{2,1,0:T(8,128)(2,1)} %get-tuple-element.153), channel_id=1, source_target_pairs={{0,4},{1,5},{2,6},{3,7},{4,0},{5,1},{6,2},{7,3},{8,12},{9,13},{10,... | collective-permute-start | bytes 147464 | tf_op jit(solution)/shard_map/ppermute | solution.py:368
  241.2 6.1 %inverse_z.1 = (bf16[4,3,64,128]{3,2,1,0:T(8,128)(2,1)}, bf16[4,3,64,128]{3,2,1,0:T(8,128)(2,1)}, bf16[4,3,64,128]{3,2,1,0:T(8,128)(2,1)}, bf16[4,3,64,128]{3,2,1,0:T(8,128)(2,1)}) custom-call(s32[2]{0:T(128)} %pad_add_fusion.where_ref, bf16[3,64,128]{2,1,0:T(8,128)(2,1)} %get-tuple-element.109.rest_0_, bf16[3,64,128]{2,1,0:T(8,128)(2,1)} %copy-done.61, ...), custom_call_target="tpu_custom_call" | custom-call | flops 4000000000 | bytes 1048576 | tf_op jit(solution)/shard_map/inverse_z/pallas_call | solution.py:337
  249.2 6.2 %collective-permute-done.84.rest_2_ = bf16[4,3,64,128]{3,2,1,0:T(8,128)(2,1)S(1)} collective-permute-done((bf16[4,3,64,128]{3,2,1,0:T(8,128)(2,1)}, bf16[4,3,64,128]{3,2,1,0:T(8,128)(2,1)S(1)}, u32[]{:S(2)}, u32[]{:S(2)}) %collective-permute-start.84) | collective-permute-done | bytes 196640 | tf_op jit(solution)/shard_map/ppermute | solution.py:368
  255.4 3.1 %collective-permute-done.85.rest_3_ = bf16[4,3,64,128]{3,2,1,0:T(8,128)(2,1)S(1)} collective-permute-done((bf16[4,3,64,128]{3,2,1,0:T(8,128)(2,1)}, bf16[4,3,64,128]{3,2,1,0:T(8,128)(2,1)S(1)}, u32[]{:S(2)}, u32[]{:S(2)}) %collective-permute-start.85) | collective-permute-done | bytes 196640 | tf_op jit(solution)/shard_map/ppermute | solution.py:368
  259.2 3.0 %result.1 = bf16[2,3,4,64,256]{4,3,2,1,0:T(8,128)(2,1)} custom-call(s32[2]{0:T(128)} %pad_add_fusion.where_ref, bf16[2,3,4,64,256]{4,3,2,1,0:T(8,128)(2,1)} %field_ref.3, bf16[64,64]{1,0:T(8,128)(2,1)} %constant.19.clone.order_ref, bf16[4,3,64,128]{3,2,1,0:T(8,128)(2,1)} %get-tuple-element.177.rest_0_, bf16[4,3,64,128]{3,2,1,0:T(8,128)(2,1)} %copy-done.32, ...), custom_call_target="tpu_custom_call" | custom-call | flops 3000000000 | bytes 1048576 | tf_op jit(solution)/shard_map/result/pallas_call | solution.py:337
  (355 shorter events, 132.4 us)
Async XLA Ops:
  47.6 19.2 %collective-permute-start.71 = (bf16[8,3,64,128]{3,2,1,0:T(8,128)(2,1)}, bf16[8,3,64,128]{3,2,1,0:T(8,128)(2,1)S(1)}, u32[]{:S(2)}, u32[]{:S(2)}) collective-permute-start(bf16[8,3,64,128]{3,2,1,0:T(8,128)(2,1)} %join.7.rest_0_), channel_id=1, source_target_pairs={{0,16},{8,24},{16,0},{24,8},{1,17},{9,25},{17,1},{25,9},{2,18},{10... | collective-permute-start | bytes 1179656 | tf_op jit(solution)/shard_map/ppermute | solution.py:368
  66.1 39.5 %collective-permute-start.70 = (bf16[8,3,64,128]{3,2,1,0:T(8,128)(2,1)}, bf16[8,3,64,128]{3,2,1,0:T(8,128)(2,1)S(1)}, u32[]{:S(2)}, u32[]{:S(2)}) collective-permute-start(bf16[8,3,64,128]{3,2,1,0:T(8,128)(2,1)} %join.7.rest_0_), channel_id=1, source_target_pairs={{0,8},{8,0},{16,24},{24,16},{1,9},{9,1},{17,25},{25,17},{2,10},{10... | collective-permute-start | bytes 1179656 | tf_op jit(solution)/shard_map/ppermute | solution.py:368
  66.2 39.5 %collective-permute-start.51 = (bf16[8,3,64,128]{3,2,1,0:T(8,128)(2,1)}, bf16[8,3,64,128]{3,2,1,0:T(8,128)(2,1)S(1)}, u32[]{:S(2)}, u32[]{:S(2)}) collective-permute-start(bf16[8,3,64,128]{3,2,1,0:T(8,128)(2,1)} %join.6.rest_0_), channel_id=1, source_target_pairs={{0,16},{8,24},{16,0},{24,8},{1,17},{9,25},{17,1},{25,9},{2,18},{10... | collective-permute-start | bytes 1179656 | tf_op jit(solution)/shard_map/ppermute | solution.py:368
  66.8 39.6 %collective-permute-start.72 = (bf16[8,3,64,128]{3,2,1,0:T(8,128)(2,1)S(1)}, bf16[8,3,64,128]{3,2,1,0:T(8,128)(2,1)S(1)}, u32[]{:S(2)}, u32[]{:S(2)}) collective-permute-start(bf16[8,3,64,128]{3,2,1,0:T(8,128)(2,1)S(1)} %collective-permute-done.71.rest_2_), channel_id=1, source_target_pairs={{0,8},{8,0},{16,24},{24,16},{1,9},{9,1},{17,25},{25,17},{2,10},{10... | collective-permute-start | bytes 1179656 | tf_op jit(solution)/shard_map/ppermute | solution.py:368
  98.7 18.7 %collective-permute-start.50 = (bf16[8,3,64,128]{3,2,1,0:T(8,128)(2,1)}, bf16[8,3,64,128]{3,2,1,0:T(8,128)(2,1)S(1)}, u32[]{:S(2)}, u32[]{:S(2)}) collective-permute-start(bf16[8,3,64,128]{3,2,1,0:T(8,128)(2,1)} %join.6.rest_0_), channel_id=1, source_target_pairs={{0,8},{8,0},{16,24},{24,16},{1,9},{9,1},{17,25},{25,17},{2,10},{10... | collective-permute-start | bytes 1179656 | tf_op jit(solution)/shard_map/ppermute | solution.py:368
  102.4 15.2 %collective-permute-start.31 = (bf16[8,3,64,128]{3,2,1,0:T(8,128)(2,1)}, bf16[8,3,64,128]{3,2,1,0:T(8,128)(2,1)S(1)}, u32[]{:S(2)}, u32[]{:S(2)}) collective-permute-start(bf16[8,3,64,128]{3,2,1,0:T(8,128)(2,1)} %join.5.rest_0_), channel_id=1, source_target_pairs={{0,16},{8,24},{16,0},{24,8},{1,17},{9,25},{17,1},{25,9},{2,18},{10... | collective-permute-start | bytes 1179656 | tf_op jit(solution)/shard_map/ppermute | solution.py:368
  105.6 24.6 %collective-permute-start.30 = (bf16[8,3,64,128]{3,2,1,0:T(8,128)(2,1)}, bf16[8,3,64,128]{3,2,1,0:T(8,128)(2,1)S(1)}, u32[]{:S(2)}, u32[]{:S(2)}) collective-permute-start(bf16[8,3,64,128]{3,2,1,0:T(8,128)(2,1)} %join.5.rest_0_), channel_id=1, source_target_pairs={{0,8},{8,0},{16,24},{24,16},{1,9},{9,1},{17,25},{25,17},{2,10},{10... | collective-permute-start | bytes 1179656 | tf_op jit(solution)/shard_map/ppermute | solution.py:368
  105.7 13.2 %collective-permute-start.11 = (bf16[8,3,64,128]{3,2,1,0:T(8,128)(2,1)}, bf16[8,3,64,128]{3,2,1,0:T(8,128)(2,1)S(1)}, u32[]{:S(2)}, u32[]{:S(2)}) collective-permute-start(bf16[8,3,64,128]{3,2,1,0:T(8,128)(2,1)} %join.4.rest_0_), channel_id=1, source_target_pairs={{0,16},{8,24},{16,0},{24,8},{1,17},{9,25},{17,1},{25,9},{2,18},{10... | collective-permute-start | bytes 1179656 | tf_op jit(solution)/shard_map/ppermute | solution.py:368
  117.5 24.4 %collective-permute-start.10 = (bf16[8,3,64,128]{3,2,1,0:T(8,128)(2,1)S(1)}, bf16[8,3,64,128]{3,2,1,0:T(8,128)(2,1)S(1)}, u32[]{:S(2)}, u32[]{:S(2)}) collective-permute-start(bf16[8,3,64,128]{3,2,1,0:T(8,128)(2,1)S(1)} %copy-done.11), channel_id=1, source_target_pairs={{0,8},{8,0},{16,24},{24,16},{1,9},{9,1},{17,25},{25,17},{2,10},{10... | collective-permute-start | bytes 1179656 | tf_op jit(solution)/shard_map/ppermute | solution.py:368
  117.7 13.1 %collective-permute-start.32 = (bf16[8,3,64,128]{3,2,1,0:T(8,128)(2,1)S(1)}, bf16[8,3,64,128]{3,2,1,0:T(8,128)(2,1)S(1)}, u32[]{:S(2)}, u32[]{:S(2)}) collective-permute-start(bf16[8,3,64,128]{3,2,1,0:T(8,128)(2,1)S(1)} %collective-permute-done.31.rest_2_), channel_id=1, source_target_pairs={{0,8},{8,0},{16,24},{24,16},{1,9},{9,1},{17,25},{25,17},{2,10},{10... | collective-permute-start | bytes 1179656 | tf_op jit(solution)/shard_map/ppermute | solution.py:368
  118.9 23.1 %collective-permute-start.12 = (bf16[8,3,64,128]{3,2,1,0:T(8,128)(2,1)S(1)}, bf16[8,3,64,128]{3,2,1,0:T(8,128)(2,1)S(1)}, u32[]{:S(2)}, u32[]{:S(2)}) collective-permute-start(bf16[8,3,64,128]{3,2,1,0:T(8,128)(2,1)S(1)} %collective-permute-done.11.rest_2_), channel_id=1, source_target_pairs={{0,8},{8,0},{16,24},{24,16},{1,9},{9,1},{17,25},{25,17},{2,10},{10... | collective-permute-start | bytes 1179656 | tf_op jit(solution)/shard_map/ppermute | solution.py:368
  118.9 40.8 %collective-permute-start.73 = (bf16[8,3,64,128]{3,2,1,0:T(8,128)(2,1)}, bf16[8,3,64,128]{3,2,1,0:T(8,128)(2,1)S(1)}, u32[]{:S(2)}, u32[]{:S(2)}) collective-permute-start(bf16[8,3,64,128]{3,2,1,0:T(8,128)(2,1)} %get-tuple-element.166), channel_id=1, source_target_pairs={{0,8},{8,0},{16,24},{24,16},{1,9},{9,1},{17,25},{25,17},{2,10},{10... | collective-permute-start | bytes 1179656 | tf_op jit(solution)/shard_map/ppermute | solution.py:368
  130.3 23.0 %collective-permute-start.74 = (bf16[8,3,64,128]{3,2,1,0:T(8,128)(2,1)S(1)}, bf16[8,3,64,128]{3,2,1,0:T(8,128)(2,1)S(1)}, u32[]{:S(2)}, u32[]{:S(2)}) collective-permute-start(bf16[8,3,64,128]{3,2,1,0:T(8,128)(2,1)S(1)} %copy-done.15), channel_id=1, source_target_pairs={{0,8},{8,0},{16,24},{24,16},{1,9},{9,1},{17,25},{25,17},{2,10},{10... | collective-permute-start | bytes 1179656 | tf_op jit(solution)/shard_map/ppermute | solution.py:368
  130.8 29.1 %collective-permute-start.53 = (bf16[8,3,64,128]{3,2,1,0:T(8,128)(2,1)}, bf16[8,3,64,128]{3,2,1,0:T(8,128)(2,1)S(1)}, u32[]{:S(2)}, u32[]{:S(2)}) collective-permute-start(bf16[8,3,64,128]{3,2,1,0:T(8,128)(2,1)} %get-tuple-element.146), channel_id=1, source_target_pairs={{0,8},{8,0},{16,24},{24,16},{1,9},{9,1},{17,25},{25,17},{2,10},{10... | collective-permute-start | bytes 1179656 | tf_op jit(solution)/shard_map/ppermute | solution.py:368
  141.9 14.2 %collective-permute-start.54 = (bf16[8,3,64,128]{3,2,1,0:T(8,128)(2,1)S(1)}, bf16[8,3,64,128]{3,2,1,0:T(8,128)(2,1)S(1)}, u32[]{:S(2)}, u32[]{:S(2)}) collective-permute-start(bf16[8,3,64,128]{3,2,1,0:T(8,128)(2,1)S(1)} %copy-done.20), channel_id=1, source_target_pairs={{0,8},{8,0},{16,24},{24,16},{1,9},{9,1},{17,25},{25,17},{2,10},{10... | collective-permute-start | bytes 1179656 | tf_op jit(solution)/shard_map/ppermute | solution.py:368
  142.0 18.3 %collective-permute-start.34 = (bf16[8,3,64,128]{3,2,1,0:T(8,128)(2,1)}, bf16[8,3,64,128]{3,2,1,0:T(8,128)(2,1)S(1)}, u32[]{:S(2)}, u32[]{:S(2)}) collective-permute-start(bf16[8,3,64,128]{3,2,1,0:T(8,128)(2,1)} %get-tuple-element.128), channel_id=1, source_target_pairs={{0,8},{8,0},{16,24},{24,16},{1,9},{9,1},{17,25},{25,17},{2,10},{10... | collective-permute-start | bytes 1179656 | tf_op jit(solution)/shard_map/ppermute | solution.py:368
  159.9 13.1 %collective-permute-start.13 = (bf16[8,3,64,128]{3,2,1,0:T(8,128)(2,1)}, bf16[8,3,64,128]{3,2,1,0:T(8,128)(2,1)S(1)}, u32[]{:S(2)}, u32[]{:S(2)}) collective-permute-start(bf16[8,3,64,128]{3,2,1,0:T(8,128)(2,1)} %get-tuple-element.106), channel_id=1, source_target_pairs={{0,8},{8,0},{16,24},{24,16},{1,9},{9,1},{17,25},{25,17},{2,10},{10... | collective-permute-start | bytes 1179656 | tf_op jit(solution)/shard_map/ppermute | solution.py:368
  160.3 16.4 %collective-permute-start.55 = (bf16[8,3,64,128]{3,2,1,0:T(8,128)(2,1)}, bf16[8,3,64,128]{3,2,1,0:T(8,128)(2,1)S(1)}, u32[]{:S(2)}, u32[]{:S(2)}) collective-permute-start(bf16[8,3,64,128]{3,2,1,0:T(8,128)(2,1)} %add.8), channel_id=1, source_target_pairs={{0,16},{8,24},{16,0},{24,8},{1,17},{9,25},{17,1},{25,9},{2,18},{10... | collective-permute-start | bytes 1179656 | tf_op jit(solution)/shard_map/ppermute | solution.py:368
  163.0 22.1 %collective-permute-start.35 = (bf16[8,3,64,128]{3,2,1,0:T(8,128)(2,1)}, bf16[8,3,64,128]{3,2,1,0:T(8,128)(2,1)S(1)}, u32[]{:S(2)}, u32[]{:S(2)}) collective-permute-start(bf16[8,3,64,128]{3,2,1,0:T(8,128)(2,1)} %add.7), channel_id=1, source_target_pairs={{0,16},{8,24},{16,0},{24,8},{1,17},{9,25},{17,1},{25,9},{2,18},{10... | collective-permute-start | bytes 1179656 | tf_op jit(solution)/shard_map/ppermute | solution.py:368
  168.3 24.7 %collective-permute-start.15 = (bf16[8,3,64,128]{3,2,1,0:T(8,128)(2,1)}, bf16[8,3,64,128]{3,2,1,0:T(8,128)(2,1)S(1)}, u32[]{:S(2)}, u32[]{:S(2)}) collective-permute-start(bf16[8,3,64,128]{3,2,1,0:T(8,128)(2,1)} %add.6), channel_id=1, source_target_pairs={{0,16},{8,24},{16,0},{24,8},{1,17},{9,25},{17,1},{25,9},{2,18},{10... | collective-permute-start | bytes 1179656 | tf_op jit(solution)/shard_map/ppermute | solution.py:368
  172.0 21.5 %collective-permute-start.76 = (bf16[3,64,128]{2,1,0:T(8,128)(2,1)}, bf16[3,64,128]{2,1,0:T(8,128)(2,1)S(1)}, u32[]{:S(2)}, u32[]{:S(2)}) collective-permute-start(bf16[3,64,128]{2,1,0:T(8,128)(2,1)} %get-tuple-element.170), channel_id=1, source_target_pairs={{0,1},{1,0},{2,3},{3,2},{4,5},{5,4},{6,7},{7,6},{8,9},{9,8},{10,11... | collective-permute-start | bytes 147464 | tf_op jit(solution)/shard_map/ppermute | solution.py:368
  173.0 22.8 %collective-permute-start.77 = (bf16[3,64,128]{2,1,0:T(8,128)(2,1)}, bf16[3,64,128]{2,1,0:T(8,128)(2,1)S(1)}, u32[]{:S(2)}, u32[]{:S(2)}) collective-permute-start(bf16[3,64,128]{2,1,0:T(8,128)(2,1)} %get-tuple-element.171), channel_id=1, source_target_pairs={{0,2},{1,3},{2,0},{3,1},{4,6},{5,7},{6,4},{7,5},{8,10},{9,11},{10,... | collective-permute-start | bytes 147464 | tf_op jit(solution)/shard_map/ppermute | solution.py:368
  176.7 20.9 %collective-permute-start.78 = (bf16[3,64,128]{2,1,0:T(8,128)(2,1)}, bf16[3,64,128]{2,1,0:T(8,128)(2,1)S(1)}, u32[]{:S(2)}, u32[]{:S(2)}) collective-permute-start(bf16[3,64,128]{2,1,0:T(8,128)(2,1)} %get-tuple-element.172), channel_id=1, source_target_pairs={{0,3},{1,2},{2,1},{3,0},{4,7},{5,6},{6,5},{7,4},{8,11},{9,10},{10,... | collective-permute-start | bytes 147464 | tf_op jit(solution)/shard_map/ppermute | solution.py:368
  185.1 13.7 %collective-permute-start.79 = (bf16[3,64,128]{2,1,0:T(8,128)(2,1)}, bf16[3,64,128]{2,1,0:T(8,128)(2,1)S(1)}, u32[]{:S(2)}, u32[]{:S(2)}) collective-permute-start(bf16[3,64,128]{2,1,0:T(8,128)(2,1)} %get-tuple-element.173), channel_id=1, source_target_pairs={{0,4},{1,5},{2,6},{3,7},{4,0},{5,1},{6,2},{7,3},{8,12},{9,13},{10,... | collective-permute-start | bytes 147464 | tf_op jit(solution)/shard_map/ppermute | solution.py:368
  (153 other events, 1863.4 us)
where the time goes:
time: 263 us; the launch traced here: 262 us
  starting transfers between devices  105 us (40%)
  Pallas kernels  83.8 us (32%)
  waiting for transfers between devices  62.8 us (24%)
  local copies, waits for them, and re-layouts  9.45 us (4%)
    ppermute x86, starting transfers between devices, send(): return lax.ppermute(value, axis, [(i, i ^ distance) for i in range(size)])  105 us
    pallas_call x20, Pallas kernels, call(): pl.pallas_call(kernel, in_specs=specs, out_specs=[vmem() for _ in shapes]...  83.8 us
    ppermute x86, waiting for transfers between devices, send(): return lax.ppermute(value, axis, [(i, i ^ distance) for i in range(size)])  62.8 us
    unnamed x185, local copies, waits for them, and re-layouts  8.78 us
  transfers between devices with their start and end apart: 86, of which 24 were waited for; matrix products, arithmetic and copies ran while one was open for 0% of the time, Pallas kernels for 24%

commit v1 on v0

--- a/solution.py
+++ b/solution.py
@@ -11,6 +11,7 @@
 
 pairing = ((0, 3, 4), (3, 1, 5), (4, 5, 2))
 
+CHUNK = 2
 VMEM = pltpu.VMEM
 f32 = jnp.float32
 bf16 = jnp.bfloat16
@@ -118,11 +119,11 @@
         outs[s][...] = scratch[me ^ s]
 
 
-def forward_z_kernel(where_ref, *rest, groups, members, held):
+def forward_z_kernel(where_ref, *rest, groups, chunk):
     pieces = rest[:groups]
-    outs = rest[groups : groups + members * held]
-    source, target = rest[groups + members * held :]
-    me, at = where_ref[0], where_ref[1]
+    outs, source = rest[groups:-1], rest[-1]
+    me = where_ref[0]
+    held = chunk * len(outs)
     planes, comps, rows, lanes = pieces[0].shape
     total = planes * groups
     for s in range(groups):
@@ -137,31 +138,29 @@
         values = [
             source[z // planes, z % planes, j, pl.ds(at_row, tile), :].astype(f32) for z in range(total)
         ]
-        even = transform_list(values, -1.0, low)
-        for k, v in enumerate(even):
-            target[2 * k, j, pl.ds(at_row, tile), :] = v.astype(bf16)
+
+        def keep(k, v):
+            out = outs[k % held // chunk]
+            out[k // held, k % chunk, j, pl.ds(at_row, tile), :] = v.astype(bf16)
+
+        for k, v in enumerate(transform_list(values, -1.0, low)):
+            keep(2 * k, v)
         turned = [times(v, -2.0 * math.pi * z / (2 * total), low) for z, v in enumerate(values)]
         for k, v in enumerate(transform_list(turned, -1.0, low)):
-            target[2 * k + 1, j, pl.ds(at_row, tile), :] = v.astype(bf16)
+            keep(2 * k + 1, v)
         return carry
 
     lax.fori_loop(0, comps * steps, step, 0)
-    for r in range(held):
-        for s in range(members):
-            outs[r * members + s][...] = target[(at ^ s) * held + r]
-
-
-def inverse_z_kernel(where_ref, *rest, groups, members, held):
-    pieces = rest[: members * held]
-    outs = rest[members * held : members * held + groups]
-    source, target = rest[members * held + groups :]
-    me, at = where_ref[0], where_ref[1]
-    comps, rows, lanes = pieces[0].shape
+
+
+def inverse_z_kernel(where_ref, *rest, groups, chunks):
+    pieces = rest[:chunks]
+    outs, target = rest[chunks:-1], rest[-1]
+    me = where_ref[0]
+    members, chunk, comps, rows, lanes = pieces[0].shape
+    held = chunk * chunks
     total = members * held // 2
     planes = total // groups
-    for r in range(held):
-        for s in range(members):
-            source[(at ^ s) * held + r] = pieces[r * members + s][...]
     tile = min(16, rows)
     steps = rows // tile
     low = lax.broadcasted_iota(jnp.int32, (tile, lanes), 1) < lanes // 2
@@ -169,7 +168,10 @@
     def step(n, carry):
         j = n // steps
         at_row = pl.multiple_of((n % steps) * tile, tile)
-        values = [source[k, j, pl.ds(at_row, tile), :].astype(f32) for k in range(2 * total)]
+        values = [
+            pieces[k % held // chunk][k // held, k % chunk, j, pl.ds(at_row, tile), :].astype(f32)
+            for k in range(2 * total)
+        ]
         even = transform_list(values[0::2], 1.0, low)
         odd = transform_list(values[1::2], 1.0, low)
         for z in range(total):
@@ -183,40 +185,50 @@
 
 
 def middle_kernel(
-    where_ref, scale_ref, tabley_hbm, forward_hbm, inverse_hbm, green_hbm, *rest, plane, groups, members
+    where_ref, scale_ref, tabley_hbm, forward_hbm, inverse_hbm, green_hbm, *rest, first, chunk, groups, members
 ):
     pieces = rest[:groups]
     outs = rest[groups : 2 * groups]
     tabley, forward, inverse, green, spread, wide, product, sems = rest[2 * groups :]
-    me, at = where_ref[0], where_ref[1]
+    me = where_ref[0]
     _, comps, rows, lanes = pieces[0].shape
     half = rows // 2
+    g = pl.program_id(0)
+    plane = first + g
     copies = [
         pltpu.make_async_copy(tabley_hbm.at[me, me ^ t], tabley.at[pl.ds(t * lanes, lanes)], sems.at[t])
         for t in range(groups)
     ]
     copies.append(pltpu.make_async_copy(forward_hbm, forward, sems.at[groups]))
-    copies.append(pltpu.make_async_copy(green_hbm.at[:, :, plane], green, sems.at[groups + 1]))
-    copies.append(pltpu.make_async_copy(inverse_hbm, inverse, sems.at[groups + 2]))
-    for c in copies:
-        c.start()
-    for c in copies[:groups]:
-        c.wait()
+    copies.append(pltpu.make_async_copy(inverse_hbm, inverse, sems.at[groups + 1]))
+    load = pltpu.make_async_copy(green_hbm.at[:, :, plane], green, sems.at[groups + 2])
+    load.start()
+
+    @pl.when(g == 0)
+    def _():
+        for c in copies:
+            c.start()
+        for c in copies[:groups]:
+            c.wait()
+
     wave = tabley.shape[1] // 2
     for s in range(members):
         block = jnp.concatenate(
             [pieces[t][s].reshape(comps * rows, lanes) for t in range(groups)], axis=1
         )
         result = jnp.dot(block, tabley[...], preferred_element_type=f32).astype(bf16)
-        start = pl.multiple_of((at ^ s) * half, half)
+        start = s * half
         for j in range(comps):
             for p in range(2):
                 spread[j, p, pl.ds(start, half), :] = result[j * rows + p * half : j * rows + (p + 1) * half]
-    copies[groups].wait()
+    @pl.when(g == 0)
+    def _():
+        copies[groups].wait()
+
     for j in range(comps):
         for p in range(2):
             wide[j, p] = jnp.dot(forward[p], spread[j, p], preferred_element_type=f32)
-    copies[groups + 1].wait()
+    load.wait()
     many = wide.shape[2] // 2
     tile = 16
 
@@ -260,7 +272,10 @@
         return carry
 
     lax.fori_loop(0, many // tile, step, 0)
-    copies[groups + 2].wait()
+    @pl.when(g == 0)
+    def _():
+        copies[groups + 1].wait()
+
     count = inverse.shape[1] // 2
     for i in range(comps):
         for p in range(2):
@@ -274,24 +289,9 @@
             ).astype(bf16)
             for b in range(members):
                 for t in range(groups):
-                    outs[t][at ^ b, i, p * half : (p + 1) * half, :] = share[
+                    outs[t][b, i, p * half : (p + 1) * half, :] = share[
                         b * half : (b + 1) * half, t * lanes : (t + 1) * lanes
                     ]
-
-
-def join_kernel(*refs):
-    ins, out = refs[:-1], refs[-1]
-    for s, piece in enumerate(ins):
-        out[s] = piece[...]
-
-
-def add_kernel(a, b, out):
-    out[...] = (a[...].astype(f32) + b[...].astype(f32)).astype(bf16)
-
-
-def finish_kernel(a, b, c, *outs):
-    for s, out in enumerate(outs):
-        out[...] = (a[s].astype(f32) + b[s].astype(f32) + c[s].astype(f32)).astype(bf16)
 
 
 def result_kernel(where_ref, field_ref, order_ref, *rest, groups, factor):
@@ -332,12 +332,13 @@
     return pl.BlockSpec(memory_space=pl.ANY)
 
 
-def call(kernel, specs, shapes, scratch, flops, args, name):
+def call(kernel, specs, shapes, scratch, flops, args, name, grid=(), out_spec=None):
     many = isinstance(shapes, list)
     return pl.pallas_call(
         kernel,
+        grid=grid,
         in_specs=specs,
-        out_specs=[vmem() for _ in shapes] if many else vmem(),
+        out_specs=[out_spec or vmem() for _ in shapes] if many else vmem(),
         out_shape=shapes,
         scratch_shapes=scratch,
         compiler_params=pltpu.CompilerParams(vmem_limit_bytes=56 * 1024 * 1024),
@@ -385,29 +386,39 @@
         "moments",
     )
     parts = exchange(parts, "zg")
+    chunk = min(CHUNK, held)
+    chunks = held // chunk
+    full = shape(members, chunk, comps, rows, lanes)
     pieces = call(
-        functools.partial(forward_z_kernel, groups=groups, members=members, held=held),
+        functools.partial(forward_z_kernel, groups=groups, chunk=chunk),
         [smem()] + [vmem()] * groups,
-        [shape(comps, rows, lanes)] * (members * held),
-        [VMEM((groups, planes, comps, rows, lanes), bf16), VMEM((length_z, comps, rows, lanes), bf16)],
+        [full] * chunks,
+        [VMEM((groups, planes, comps, rows, lanes), bf16)],
         4e9,
         (where, *parts),
         "forward_z",
     )
-    full = shape(members, comps, rows, lanes)
-    returned = []
-    for r in range(held):
-        mine = exchange(pieces[r * members : (r + 1) * members], "xy")
-        gathered = [call(join_kernel, [vmem()] * members, full, [], 1e9, mine, "join")]
-        have = {0: gathered[0]}
+    block = pl.BlockSpec((members, None, comps, rows, lanes), lambda g: (0, g, 0, 0, 0))
+
+    def after(value, *others):
+        return lax.optimization_barrier((value, *others))[0] if others else value
+
+    def across(value):
+        return lax.all_to_all(value, "xy", 0, 0, tiled=True)
+
+    def gather(value):
+        have = {0: value}
         bit = groups // 2
         while bit:
             for t in sorted(have):
                 have[t ^ bit] = send(have[t], "zg", groups, bit)
             bit //= 2
-        shares = call(
-            functools.partial(middle_kernel, plane=r, groups=groups, members=members),
-            [smem(), smem(), hbm(), hbm(), hbm(), hbm()] + [vmem()] * groups,
+        return [have[t] for t in range(groups)]
+
+    def middle(r, have):
+        return call(
+            functools.partial(middle_kernel, first=r * chunk, chunk=chunk, groups=groups, members=members),
+            [smem(), smem(), hbm(), hbm(), hbm(), hbm()] + [block] * groups,
             [full] * groups,
             [
                 VMEM((groups * lanes, 2 * wave), bf16),
@@ -419,32 +430,46 @@
                 VMEM((comps, 2, length_x // 2, 2 * wave), bf16),
                 pltpu.SemaphoreType.DMA((groups + 3,)),
             ],
-            8e9,
-            (where, green_scale, tabley, forward, inverse, green_spectrum, *[have[t] for t in range(groups)]),
+            8e9 * chunk,
+            (where, green_scale, tabley, forward, inverse, green_spectrum, *have),
             "middle",
+            grid=(chunk,),
+            out_spec=block,
         )
-        held_shares = dict(enumerate(shares))
+
+    def reduce(shares):
+        shares = dict(enumerate(shares))
         bit = 1
         while bit < groups // 2:
-            moved = {t: send(held_shares[t ^ bit], "zg", groups, bit) for t in held_shares if not t & bit}
-            later = {}
-            for t in moved:
-                if t:
-                    later[t] = call(add_kernel, [vmem()] * 2, full, [], 1e9, (held_shares[t], moved[t]), "add")
-                else:
-                    own = (held_shares[t], moved[t])
-            held_shares = later
+            moved = {t: send(shares[t ^ bit], "zg", groups, bit) for t in shares if not t & bit}
+            shares = {
+                t: (shares[t].astype(f32) + moved[t].astype(f32)).astype(bf16) if t else (shares[t], moved[t])
+                for t in moved
+            }
             bit *= 2
-        last = send(held_shares[bit], "zg", groups, bit)
-        split = call(
-            finish_kernel, [vmem()] * 3, [shape(comps, rows, lanes)] * members, [], 1e9, (*own, last), "finish"
-        )
-        returned += exchange(split, "xy")
+        own, moved = shares[0]
+        last = send(shares[bit], "zg", groups, bit)
+        return (own.astype(f32) + moved.astype(f32) + last.astype(f32)).astype(bf16)
+
+    arrived, shared, totals = [], [], []
+    for r in range(chunks):
+        value = after(pieces[r], *arrived[-1:])
+        arrived.append(across(value))
+    ready = []
+    for r in range(chunks):
+        have = gather(after(arrived[r], *(shared[r - 2][:1] if r >= 2 else [])))
+        ready.append(have)
+        if r + 1 < chunks:
+            have = [after(have[0], arrived[r + 1])] + have[1:]
+        shared.append(middle(r, have))
+    returned = []
+    for r in range(chunks):
+        returned.append(across(after(reduce(shared[r]), *returned[-1:])))
     parts = call(
-        functools.partial(inverse_z_kernel, groups=groups, members=members, held=held),
-        [smem()] + [vmem()] * (members * held),
+        functools.partial(inverse_z_kernel, groups=groups, chunks=chunks),
+        [smem()] + [vmem()] * chunks,
         [shape(planes, comps, rows, lanes)] * groups,
-        [VMEM((length_z, comps, rows, lanes), bf16), VMEM((groups, planes, comps, rows, lanes), bf16)],
+        [VMEM((groups, planes, comps, rows, lanes), bf16)],
         4e9,
         (where, *returned),
         "inverse_z",

time: 263 us -> 199 us (0.76)
  starting transfers between devices: 105 us -> 18.1 us
  blocking collectives: 0 us -> 52 us
  Pallas kernels: 83.8 us -> 57.2 us
  waiting for transfers between devices: 62.8 us -> 58.8 us
  other arithmetic: 0.59 us -> 4.07 us
    ppermute x86 -> x18, starting transfers between devices: 105 us -> 10.8 us  [send(): return lax.ppermute(value, axis, [(i, i ^ distance) for i in range(size)])]
    all_to_all x0 -> x2, blocking collectives: none -> 52 us  [across(): return lax.all_to_all(value, 'xy', 0, 0, tiled=True)]
    pallas_call x20 -> x6, Pallas kernels: 83.8 us -> 57.2 us  [call(): pl.pallas_call(kernel, grid=grid, in_specs=specs, out_specs=[out_spec or...]
    ppermute x86 -> x18, waiting for transfers between devices: 62.8 us -> 52.7 us  [send(): return lax.ppermute(value, axis, [(i, i ^ distance) for i in range(size)])]
    all_to_all x0 -> x2, starting transfers between devices: none -> 7.32 us  [across(): return lax.all_to_all(value, 'xy', 0, 0, tiled=True)]
    all_to_all x0 -> x2, waiting for transfers between devices: none -> 6.15 us  [across(): return lax.all_to_all(value, 'xy', 0, 0, tiled=True)]
    convert_element_type x0 -> x4, other arithmetic: none -> 3.46 us  [the longest x2 1.73 us: reduce(): return (own.astype(f32) + moved.astype(f32) + last.astype(f32)).astype(bf16)]
    unnamed x185 -> x41, local copies, waits for them, and re-layouts: 8.78 us -> 7.08 us
  transfers between devices with their start and end apart: 86 -> 20, of which waited for: 24 -> 10; matrix products, arithmetic and copies ran while one was open for 0% -> 2% of each run, Pallas kernels for 24% -> 19%
where the time goes in v1:
time: 199 us; the launch traced here: 198 us
  waiting for transfers between devices  58.8 us (30%)
  Pallas kernels  57.2 us (29%)
  blocking collectives  52 us (26%)
  starting transfers between devices  18.1 us (9%)
  local copies, waits for them, and re-layouts  7.69 us (4%)
  other arithmetic  4.07 us (2%)
    pallas_call x6, Pallas kernels, call(): pl.pallas_call(kernel, grid=grid, in_specs=specs, out_specs=[out_spec or...  57.2 us
    ppermute x18, waiting for transfers between devices, send(): return lax.ppermute(value, axis, [(i, i ^ distance) for i in range(size)])  52.7 us
    all_to_all x2, blocking collectives, across(): return lax.all_to_all(value, 'xy', 0, 0, tiled=True)  52 us
    ppermute x18, starting transfers between devices, send(): return lax.ppermute(value, axis, [(i, i ^ distance) for i in range(size)])  10.8 us
    all_to_all x2, starting transfers between devices, across(): return lax.all_to_all(value, 'xy', 0, 0, tiled=True)  7.32 us
    unnamed x41, local copies, waits for them, and re-layouts  7.08 us
    all_to_all x2, waiting for transfers between devices, across(): return lax.all_to_all(value, 'xy', 0, 0, tiled=True)  6.15 us
  transfers between devices with their start and end apart: 20, of which 10 were waited for; matrix products, arithmetic and copies ran while one was open for 2% of the time, Pallas kernels for 19%

profile of v1, /device:TPU:0, one launch (start us, length us, event | category | flops | bytes accessed | tf_op | source)
XLA Modules:
  0.0 198.1 jit_solution(8964731483942385662)
XLA Ops:
  1.4 1.4 copy.15.material_ref
  3.5 3.9 %moments.1 = (bf16[4,3,64,128]{3,2,1,0:T(8,128)(2,1)}, bf16[4,3,64,128]{3,2,1,0:T(8,128)(2,1)}, bf16[4,3,64,128]{3,2,1,0:T(8,128)(2,1)}, bf16[4,3,64,128]{3,2,1,0:T(8,128)(2,1)}) custom-call(s32[2]{0:T(128)} %pad_add_fusion.where_ref, f32[72]{0:T(128)} %reshape.3.alpha_ref, bf16[2,3,4,64,256]{4,3,2,1,0:T(8,128)(2,1)} %field_ref.3, ...), custom_call_target="tpu_custom_call" | custom-call | flops 5000000000 | bytes 1048576 | tf_op jit(solution)/shard_map/moments/pallas_call | solution.py:337
  7.9 2.5 %collective-permute-start.1 = (bf16[4,3,64,128]{3,2,1,0:T(8,128)(2,1)}, bf16[4,3,64,128]{3,2,1,0:T(8,128)(2,1)S(1)}, u32[]{:S(2)}, u32[]{:S(2)}) collective-permute-start(bf16[4,3,64,128]{3,2,1,0:T(8,128)(2,1)} %get-tuple-element.28), channel_id=1, source_target_pairs={{0,16},{8,24},{16,0},{24,8},{1,17},{9,25},{17,1},{25,9},{2,18},{10... | collective-permute-start | bytes 589832 | tf_op jit(solution)/shard_map/ppermute | solution.py:369
  10.5 5.8 %collective-permute-done.1.rest_2_ = bf16[4,3,64,128]{3,2,1,0:T(8,128)(2,1)S(1)} collective-permute-done((bf16[4,3,64,128]{3,2,1,0:T(8,128)(2,1)}, bf16[4,3,64,128]{3,2,1,0:T(8,128)(2,1)S(1)}, u32[]{:S(2)}, u32[]{:S(2)}) %collective-permute-start.1) | collective-permute-done | bytes 196640 | tf_op jit(solution)/shard_map/ppermute | solution.py:369
  16.4 3.8 %collective-permute-done.2.rest_3_ = bf16[4,3,64,128]{3,2,1,0:T(8,128)(2,1)S(1)} collective-permute-done((bf16[4,3,64,128]{3,2,1,0:T(8,128)(2,1)}, bf16[4,3,64,128]{3,2,1,0:T(8,128)(2,1)S(1)}, u32[]{:S(2)}, u32[]{:S(2)}) %collective-permute-start.2) | collective-permute-done | bytes 196640 | tf_op jit(solution)/shard_map/ppermute | solution.py:369
  20.9 6.2 %forward_z.1 = (bf16[8,2,3,64,128]{4,3,2,1,0:T(8,128)(2,1)}, bf16[8,2,3,64,128]{4,3,2,1,0:T(8,128)(2,1)}) custom-call(s32[2]{0:T(128)} %pad_add_fusion.where_ref, bf16[4,3,64,128]{3,2,1,0:T(8,128)(2,1)} %get-tuple-element.26.rest_0_, bf16[4,3,64,128]{3,2,1,0:T(8,128)(2,1)} %copy-done.13, bf16[4,3,64,128]{3,2,1,0:T(8,128)(2,1)} %copy-done.15, ...), custom_call_target="tpu_custom_call" | custom-call | flops 4000000000 | bytes 1048576 | tf_op jit(solution)/shard_map/forward_z/pallas_call | solution.py:337
  27.1 26.5 %all_to_all.20.rest_0_ = bf16[8,2,3,64,128]{4,3,2,1,0:T(8,128)(2,1)S(1)} all-to-all(bf16[8,2,3,64,128]{4,3,2,1,0:T(8,128)(2,1)} %get-tuple-element.30), channel_id=1, replica_groups=mesh['zg'=4,'xy'=8] {'xy'}, dimensions={0} | all-to-all | bytes 1572864 | tf_op jit(solution)/shard_map/all_to_all | solution.py:407
  53.6 1.5 collective-permute-start.4
  55.0 3.6 %all-to-all-start.1 = ((bf16[8,2,3,64,128]{4,3,2,1,0:T(8,128)(2,1)}), bf16[8,2,3,64,128]{4,3,2,1,0:T(8,128)(2,1)S(1)}, u32[]{:S(2)}, u32[]{:S(2)}) async-start(bf16[8,2,3,64,128]{4,3,2,1,0:T(8,128)(2,1)} %get-tuple-element.32), calls=%async_computation.1 | async-start | bytes 1572864 | tf_op jit(solution)/shard_map/all_to_all | solution.py:407
  58.7 13.1 %collective-permute-done.4.rest_2_ = bf16[8,2,3,64,128]{4,3,2,1,0:T(8,128)(2,1)S(1)} collective-permute-done((bf16[8,2,3,64,128]{4,3,2,1,0:T(8,128)(2,1)S(1)}, bf16[8,2,3,64,128]{4,3,2,1,0:T(8,128)(2,1)S(1)}, u32[]{:S(2)}, u32[]{:S(2)}) %collective-permute-start.4) | collective-permute-done | bytes 786464 | tf_op jit(solution)/shard_map/ppermute | solution.py:369
  72.7 6.0 %all-to-all-done.1.rest_0_ = bf16[8,2,3,64,128]{4,3,2,1,0:T(8,128)(2,1)S(1)} async-done(((bf16[8,2,3,64,128]{4,3,2,1,0:T(8,128)(2,1)}), bf16[8,2,3,64,128]{4,3,2,1,0:T(8,128)(2,1)S(1)}, u32[]{:S(2)}, u32[]{:S(2)}) %all-to-all-start.1) | async-done | bytes 786464 | tf_op jit(solution)/shard_map/all_to_all | solution.py:407
  80.1 19.1 %middle.2 = (bf16[8,2,3,64,128]{4,3,2,1,0:T(8,128)(2,1)}, bf16[8,2,3,64,128]{4,3,2,1,0:T(8,128)(2,1)}, bf16[8,2,3,64,128]{4,3,2,1,0:T(8,128)(2,1)}, bf16[8,2,3,64,128]{4,3,2,1,0:T(8,128)(2,1)}) custom-call(s32[2]{0:T(128)} %pad_add_fusion.where_ref, f32[6,4]{1,0:T(8,128)} %copy.16.scale_ref, bf16[4,4,128,256]{3,2,1,0:T(8,128)(2,1)} %constant.16.clone.tabley_hbm, ...), custom_call_target="tpu_custom_call" | custom-call | flops 16000000000 | bytes 1048576 | tf_op jit(solution)/shard_map/middle/pallas_call | solution.py:337
  100.3 1.5 collective-permute-done.7
  101.7 1.4 add_convert_fusion.3
  103.2 1.6 collective-permute-start.8
  106.5 19.1 %middle.3 = (bf16[8,2,3,64,128]{4,3,2,1,0:T(8,128)(2,1)}, bf16[8,2,3,64,128]{4,3,2,1,0:T(8,128)(2,1)}, bf16[8,2,3,64,128]{4,3,2,1,0:T(8,128)(2,1)}, bf16[8,2,3,64,128]{4,3,2,1,0:T(8,128)(2,1)}) custom-call(s32[2]{0:T(128)} %pad_add_fusion.where_ref, f32[6,4]{1,0:T(8,128)} %copy.16.scale_ref, bf16[4,4,128,256]{3,2,1,0:T(8,128)(2,1)} %constant.16.clone.tabley_hbm, ...), custom_call_target="tpu_custom_call" | custom-call | flops 16000000000 | bytes 1048576 | tf_op jit(solution)/shard_map/middle/pallas_call | solution.py:337
  125.7 1.3 add_convert_fusion.2
  127.0 3.7 %all-to-all-start.2 = ((bf16[8,2,3,64,128]{4,3,2,1,0:T(8,128)(2,1)}), bf16[8,2,3,64,128]{4,3,2,1,0:T(8,128)(2,1)S(1)}, u32[]{:S(2)}, u32[]{:S(2)}) async-start(bf16[8,2,3,64,128]{4,3,2,1,0:T(8,128)(2,1)} %add_convert_fusion.2), calls=%async_computation.2 | async-start | bytes 1572864 | tf_op jit(solution)/shard_map/all_to_all | solution.py:407
  133.2 17.9 %collective-permute-done.14 = bf16[8,2,3,64,128]{4,3,2,1,0:T(8,128)(2,1)S(1)} collective-permute-done((bf16[8,2,3,64,128]{4,3,2,1,0:T(8,128)(2,1)S(1)}, bf16[8,2,3,64,128]{4,3,2,1,0:T(8,128)(2,1)S(1)}, u32[]{:S(2)}, u32[]{:S(2)}) %collective-permute-start.14) | collective-permute-done | bytes 786464 | tf_op jit(solution)/shard_map/ppermute | solution.py:369
  151.7 25.5 %all_to_all.21.rest_1_ = bf16[8,2,3,64,128]{4,3,2,1,0:T(8,128)(2,1)} all-to-all(bf16[8,2,3,64,128]{4,3,2,1,0:T(8,128)(2,1)S(1)} %add_convert_fusion), channel_id=1, replica_groups=mesh['zg'=4,'xy'=8] {'xy'}, dimensions={0} | all-to-all | bytes 1572864 | tf_op jit(solution)/shard_map/all_to_all | solution.py:407
  177.2 6.0 %inverse_z.1 = (bf16[4,3,64,128]{3,2,1,0:T(8,128)(2,1)}, bf16[4,3,64,128]{3,2,1,0:T(8,128)(2,1)}, bf16[4,3,64,128]{3,2,1,0:T(8,128)(2,1)}, bf16[4,3,64,128]{3,2,1,0:T(8,128)(2,1)}) custom-call(s32[2]{0:T(128)} %pad_add_fusion.where_ref, bf16[8,2,3,64,128]{4,3,2,1,0:T(8,128)(2,1)} %copy-done.1, bf16[8,2,3,64,128]{4,3,2,1,0:T(8,128)(2,1)} %all_to_all.21.rest_1_), custom_call_target="tpu_custom_call" | custom-call | flops 4000000000 | bytes 1048576 | tf_op jit(solution)/shard_map/inverse_z/pallas_call | solution.py:337
  185.1 6.1 %collective-permute-done.16.rest_2_ = bf16[4,3,64,128]{3,2,1,0:T(8,128)(2,1)S(1)} collective-permute-done((bf16[4,3,64,128]{3,2,1,0:T(8,128)(2,1)}, bf16[4,3,64,128]{3,2,1,0:T(8,128)(2,1)S(1)}, u32[]{:S(2)}, u32[]{:S(2)}) %collective-permute-start.16) | collective-permute-done | bytes 196640 | tf_op jit(solution)/shard_map/ppermute | solution.py:369
  191.2 3.3 %collective-permute-done.17.rest_3_ = bf16[4,3,64,128]{3,2,1,0:T(8,128)(2,1)S(1)} collective-permute-done((bf16[4,3,64,128]{3,2,1,0:T(8,128)(2,1)}, bf16[4,3,64,128]{3,2,1,0:T(8,128)(2,1)S(1)}, u32[]{:S(2)}, u32[]{:S(2)}) %collective-permute-start.17) | collective-permute-done | bytes 196640 | tf_op jit(solution)/shard_map/ppermute | solution.py:369
  195.1 3.0 %result.1 = bf16[2,3,4,64,256]{4,3,2,1,0:T(8,128)(2,1)} custom-call(s32[2]{0:T(128)} %pad_add_fusion.where_ref, bf16[2,3,4,64,256]{4,3,2,1,0:T(8,128)(2,1)} %field_ref.3, bf16[64,64]{1,0:T(8,128)(2,1)} %constant.19.clone.order_ref, bf16[4,3,64,128]{3,2,1,0:T(8,128)(2,1)} %get-tuple-element.43.rest_0_, bf16[4,3,64,128]{3,2,1,0:T(8,128)(2,1)} %copy-done.14, ...), custom_call_target="tpu_custom_call" | custom-call | flops 3000000000 | bytes 1048576 | tf_op jit(solution)/shard_map/result/pallas_call | solution.py:337
  (71 shorter events, 14.1 us)
Async XLA Ops:
  7.4 3.1 %collective-permute-start = (bf16[4,3,64,128]{3,2,1,0:T(8,128)(2,1)}, bf16[4,3,64,128]{3,2,1,0:T(8,128)(2,1)S(1)}, u32[]{:S(2)}, u32[]{:S(2)}) collective-permute-start(bf16[4,3,64,128]{3,2,1,0:T(8,128)(2,1)} %get-tuple-element.27), channel_id=1, source_target_pairs={{0,8},{8,0},{16,24},{24,16},{1,9},{9,1},{17,25},{25,17},{2,10},{10... | collective-permute-start | bytes 589832 | tf_op jit(solution)/shard_map/ppermute | solution.py:369
  7.9 8.4 %collective-permute-start.1 = (bf16[4,3,64,128]{3,2,1,0:T(8,128)(2,1)}, bf16[4,3,64,128]{3,2,1,0:T(8,128)(2,1)S(1)}, u32[]{:S(2)}, u32[]{:S(2)}) collective-permute-start(bf16[4,3,64,128]{3,2,1,0:T(8,128)(2,1)} %get-tuple-element.28), channel_id=1, source_target_pairs={{0,16},{8,24},{16,0},{24,8},{1,17},{9,25},{17,1},{25,9},{2,18},{10... | collective-permute-start | bytes 589832 | tf_op jit(solution)/shard_map/ppermute | solution.py:369
  10.4 9.8 %collective-permute-start.2 = (bf16[4,3,64,128]{3,2,1,0:T(8,128)(2,1)}, bf16[4,3,64,128]{3,2,1,0:T(8,128)(2,1)S(1)}, u32[]{:S(2)}, u32[]{:S(2)}) collective-permute-start(bf16[4,3,64,128]{3,2,1,0:T(8,128)(2,1)} %get-tuple-element.29), channel_id=1, source_target_pairs={{0,24},{8,16},{16,8},{24,0},{1,25},{9,17},{17,9},{25,1},{2,26},{10... | collective-permute-start | bytes 589832 | tf_op jit(solution)/shard_map/ppermute | solution.py:369
  27.1 44.8 %copy-start.6 = (f32[6,4]{0,1:T(4,128)S(1)}, f32[6,4]{0,1:T(4,128)}, u32[]{:S(2)}) copy-start(f32[6,4]{0,1:T(4,128)} %param.13) | copy-start | bytes 292
  53.6 25.7 %copy-start.2 = (bf16[8,2,3,64,128]{4,3,2,1,0:T(8,128)(2,1)}, bf16[8,2,3,64,128]{4,3,2,1,0:T(8,128)(2,1)S(1)}, u32[]{:S(2)}) copy-start(bf16[8,2,3,64,128]{4,3,2,1,0:T(8,128)(2,1)S(1)} %all_to_all.20.rest_0_) | copy-start | bytes 2359300
  53.6 18.3 %collective-permute-start.4 = (bf16[8,2,3,64,128]{4,3,2,1,0:T(8,128)(2,1)S(1)}, bf16[8,2,3,64,128]{4,3,2,1,0:T(8,128)(2,1)S(1)}, u32[]{:S(2)}, u32[]{:S(2)}) collective-permute-start(bf16[8,2,3,64,128]{4,3,2,1,0:T(8,128)(2,1)S(1)} %all_to_all.20.rest_0_), channel_id=1, source_target_pairs={{0,16},{8,24},{16,0},{24,8},{1,17},{9,25},{17,1},{25,9},{2,18},{10... | collective-permute-start | bytes 2359304 | tf_op jit(solution)/shard_map/ppermute | solution.py:369
  55.0 23.6 %all-to-all-start.1 = ((bf16[8,2,3,64,128]{4,3,2,1,0:T(8,128)(2,1)}), bf16[8,2,3,64,128]{4,3,2,1,0:T(8,128)(2,1)S(1)}, u32[]{:S(2)}, u32[]{:S(2)}) async-start(bf16[8,2,3,64,128]{4,3,2,1,0:T(8,128)(2,1)} %get-tuple-element.32), calls=%async_computation.1 | async-start | bytes 1572864 | tf_op jit(solution)/shard_map/all_to_all | solution.py:407
  58.7 20.5 %collective-permute-start.3 = (bf16[8,2,3,64,128]{4,3,2,1,0:T(8,128)(2,1)S(1)}, bf16[8,2,3,64,128]{4,3,2,1,0:T(8,128)(2,1)S(1)}, u32[]{:S(2)}, u32[]{:S(2)}) collective-permute-start(bf16[8,2,3,64,128]{4,3,2,1,0:T(8,128)(2,1)S(1)} %all_to_all.20.rest_0_), channel_id=1, source_target_pairs={{0,8},{8,0},{16,24},{24,16},{1,9},{9,1},{17,25},{25,17},{2,10},{10... | collective-permute-start | bytes 2359304 | tf_op jit(solution)/shard_map/ppermute | solution.py:369
  71.9 7.3 %collective-permute-start.5 = (bf16[8,2,3,64,128]{4,3,2,1,0:T(8,128)(2,1)S(1)}, bf16[8,2,3,64,128]{4,3,2,1,0:T(8,128)(2,1)}, u32[]{:S(2)}, u32[]{:S(2)}) collective-permute-start(bf16[8,2,3,64,128]{4,3,2,1,0:T(8,128)(2,1)S(1)} %collective-permute-done.4.rest_2_), channel_id=1, source_target_pairs={{0,8},{8,0},{16,24},{24,16},{1,9},{9,1},{17,25},{25,17},{2,10},{10... | collective-permute-start | bytes 2359304 | tf_op jit(solution)/shard_map/ppermute | solution.py:369
  78.7 21.1 %collective-permute-start.10 = (bf16[8,2,3,64,128]{4,3,2,1,0:T(8,128)(2,1)S(1)}, bf16[8,2,3,64,128]{4,3,2,1,0:T(8,128)(2,1)S(1)}, u32[]{:S(2)}, u32[]{:S(2)}) collective-permute-start(bf16[8,2,3,64,128]{4,3,2,1,0:T(8,128)(2,1)S(1)} %all-to-all-done.1.rest_0_), channel_id=1, source_target_pairs={{0,16},{8,24},{16,0},{24,8},{1,17},{9,25},{17,1},{25,9},{2,18},{10... | collective-permute-start | bytes 2359304 | tf_op jit(solution)/shard_map/ppermute | solution.py:369
  99.2 2.6 %collective-permute-start.7 = (bf16[8,2,3,64,128]{4,3,2,1,0:T(8,128)(2,1)}, bf16[8,2,3,64,128]{4,3,2,1,0:T(8,128)(2,1)S(1)}, u32[]{:S(2)}, u32[]{:S(2)}) collective-permute-start(bf16[8,2,3,64,128]{4,3,2,1,0:T(8,128)(2,1)} %get-tuple-element.37), channel_id=1, source_target_pairs={{0,8},{8,0},{16,24},{24,16},{1,9},{9,1},{17,25},{25,17},{2,10},{10... | collective-permute-start | bytes 2359304 | tf_op jit(solution)/shard_map/ppermute | solution.py:369
  99.2 5.5 %collective-permute-start.9 = (bf16[8,2,3,64,128]{4,3,2,1,0:T(8,128)(2,1)S(1)}, bf16[8,2,3,64,128]{4,3,2,1,0:T(8,128)(2,1)S(1)}, u32[]{:S(2)}, u32[]{:S(2)}) collective-permute-start(bf16[8,2,3,64,128]{4,3,2,1,0:T(8,128)(2,1)S(1)} %all-to-all-done.1.rest_0_), channel_id=1, source_target_pairs={{0,8},{8,0},{16,24},{24,16},{1,9},{9,1},{17,25},{25,17},{2,10},{10... | collective-permute-start | bytes 2359304 | tf_op jit(solution)/shard_map/ppermute | solution.py:369
  99.7 5.0 %collective-permute-start.11 = (bf16[8,2,3,64,128]{4,3,2,1,0:T(8,128)(2,1)S(1)}, bf16[8,2,3,64,128]{4,3,2,1,0:T(8,128)(2,1)S(1)}, u32[]{:S(2)}, u32[]{:S(2)}) collective-permute-start(bf16[8,2,3,64,128]{4,3,2,1,0:T(8,128)(2,1)S(1)} %collective-permute-done.10.rest_2_), channel_id=1, source_target_pairs={{0,8},{8,0},{16,24},{24,16},{1,9},{9,1},{17,25},{25,17},{2,10},{10... | collective-permute-start | bytes 2359304 | tf_op jit(solution)/shard_map/ppermute | solution.py:369
  99.8 25.8 %collective-permute-start.6 = (bf16[8,2,3,64,128]{4,3,2,1,0:T(8,128)(2,1)}, bf16[8,2,3,64,128]{4,3,2,1,0:T(8,128)(2,1)S(1)}, u32[]{:S(2)}, u32[]{:S(2)}) collective-permute-start(bf16[8,2,3,64,128]{4,3,2,1,0:T(8,128)(2,1)} %get-tuple-element.35), channel_id=1, source_target_pairs={{0,8},{8,0},{16,24},{24,16},{1,9},{9,1},{17,25},{25,17},{2,10},{10... | collective-permute-start | bytes 2359304 | tf_op jit(solution)/shard_map/ppermute | solution.py:369
  103.2 22.5 %copy-start.3 = (bf16[8,2,3,64,128]{4,3,2,1,0:T(8,128)(2,1)S(1)}, bf16[8,2,3,64,128]{4,3,2,1,0:T(8,128)(2,1)}, u32[]{:S(2)}) copy-start(bf16[8,2,3,64,128]{4,3,2,1,0:T(8,128)(2,1)} %get-tuple-element.34) | copy-start | bytes 2359300
  103.2 22.5 %collective-permute-start.8 = (bf16[8,2,3,64,128]{4,3,2,1,0:T(8,128)(2,1)S(1)}, bf16[8,2,3,64,128]{4,3,2,1,0:T(8,128)(2,1)S(1)}, u32[]{:S(2)}, u32[]{:S(2)}) collective-permute-start(bf16[8,2,3,64,128]{4,3,2,1,0:T(8,128)(2,1)S(1)} %add_convert_fusion.3), channel_id=1, source_target_pairs={{0,16},{8,24},{16,0},{24,8},{1,17},{9,25},{17,1},{25,9},{2,18},{10... | collective-permute-start | bytes 2359304 | tf_op jit(solution)/shard_map/ppermute | solution.py:369
  125.6 5.7 %collective-permute-start.13 = (bf16[8,2,3,64,128]{4,3,2,1,0:T(8,128)(2,1)}, bf16[8,2,3,64,128]{4,3,2,1,0:T(8,128)(2,1)S(1)}, u32[]{:S(2)}, u32[]{:S(2)}) collective-permute-start(bf16[8,2,3,64,128]{4,3,2,1,0:T(8,128)(2,1)} %get-tuple-element.41), channel_id=1, source_target_pairs={{0,8},{8,0},{16,24},{24,16},{1,9},{9,1},{17,25},{25,17},{2,10},{10... | collective-permute-start | bytes 2359304 | tf_op jit(solution)/shard_map/ppermute | solution.py:369
  127.0 24.7 %all-to-all-start.2 = ((bf16[8,2,3,64,128]{4,3,2,1,0:T(8,128)(2,1)}), bf16[8,2,3,64,128]{4,3,2,1,0:T(8,128)(2,1)S(1)}, u32[]{:S(2)}, u32[]{:S(2)}) async-start(bf16[8,2,3,64,128]{4,3,2,1,0:T(8,128)(2,1)} %add_convert_fusion.2), calls=%async_computation.2 | async-start | bytes 1572864 | tf_op jit(solution)/shard_map/all_to_all | solution.py:407
  130.7 2.5 %collective-permute-start.12 = (bf16[8,2,3,64,128]{4,3,2,1,0:T(8,128)(2,1)S(1)}, bf16[8,2,3,64,128]{4,3,2,1,0:T(8,128)(2,1)S(1)}, u32[]{:S(2)}, u32[]{:S(2)}) collective-permute-start(bf16[8,2,3,64,128]{4,3,2,1,0:T(8,128)(2,1)S(1)} %copy-done.8), channel_id=1, source_target_pairs={{0,8},{8,0},{16,24},{24,16},{1,9},{9,1},{17,25},{25,17},{2,10},{10... | collective-permute-start | bytes 2359304 | tf_op jit(solution)/shard_map/ppermute | solution.py:369
  131.6 19.5 %collective-permute-start.14 = (bf16[8,2,3,64,128]{4,3,2,1,0:T(8,128)(2,1)S(1)}, bf16[8,2,3,64,128]{4,3,2,1,0:T(8,128)(2,1)S(1)}, u32[]{:S(2)}, u32[]{:S(2)}) collective-permute-start(bf16[8,2,3,64,128]{4,3,2,1,0:T(8,128)(2,1)S(1)} %add_convert_fusion.1), channel_id=1, source_target_pairs={{0,16},{8,24},{16,0},{24,8},{1,17},{9,25},{17,1},{25,9},{2,18},{10... | collective-permute-start | bytes 2359304 | tf_op jit(solution)/shard_map/ppermute | solution.py:369
  151.7 25.5 %copy-start.1 = (bf16[8,2,3,64,128]{4,3,2,1,0:T(8,128)(2,1)}, bf16[8,2,3,64,128]{4,3,2,1,0:T(8,128)(2,1)S(1)}, u32[]{:S(2)}) copy-start(bf16[8,2,3,64,128]{4,3,2,1,0:T(8,128)(2,1)S(1)} %all-to-all-done.2.rest_0_) | copy-start | bytes 2359300
  183.2 1.9 collective-permute-start.15
  183.2 8.0 %collective-permute-start.16 = (bf16[4,3,64,128]{3,2,1,0:T(8,128)(2,1)}, bf16[4,3,64,128]{3,2,1,0:T(8,128)(2,1)S(1)}, u32[]{:S(2)}, u32[]{:S(2)}) collective-permute-start(bf16[4,3,64,128]{3,2,1,0:T(8,128)(2,1)} %get-tuple-element.45), channel_id=1, source_target_pairs={{0,16},{8,24},{16,0},{24,8},{1,17},{9,25},{17,1},{25,9},{2,18},{10... | collective-permute-start | bytes 589832 | tf_op jit(solution)/shard_map/ppermute | solution.py:369
  183.7 10.7 %collective-permute-start.17 = (bf16[4,3,64,128]{3,2,1,0:T(8,128)(2,1)}, bf16[4,3,64,128]{3,2,1,0:T(8,128)(2,1)S(1)}, u32[]{:S(2)}, u32[]{:S(2)}) collective-permute-start(bf16[4,3,64,128]{3,2,1,0:T(8,128)(2,1)} %get-tuple-element.46), channel_id=1, source_target_pairs={{0,24},{8,16},{16,8},{24,0},{1,25},{9,17},{17,9},{25,1},{2,26},{10... | collective-permute-start | bytes 589832 | tf_op jit(solution)/shard_map/ppermute | solution.py:369
  (15 other events, 91.6 us)

commit v2 on v1

--- a/solution.py
+++ b/solution.py
@@ -11,7 +11,6 @@
 
 pairing = ((0, 3, 4), (3, 1, 5), (4, 5, 2))
 
-CHUNK = 2
 VMEM = pltpu.VMEM
 f32 = jnp.float32
 bf16 = jnp.bfloat16
@@ -82,115 +81,114 @@
     return [e + o for e, o in zip(even, odd)] + [e - o for e, o in zip(even, odd)]
 
 
-def moments_kernel(where_ref, alpha_ref, field_ref, material_ref, order_ref, *rest, groups, counts):
+def moments_kernel(alpha_ref, field_ref, material_ref, order_ref, *rest, groups, counts):
     outs, scratch = rest[:groups], rest[groups]
-    me = where_ref[0]
-    _, _, planes, rows, many = field_ref.shape
-    blocks = material_ref.shape[2]
+    me = lax.axis_index("zg")
+    _, comps, rows, many = field_ref.shape
+    blocks = material_ref.shape[0]
     cols = many // blocks
     part = many // groups
+    per = cols // part
     low = lax.broadcasted_iota(jnp.int32, (rows, 2 * part), 1) < part
-    for z in range(planes):
-        for b in range(blocks):
-            mat = jnp.broadcast_to(material_ref[z, :, b : b + 1], (rows, cols))
-            masks = [mat == n for n in range(1, counts)]
-
-            def pick(c, i, j):
-                value = jnp.full((rows, cols), alpha_ref[((0 * 2 + c) * 3 + i) * 3 + j], f32)
-                for n in range(1, counts):
-                    value = jnp.where(masks[n - 1], alpha_ref[((n * 2 + c) * 3 + i) * 3 + j], value)
-                return value
-
-            reals = [field_ref[0, j, z, :, b * cols : (b + 1) * cols].astype(f32) for j in range(3)]
-            imags = [field_ref[1, j, z, :, b * cols : (b + 1) * cols].astype(f32) for j in range(3)]
-            for i in range(3):
-                re = im = None
-                for j in range(3):
-                    ar, ai = pick(0, i, j), pick(1, i, j)
-                    r = ar * reals[j] - ai * imags[j]
-                    m = ar * imags[j] + ai * reals[j]
-                    re, im = (r, m) if re is None else (re + r, im + m)
-                first = jnp.where(low, re, swapped(im)).astype(bf16)
-                second = jnp.where(low, swapped(re), im).astype(bf16)
-                for h, v in enumerate((first, second)):
-                    v = jnp.dot(order_ref[...], v, preferred_element_type=f32).astype(bf16)
-                    scratch[2 * b + h, z, i] = v
+    diagonal = lax.broadcasted_iota(jnp.int32, (rows, rows), 0) == lax.broadcasted_iota(jnp.int32, (rows, rows), 1)
+    for b in range(blocks):
+        along = jnp.broadcast_to(material_ref[b : b + 1, :].astype(f32), (rows, rows))
+        mat = jnp.sum(jnp.where(diagonal, along, 0.0), axis=1, keepdims=True)
+        mat = jnp.broadcast_to(mat, (rows, cols))
+        masks = [mat == float(n) for n in range(1, counts)]
+
+        def pick(c, i, j):
+            value = jnp.full((rows, cols), alpha_ref[i, j, c, 0], f32)
+            for n in range(1, counts):
+                value = jnp.where(masks[n - 1], alpha_ref[i, j, c, n], value)
+            return value
+
+        reals = [field_ref[0, j, :, b * cols : (b + 1) * cols].astype(f32) for j in range(comps)]
+        imags = [field_ref[1, j, :, b * cols : (b + 1) * cols].astype(f32) for j in range(comps)]
+        for i in range(comps):
+            re = im = None
+            for j in range(comps):
+                ar, ai = pick(0, i, j), pick(1, i, j)
+                r = ar * reals[j] - ai * imags[j]
+                m = ar * imags[j] + ai * reals[j]
+                re, im = (r, m) if re is None else (re + r, im + m)
+            first = jnp.where(low, re, swapped(im)).astype(bf16)
+            second = jnp.where(low, swapped(re), im).astype(bf16)
+            for h, v in enumerate((first, second)):
+                scratch[per * b + h, i] = jnp.dot(order_ref[...], v, preferred_element_type=f32).astype(bf16)
     for s in range(groups):
         outs[s][...] = scratch[me ^ s]
 
 
-def forward_z_kernel(where_ref, *rest, groups, chunk):
+def forward_z_kernel(*rest, groups, places):
     pieces = rest[:groups]
     outs, source = rest[groups:-1], rest[-1]
-    me = where_ref[0]
-    held = chunk * len(outs)
-    planes, comps, rows, lanes = pieces[0].shape
+    me = lax.axis_index("zg")
+    held = len(places)
+    planes, rows, lanes = pieces[0].shape
     total = planes * groups
     for s in range(groups):
         source[me ^ s] = pieces[s][...]
     tile = min(16, rows)
-    steps = rows // tile
     low = lax.broadcasted_iota(jnp.int32, (tile, lanes), 1) < lanes // 2
 
     def step(n, carry):
-        j = n // steps
-        at_row = pl.multiple_of((n % steps) * tile, tile)
-        values = [
-            source[z // planes, z % planes, j, pl.ds(at_row, tile), :].astype(f32) for z in range(total)
-        ]
+        top = pl.multiple_of(n * tile, tile)
+
+        def values():
+            return [source[z // planes, z % planes, pl.ds(top, tile), :].astype(f32) for z in range(total)]
 
         def keep(k, v):
-            out = outs[k % held // chunk]
-            out[k // held, k % chunk, j, pl.ds(at_row, tile), :] = v.astype(bf16)
-
-        for k, v in enumerate(transform_list(values, -1.0, low)):
+            chunk, place = places[k % held]
+            outs[chunk][k // held, place, pl.ds(top, tile), :] = v.astype(bf16)
+
+        for k, v in enumerate(transform_list(values(), -1.0, low)):
             keep(2 * k, v)
-        turned = [times(v, -2.0 * math.pi * z / (2 * total), low) for z, v in enumerate(values)]
+        turned = [times(v, -2.0 * math.pi * z / (2 * total), low) for z, v in enumerate(values())]
         for k, v in enumerate(transform_list(turned, -1.0, low)):
             keep(2 * k + 1, v)
         return carry
 
-    lax.fori_loop(0, comps * steps, step, 0)
-
-
-def inverse_z_kernel(where_ref, *rest, groups, chunks):
+    lax.fori_loop(0, rows // tile, step, 0)
+
+
+def inverse_z_kernel(*rest, groups, places, chunks):
     pieces = rest[:chunks]
     outs, target = rest[chunks:-1], rest[-1]
-    me = where_ref[0]
-    members, chunk, comps, rows, lanes = pieces[0].shape
-    held = chunk * chunks
+    me = lax.axis_index("zg")
+    members, _, rows, lanes = pieces[0].shape
+    held = len(places)
     total = members * held // 2
     planes = total // groups
     tile = min(16, rows)
-    steps = rows // tile
     low = lax.broadcasted_iota(jnp.int32, (tile, lanes), 1) < lanes // 2
 
     def step(n, carry):
-        j = n // steps
-        at_row = pl.multiple_of((n % steps) * tile, tile)
-        values = [
-            pieces[k % held // chunk][k // held, k % chunk, j, pl.ds(at_row, tile), :].astype(f32)
-            for k in range(2 * total)
-        ]
-        even = transform_list(values[0::2], 1.0, low)
-        odd = transform_list(values[1::2], 1.0, low)
+        top = pl.multiple_of(n * tile, tile)
+
+        def value(k):
+            chunk, place = places[k % held]
+            return pieces[chunk][k // held, place, pl.ds(top, tile), :].astype(f32)
+
+        even = transform_list([value(k) for k in range(0, 2 * total, 2)], 1.0, low)
+        odd = transform_list([value(k) for k in range(1, 2 * total, 2)], 1.0, low)
         for z in range(total):
             v = even[z] + times(odd[z], 2.0 * math.pi * z / (2 * total), low)
-            target[z // planes, z % planes, j, pl.ds(at_row, tile), :] = v.astype(bf16)
+            target[z // planes, z % planes, pl.ds(top, tile), :] = v.astype(bf16)
         return carry
 
-    lax.fori_loop(0, comps * steps, step, 0)
+    lax.fori_loop(0, rows // tile, step, 0)
     for s in range(groups):
         outs[s][...] = target[me ^ s]
 
 
 def middle_kernel(
-    where_ref, scale_ref, tabley_hbm, forward_hbm, inverse_hbm, green_hbm, *rest, first, chunk, groups, members
+    scale_ref, tabley_hbm, forward_hbm, inverse_hbm, green_hbm, *rest, first, chunk, groups, members
 ):
     pieces = rest[:groups]
     outs = rest[groups : 2 * groups]
     tabley, forward, inverse, green, spread, wide, product, sems = rest[2 * groups :]
-    me = where_ref[0]
+    me = lax.axis_index("zg")
     _, comps, rows, lanes = pieces[0].shape
     half = rows // 2
     g = pl.program_id(0)
@@ -247,7 +245,7 @@
         for h in range(2):
             weights = [
                 tuple(
-                    green[c, e, pl.ds(h * many + top, tile), :].astype(f32) * scale_ref[e, plane]
+                    green[c, e, pl.ds(h * many + top, tile), :].astype(f32) * scale_ref[plane, e]
                     for c in range(2)
                 )
                 for e in range(2 * comps)
@@ -294,17 +292,17 @@
                     ]
 
 
-def result_kernel(where_ref, field_ref, order_ref, *rest, groups, factor):
+def result_kernel(field_ref, order_ref, *rest, groups, factor):
     pieces, out, scratch = rest[:groups], rest[groups], rest[groups + 1]
-    me = where_ref[0]
-    _, _, planes, rows, many = field_ref.shape
+    me = lax.axis_index("zg")
+    _, comps, planes, rows, many = field_ref.shape
     part = many // groups
     lanes = 2 * part
     for s in range(groups):
         scratch[me ^ s] = pieces[s][...]
     low = lax.broadcasted_iota(jnp.int32, (rows, lanes), 1) < part
     for z in range(planes):
-        for i in range(3):
+        for i in range(comps):
             for b in range(groups // 2):
                 first, second = [
                     lax.dot_general(
@@ -338,13 +336,18 @@
         kernel,
         grid=grid,
         in_specs=specs,
-        out_specs=[out_spec or vmem() for _ in shapes] if many else vmem(),
+        out_specs=(out_spec if isinstance(out_spec, list) else [out_spec] * len(shapes)) if many else out_spec,
         out_shape=shapes,
         scratch_shapes=scratch,
         compiler_params=pltpu.CompilerParams(vmem_limit_bytes=56 * 1024 * 1024),
         cost_estimate=pl.CostEstimate(flops=int(flops), transcendentals=0, bytes_accessed=1 << 20),
         name=name,
     )(*args)
+
+
+def chunk_sizes(held):
+    edge = max(1, held // 2)
+    return [edge] * (held // edge)
 
 
 def on_device(dipole_field, material, alpha_table, green_spectrum, green_scale):
@@ -360,7 +363,6 @@
     lanes = 2 * part
     wave = length_y // groups
     counts = alpha_table.shape[0]
-    where = jnp.stack([lax.axis_index("zg"), lax.axis_index("xy")]).astype(jnp.int32)
     tabley = table_y(rows_y, length_y, groups)
     forward, inverse = tables_x(rows_x, length_x)
     order = parity_order(rows)
@@ -374,29 +376,39 @@
     def shape(*dims):
         return jax.ShapeDtypeStruct(dims, bf16)
 
-    cycle = 1e6
-
+    plane_block = pl.BlockSpec((2, comps, None, rows, rows_y), lambda z: (0, 0, z, 0, 0))
+    part_block = pl.BlockSpec((None, comps, rows, lanes), lambda z: (z, 0, 0, 0))
+    blocks = material.shape[2]
     parts = call(
         functools.partial(moments_kernel, groups=groups, counts=counts),
-        [smem(), smem(), vmem(), vmem(), vmem()],
+        [smem(), plane_block, pl.BlockSpec((None, blocks, rows), lambda z: (z, 0, 0)), vmem()],
         [shape(planes, comps, rows, lanes)] * groups,
-        [VMEM((groups, planes, comps, rows, lanes), bf16)],
+        [VMEM((groups, comps, rows, lanes), bf16)],
         5e9,
-        (where, alpha_table.reshape(-1), dipole_field, material, order),
+        (jnp.transpose(alpha_table, (2, 3, 1, 0)), dipole_field, jnp.transpose(material, (0, 2, 1)), order),
         "moments",
+        grid=(planes,),
+        out_spec=part_block,
     )
     parts = exchange(parts, "zg")
-    chunk = min(CHUNK, held)
-    chunks = held // chunk
-    full = shape(members, chunk, comps, rows, lanes)
+    sizes = chunk_sizes(held)
+    chunks = len(sizes)
+    places = [(c, n) for c, size in enumerate(sizes) for n in range(size)]
+    fulls = [shape(members, size, comps, rows, lanes) for size in sizes]
+    comp_block = pl.BlockSpec((planes, None, rows, lanes), lambda j: (0, j, 0, 0))
+    chunk_blocks = [
+        pl.BlockSpec((members, size, None, rows, lanes), lambda j: (0, 0, j, 0, 0)) for size in sizes
+    ]
     pieces = call(
-        functools.partial(forward_z_kernel, groups=groups, chunk=chunk),
-        [smem()] + [vmem()] * groups,
-        [full] * chunks,
-        [VMEM((groups, planes, comps, rows, lanes), bf16)],
+        functools.partial(forward_z_kernel, groups=groups, places=places),
+        [comp_block] * groups,
+        fulls,
+        [VMEM((groups, planes, rows, lanes), bf16)],
         4e9,
-        (where, *parts),
+        tuple(parts),
         "forward_z",
+        grid=(comps,),
+        out_spec=chunk_blocks,
     )
     block = pl.BlockSpec((members, None, comps, rows, lanes), lambda g: (0, g, 0, 0, 0))
 
@@ -417,9 +429,11 @@
 
     def middle(r, have):
         return call(
-            functools.partial(middle_kernel, first=r * chunk, chunk=chunk, groups=groups, members=members),
-            [smem(), smem(), hbm(), hbm(), hbm(), hbm()] + [block] * groups,
-            [full] * groups,
+            functools.partial(
+                middle_kernel, first=sum(sizes[:r]), chunk=sizes[r], groups=groups, members=members
+            ),
+            [smem(), hbm(), hbm(), hbm(), hbm()] + [block] * groups,
+            [fulls[r]] * groups,
             [
                 VMEM((groups * lanes, 2 * wave), bf16),
                 VMEM(forward.shape, bf16),
@@ -430,10 +444,10 @@
                 VMEM((comps, 2, length_x // 2, 2 * wave), bf16),
                 pltpu.SemaphoreType.DMA((groups + 3,)),
             ],
-            8e9 * chunk,
-            (where, green_scale, tabley, forward, inverse, green_spectrum, *have),
+            8e9 * sizes[r],
+            (jnp.transpose(green_scale), tabley, forward, inverse, green_spectrum, *have),
             "middle",
-            grid=(chunk,),
+            grid=(sizes[r],),
             out_spec=block,
         )
 
@@ -466,23 +480,26 @@
     for r in range(chunks):
         returned.append(across(after(reduce(shared[r]), *returned[-1:])))
     parts = call(
-        functools.partial(inverse_z_kernel, groups=groups, chunks=chunks),
-        [smem()] + [vmem()] * chunks,
+        functools.partial(inverse_z_kernel, groups=groups, places=places, chunks=chunks),
+        chunk_blocks,
         [shape(planes, comps, rows, lanes)] * groups,
-        [VMEM((groups, planes, comps, rows, lanes), bf16)],
+        [VMEM((groups, planes, rows, lanes), bf16)],
         4e9,
-        (where, *returned),
+        tuple(returned),
         "inverse_z",
+        grid=(comps,),
+        out_spec=comp_block,
     )
     parts = exchange(parts, "zg")
     return call(
         functools.partial(result_kernel, groups=groups, factor=1.0 / float(length_x * length_y * length_z)),
-        [smem(), vmem(), vmem()] + [vmem()] * groups,
+        [vmem()] * (2 + groups),
         shape(*dipole_field.shape),
         [VMEM((groups, planes, comps, rows, lanes), bf16)],
         3e9,
-        (where, dipole_field, order, *parts),
+        (dipole_field, order, *parts),
         "result",
+        out_spec=vmem(),
     )
 
 

time: 199 us -> 195 us (0.980)
  local copies, waits for them, and re-layouts: 7.69 us -> 4.02 us
    unnamed x41 -> x36, local copies, waits for them, and re-layouts: 7.08 us -> 4.02 us
  transfers between devices with their start and end apart: 20 -> 20, of which waited for: 10 -> 10; matrix products, arithmetic and copies ran while one was open for 2% -> 2% of each run, Pallas kernels for 19% -> 20%
where the time goes in v2:
time: 195 us; the launch traced here: 194 us
  waiting for transfers between devices  59.6 us (31%)
  Pallas kernels  56.8 us (29%)
  blocking collectives  51.9 us (27%)
  starting transfers between devices  18.3 us (9%)
  local copies, waits for them, and re-layouts  4.02 us (2%)
  other arithmetic  3.46 us (2%)
    pallas_call x6, Pallas kernels, call(): pl.pallas_call(kernel, grid=grid, in_specs=specs, out_specs=(out_spec if...  56.8 us
    ppermute x18, waiting for transfers between devices, send(): return lax.ppermute(value, axis, [(i, i ^ distance) for i in range(size)])  52.9 us
    all_to_all x2, blocking collectives, across(): return lax.all_to_all(value, 'xy', 0, 0, tiled=True)  51.9 us
    ppermute x18, starting transfers between devices, send(): return lax.ppermute(value, axis, [(i, i ^ distance) for i in range(size)])  10.9 us
    all_to_all x2, starting transfers between devices, across(): return lax.all_to_all(value, 'xy', 0, 0, tiled=True)  7.32 us
    all_to_all x2, waiting for transfers between devices, across(): return lax.all_to_all(value, 'xy', 0, 0, tiled=True)  6.67 us
    unnamed x36, local copies, waits for them, and re-layouts  4.02 us
  transfers between devices with their start and end apart: 20, of which 10 were waited for; matrix products, arithmetic and copies ran while one was open for 2% of the time, Pallas kernels for 20%

profile of v2, /device:TPU:0, one launch (start us, length us, event | category | flops | bytes accessed | tf_op | source)
XLA Modules:
  0.0 194.3 jit_solution(15508213332720731213)
XLA Ops:
  0.0 4.5 %moments.1 = (bf16[4,3,64,128]{3,2,1,0:T(8,128)(2,1)}, bf16[4,3,64,128]{3,2,1,0:T(8,128)(2,1)}, bf16[4,3,64,128]{3,2,1,0:T(8,128)(2,1)}, bf16[4,3,64,128]{3,2,1,0:T(8,128)(2,1)}) custom-call(f32[3,3,2,4]{3,2,1,0:T(2,128)} %bitcast.3, bf16[2,3,4,64,256]{4,3,2,1,0:T(8,128)(2,1)} %field_ref.3, s32[4,2,64]{2,1,0:T(2,128)} %bitcast.4, ...), custom_call_target="tpu_custom_call" | custom-call | flops 5000000000 | bytes 1048576 | tf_op jit(solution)/shard_map/moments/pallas_call | solution.py:335
  5.1 2.6 %collective-permute-start.1 = (bf16[4,3,64,128]{3,2,1,0:T(8,128)(2,1)}, bf16[4,3,64,128]{3,2,1,0:T(8,128)(2,1)S(1)}, u32[]{:S(2)}, u32[]{:S(2)}) collective-permute-start(bf16[4,3,64,128]{3,2,1,0:T(8,128)(2,1)} %get-tuple-element.28), channel_id=1, source_target_pairs={{0,16},{8,24},{16,0},{24,8},{1,17},{9,25},{17,1},{25,9},{2,18},{10... | collective-permute-start | bytes 589832 | tf_op jit(solution)/shard_map/ppermute | solution.py:371
  7.7 5.9 %collective-permute-done.1.rest_2_ = bf16[4,3,64,128]{3,2,1,0:T(8,128)(2,1)S(1)} collective-permute-done((bf16[4,3,64,128]{3,2,1,0:T(8,128)(2,1)}, bf16[4,3,64,128]{3,2,1,0:T(8,128)(2,1)S(1)}, u32[]{:S(2)}, u32[]{:S(2)}) %collective-permute-start.1) | collective-permute-done | bytes 196640 | tf_op jit(solution)/shard_map/ppermute | solution.py:371
  13.7 3.7 %collective-permute-done.2.rest_3_ = bf16[4,3,64,128]{3,2,1,0:T(8,128)(2,1)S(1)} collective-permute-done((bf16[4,3,64,128]{3,2,1,0:T(8,128)(2,1)}, bf16[4,3,64,128]{3,2,1,0:T(8,128)(2,1)S(1)}, u32[]{:S(2)}, u32[]{:S(2)}) %collective-permute-start.2) | collective-permute-done | bytes 196640 | tf_op jit(solution)/shard_map/ppermute | solution.py:371
  18.1 5.7 %forward_z.1 = (bf16[8,2,3,64,128]{4,3,2,1,0:T(8,128)(2,1)}, bf16[8,2,3,64,128]{4,3,2,1,0:T(8,128)(2,1)}) custom-call(bf16[4,3,64,128]{3,2,1,0:T(8,128)(2,1)} %get-tuple-element.26.rest_0_, bf16[4,3,64,128]{3,2,1,0:T(8,128)(2,1)} %copy-done.12, bf16[4,3,64,128]{3,2,1,0:T(8,128)(2,1)} %copy-done.14, bf16[4,3,64,128]{3,2,1,0:T(8,128)(2,1)} %copy-done.16), custom_call_target="tpu_custom_call" | custom-call | flops 4000000000 | bytes 1048576 | tf_op jit(solution)/shard_map/forward_z/pallas_call | solution.py:335
  23.7 26.4 %all_to_all.20.rest_0_ = bf16[8,2,3,64,128]{4,3,2,1,0:T(8,128)(2,1)S(1)} all-to-all(bf16[8,2,3,64,128]{4,3,2,1,0:T(8,128)(2,1)} %get-tuple-element.30), channel_id=1, replica_groups=mesh['zg'=4,'xy'=8] {'xy'}, dimensions={0} | all-to-all | bytes 1572864 | tf_op jit(solution)/shard_map/all_to_all | solution.py:419
  50.2 1.5 collective-permute-start.4
  51.6 3.6 %all-to-all-start.1 = ((bf16[8,2,3,64,128]{4,3,2,1,0:T(8,128)(2,1)}), bf16[8,2,3,64,128]{4,3,2,1,0:T(8,128)(2,1)S(1)}, u32[]{:S(2)}, u32[]{:S(2)}) async-start(bf16[8,2,3,64,128]{4,3,2,1,0:T(8,128)(2,1)} %get-tuple-element.32), calls=%async_computation.1 | async-start | bytes 1572864 | tf_op jit(solution)/shard_map/all_to_all | solution.py:419
  55.3 13.5 %collective-permute-done.4.rest_2_ = bf16[8,2,3,64,128]{4,3,2,1,0:T(8,128)(2,1)S(1)} collective-permute-done((bf16[8,2,3,64,128]{4,3,2,1,0:T(8,128)(2,1)S(1)}, bf16[8,2,3,64,128]{4,3,2,1,0:T(8,128)(2,1)S(1)}, u32[]{:S(2)}, u32[]{:S(2)}) %collective-permute-start.4) | collective-permute-done | bytes 786464 | tf_op jit(solution)/shard_map/ppermute | solution.py:371
  68.8 6.5 %all-to-all-done.1.rest_0_ = bf16[8,2,3,64,128]{4,3,2,1,0:T(8,128)(2,1)S(1)} async-done(((bf16[8,2,3,64,128]{4,3,2,1,0:T(8,128)(2,1)}), bf16[8,2,3,64,128]{4,3,2,1,0:T(8,128)(2,1)S(1)}, u32[]{:S(2)}, u32[]{:S(2)}) %all-to-all-start.1) | async-done | bytes 786464 | tf_op jit(solution)/shard_map/all_to_all | solution.py:419
  76.8 19.0 %middle.2 = (bf16[8,2,3,64,128]{4,3,2,1,0:T(8,128)(2,1)}, bf16[8,2,3,64,128]{4,3,2,1,0:T(8,128)(2,1)}, bf16[8,2,3,64,128]{4,3,2,1,0:T(8,128)(2,1)}, bf16[8,2,3,64,128]{4,3,2,1,0:T(8,128)(2,1)}) custom-call(f32[4,6]{1,0:T(4,128)} %bitcast.5, bf16[4,4,128,256]{3,2,1,0:T(8,128)(2,1)} %constant.8.clone.tabley_hbm, ...), custom_call_target="tpu_custom_call" | custom-call | flops 16000000000 | bytes 1048576 | tf_op jit(solution)/shard_map/middle/pallas_call | solution.py:335
  96.9 1.5 collective-permute-done.7
  98.3 1.4 add_convert_fusion.3
  99.8 1.6 collective-permute-start.8
  103.1 19.0 %middle.3 = (bf16[8,2,3,64,128]{4,3,2,1,0:T(8,128)(2,1)}, bf16[8,2,3,64,128]{4,3,2,1,0:T(8,128)(2,1)}, bf16[8,2,3,64,128]{4,3,2,1,0:T(8,128)(2,1)}, bf16[8,2,3,64,128]{4,3,2,1,0:T(8,128)(2,1)}) custom-call(f32[4,6]{1,0:T(4,128)} %bitcast.6, bf16[4,4,128,256]{3,2,1,0:T(8,128)(2,1)} %constant.8.clone.tabley_hbm, ...), custom_call_target="tpu_custom_call" | custom-call | flops 16000000000 | bytes 1048576 | tf_op jit(solution)/shard_map/middle/pallas_call | solution.py:335
  122.3 1.3 add_convert_fusion.2
  123.6 3.7 %all-to-all-start.2 = ((bf16[8,2,3,64,128]{4,3,2,1,0:T(8,128)(2,1)}), bf16[8,2,3,64,128]{4,3,2,1,0:T(8,128)(2,1)S(1)}, u32[]{:S(2)}, u32[]{:S(2)}) async-start(bf16[8,2,3,64,128]{4,3,2,1,0:T(8,128)(2,1)} %add_convert_fusion.2), calls=%async_computation.2 | async-start | bytes 1572864 | tf_op jit(solution)/shard_map/all_to_all | solution.py:419
  129.8 17.9 %collective-permute-done.14 = bf16[8,2,3,64,128]{4,3,2,1,0:T(8,128)(2,1)S(1)} collective-permute-done((bf16[8,2,3,64,128]{4,3,2,1,0:T(8,128)(2,1)S(1)}, bf16[8,2,3,64,128]{4,3,2,1,0:T(8,128)(2,1)S(1)}, u32[]{:S(2)}, u32[]{:S(2)}) %collective-permute-start.14) | collective-permute-done | bytes 786464 | tf_op jit(solution)/shard_map/ppermute | solution.py:371
  148.3 25.5 %all_to_all.21.rest_1_ = bf16[8,2,3,64,128]{4,3,2,1,0:T(8,128)(2,1)} all-to-all(bf16[8,2,3,64,128]{4,3,2,1,0:T(8,128)(2,1)S(1)} %add_convert_fusion), channel_id=1, replica_groups=mesh['zg'=4,'xy'=8] {'xy'}, dimensions={0} | all-to-all | bytes 1572864 | tf_op jit(solution)/shard_map/all_to_all | solution.py:419
  173.8 5.6 %inverse_z.1 = (bf16[4,3,64,128]{3,2,1,0:T(8,128)(2,1)}, bf16[4,3,64,128]{3,2,1,0:T(8,128)(2,1)}, bf16[4,3,64,128]{3,2,1,0:T(8,128)(2,1)}, bf16[4,3,64,128]{3,2,1,0:T(8,128)(2,1)}) custom-call(bf16[8,2,3,64,128]{4,3,2,1,0:T(8,128)(2,1)} %copy-done.1, bf16[8,2,3,64,128]{4,3,2,1,0:T(8,128)(2,1)} %all_to_all.21.rest_1_), custom_call_target="tpu_custom_call" | custom-call | flops 4000000000 | bytes 1048576 | tf_op jit(solution)/shard_map/inverse_z/pallas_call | solution.py:335
  180.0 1.3 collective-permute-start.17
  181.2 6.2 %collective-permute-done.16.rest_2_ = bf16[4,3,64,128]{3,2,1,0:T(8,128)(2,1)S(1)} collective-permute-done((bf16[4,3,64,128]{3,2,1,0:T(8,128)(2,1)}, bf16[4,3,64,128]{3,2,1,0:T(8,128)(2,1)S(1)}, u32[]{:S(2)}, u32[]{:S(2)}) %collective-permute-start.16) | collective-permute-done | bytes 196640 | tf_op jit(solution)/shard_map/ppermute | solution.py:371
  187.4 3.2 %collective-permute-done.17.rest_3_ = bf16[4,3,64,128]{3,2,1,0:T(8,128)(2,1)S(1)} collective-permute-done((bf16[4,3,64,128]{3,2,1,0:T(8,128)(2,1)}, bf16[4,3,64,128]{3,2,1,0:T(8,128)(2,1)S(1)}, u32[]{:S(2)}, u32[]{:S(2)}) %collective-permute-start.17) | collective-permute-done | bytes 196640 | tf_op jit(solution)/shard_map/ppermute | solution.py:371
  191.3 3.0 %result.1 = bf16[2,3,4,64,256]{4,3,2,1,0:T(8,128)(2,1)} custom-call(bf16[2,3,4,64,256]{4,3,2,1,0:T(8,128)(2,1)} %field_ref.3, bf16[64,64]{1,0:T(8,128)(2,1)} %constant.11.clone.order_ref, bf16[4,3,64,128]{3,2,1,0:T(8,128)(2,1)} %get-tuple-element.43.rest_0_, bf16[4,3,64,128]{3,2,1,0:T(8,128)(2,1)} %copy-done.13, bf16[4,3,64,128]{3,2,1,0:T(8,128)(2,1)} %copy-done.15, ...), custom_call_target="tpu_custom_call" | custom-call | flops 3000000000 | bytes 1048576 | tf_op jit(solution)/shard_map/result/pallas_call | solution.py:335
  (64 shorter events, 10.0 us)
Async XLA Ops:
  4.5 3.2 %collective-permute-start = (bf16[4,3,64,128]{3,2,1,0:T(8,128)(2,1)}, bf16[4,3,64,128]{3,2,1,0:T(8,128)(2,1)S(1)}, u32[]{:S(2)}, u32[]{:S(2)}) collective-permute-start(bf16[4,3,64,128]{3,2,1,0:T(8,128)(2,1)} %get-tuple-element.27), channel_id=1, source_target_pairs={{0,8},{8,0},{16,24},{24,16},{1,9},{9,1},{17,25},{25,17},{2,10},{10... | collective-permute-start | bytes 589832 | tf_op jit(solution)/shard_map/ppermute | solution.py:371
  5.1 8.5 %collective-permute-start.1 = (bf16[4,3,64,128]{3,2,1,0:T(8,128)(2,1)}, bf16[4,3,64,128]{3,2,1,0:T(8,128)(2,1)S(1)}, u32[]{:S(2)}, u32[]{:S(2)}) collective-permute-start(bf16[4,3,64,128]{3,2,1,0:T(8,128)(2,1)} %get-tuple-element.28), channel_id=1, source_target_pairs={{0,16},{8,24},{16,0},{24,8},{1,17},{9,25},{17,1},{25,9},{2,18},{10... | collective-permute-start | bytes 589832 | tf_op jit(solution)/shard_map/ppermute | solution.py:371
  7.7 9.7 %collective-permute-start.2 = (bf16[4,3,64,128]{3,2,1,0:T(8,128)(2,1)}, bf16[4,3,64,128]{3,2,1,0:T(8,128)(2,1)S(1)}, u32[]{:S(2)}, u32[]{:S(2)}) collective-permute-start(bf16[4,3,64,128]{3,2,1,0:T(8,128)(2,1)} %get-tuple-element.29), channel_id=1, source_target_pairs={{0,24},{8,16},{16,8},{24,0},{1,25},{9,17},{17,9},{25,1},{2,26},{10... | collective-permute-start | bytes 589832 | tf_op jit(solution)/shard_map/ppermute | solution.py:371
  50.1 25.7 %copy-start.2 = (bf16[8,2,3,64,128]{4,3,2,1,0:T(8,128)(2,1)}, bf16[8,2,3,64,128]{4,3,2,1,0:T(8,128)(2,1)S(1)}, u32[]{:S(2)}) copy-start(bf16[8,2,3,64,128]{4,3,2,1,0:T(8,128)(2,1)S(1)} %all_to_all.20.rest_0_) | copy-start | bytes 2359300
  50.2 18.7 %collective-permute-start.4 = (bf16[8,2,3,64,128]{4,3,2,1,0:T(8,128)(2,1)S(1)}, bf16[8,2,3,64,128]{4,3,2,1,0:T(8,128)(2,1)S(1)}, u32[]{:S(2)}, u32[]{:S(2)}) collective-permute-start(bf16[8,2,3,64,128]{4,3,2,1,0:T(8,128)(2,1)S(1)} %all_to_all.20.rest_0_), channel_id=1, source_target_pairs={{0,16},{8,24},{16,0},{24,8},{1,17},{9,25},{17,1},{25,9},{2,18},{10... | collective-permute-start | bytes 2359304 | tf_op jit(solution)/shard_map/ppermute | solution.py:371
  51.6 23.7 %all-to-all-start.1 = ((bf16[8,2,3,64,128]{4,3,2,1,0:T(8,128)(2,1)}), bf16[8,2,3,64,128]{4,3,2,1,0:T(8,128)(2,1)S(1)}, u32[]{:S(2)}, u32[]{:S(2)}) async-start(bf16[8,2,3,64,128]{4,3,2,1,0:T(8,128)(2,1)} %get-tuple-element.32), calls=%async_computation.1 | async-start | bytes 1572864 | tf_op jit(solution)/shard_map/all_to_all | solution.py:419
  55.3 20.6 %collective-permute-start.3 = (bf16[8,2,3,64,128]{4,3,2,1,0:T(8,128)(2,1)S(1)}, bf16[8,2,3,64,128]{4,3,2,1,0:T(8,128)(2,1)S(1)}, u32[]{:S(2)}, u32[]{:S(2)}) collective-permute-start(bf16[8,2,3,64,128]{4,3,2,1,0:T(8,128)(2,1)S(1)} %all_to_all.20.rest_0_), channel_id=1, source_target_pairs={{0,8},{8,0},{16,24},{24,16},{1,9},{9,1},{17,25},{25,17},{2,10},{10... | collective-permute-start | bytes 2359304 | tf_op jit(solution)/shard_map/ppermute | solution.py:371
  68.8 7.1 %collective-permute-start.5 = (bf16[8,2,3,64,128]{4,3,2,1,0:T(8,128)(2,1)S(1)}, bf16[8,2,3,64,128]{4,3,2,1,0:T(8,128)(2,1)}, u32[]{:S(2)}, u32[]{:S(2)}) collective-permute-start(bf16[8,2,3,64,128]{4,3,2,1,0:T(8,128)(2,1)S(1)} %collective-permute-done.4.rest_2_), channel_id=1, source_target_pairs={{0,8},{8,0},{16,24},{24,16},{1,9},{9,1},{17,25},{25,17},{2,10},{10... | collective-permute-start | bytes 2359304 | tf_op jit(solution)/shard_map/ppermute | solution.py:371
  75.3 20.5 %copy-start = (bf16[8,2,3,64,128]{4,3,2,1,0:T(8,128)(2,1)}, bf16[8,2,3,64,128]{4,3,2,1,0:T(8,128)(2,1)S(1)}, u32[]{:S(2)}) copy-start(bf16[8,2,3,64,128]{4,3,2,1,0:T(8,128)(2,1)S(1)} %all-to-all-done.1.rest_0_) | copy-start | bytes 2359300
  75.3 21.0 %collective-permute-start.10 = (bf16[8,2,3,64,128]{4,3,2,1,0:T(8,128)(2,1)S(1)}, bf16[8,2,3,64,128]{4,3,2,1,0:T(8,128)(2,1)S(1)}, u32[]{:S(2)}, u32[]{:S(2)}) collective-permute-start(bf16[8,2,3,64,128]{4,3,2,1,0:T(8,128)(2,1)S(1)} %all-to-all-done.1.rest_0_), channel_id=1, source_target_pairs={{0,16},{8,24},{16,0},{24,8},{1,17},{9,25},{17,1},{25,9},{2,18},{10... | collective-permute-start | bytes 2359304 | tf_op jit(solution)/shard_map/ppermute | solution.py:371
  95.8 2.6 %collective-permute-start.7 = (bf16[8,2,3,64,128]{4,3,2,1,0:T(8,128)(2,1)}, bf16[8,2,3,64,128]{4,3,2,1,0:T(8,128)(2,1)S(1)}, u32[]{:S(2)}, u32[]{:S(2)}) collective-permute-start(bf16[8,2,3,64,128]{4,3,2,1,0:T(8,128)(2,1)} %get-tuple-element.37), channel_id=1, source_target_pairs={{0,8},{8,0},{16,24},{24,16},{1,9},{9,1},{17,25},{25,17},{2,10},{10... | collective-permute-start | bytes 2359304 | tf_op jit(solution)/shard_map/ppermute | solution.py:371
  95.9 5.5 %collective-permute-start.9 = (bf16[8,2,3,64,128]{4,3,2,1,0:T(8,128)(2,1)S(1)}, bf16[8,2,3,64,128]{4,3,2,1,0:T(8,128)(2,1)S(1)}, u32[]{:S(2)}, u32[]{:S(2)}) collective-permute-start(bf16[8,2,3,64,128]{4,3,2,1,0:T(8,128)(2,1)S(1)} %all-to-all-done.1.rest_0_), channel_id=1, source_target_pairs={{0,8},{8,0},{16,24},{24,16},{1,9},{9,1},{17,25},{25,17},{2,10},{10... | collective-permute-start | bytes 2359304 | tf_op jit(solution)/shard_map/ppermute | solution.py:371
  96.4 5.0 %collective-permute-start.11 = (bf16[8,2,3,64,128]{4,3,2,1,0:T(8,128)(2,1)S(1)}, bf16[8,2,3,64,128]{4,3,2,1,0:T(8,128)(2,1)S(1)}, u32[]{:S(2)}, u32[]{:S(2)}) collective-permute-start(bf16[8,2,3,64,128]{4,3,2,1,0:T(8,128)(2,1)S(1)} %collective-permute-done.10.rest_2_), channel_id=1, source_target_pairs={{0,8},{8,0},{16,24},{24,16},{1,9},{9,1},{17,25},{25,17},{2,10},{10... | collective-permute-start | bytes 2359304 | tf_op jit(solution)/shard_map/ppermute | solution.py:371
  96.5 25.8 %collective-permute-start.6 = (bf16[8,2,3,64,128]{4,3,2,1,0:T(8,128)(2,1)}, bf16[8,2,3,64,128]{4,3,2,1,0:T(8,128)(2,1)S(1)}, u32[]{:S(2)}, u32[]{:S(2)}) collective-permute-start(bf16[8,2,3,64,128]{4,3,2,1,0:T(8,128)(2,1)} %get-tuple-element.35), channel_id=1, source_target_pairs={{0,8},{8,0},{16,24},{24,16},{1,9},{9,1},{17,25},{25,17},{2,10},{10... | collective-permute-start | bytes 2359304 | tf_op jit(solution)/shard_map/ppermute | solution.py:371
  99.8 22.5 %copy-start.3 = (bf16[8,2,3,64,128]{4,3,2,1,0:T(8,128)(2,1)S(1)}, bf16[8,2,3,64,128]{4,3,2,1,0:T(8,128)(2,1)}, u32[]{:S(2)}) copy-start(bf16[8,2,3,64,128]{4,3,2,1,0:T(8,128)(2,1)} %get-tuple-element.34) | copy-start | bytes 2359300
  99.8 22.5 %collective-permute-start.8 = (bf16[8,2,3,64,128]{4,3,2,1,0:T(8,128)(2,1)S(1)}, bf16[8,2,3,64,128]{4,3,2,1,0:T(8,128)(2,1)S(1)}, u32[]{:S(2)}, u32[]{:S(2)}) collective-permute-start(bf16[8,2,3,64,128]{4,3,2,1,0:T(8,128)(2,1)S(1)} %add_convert_fusion.3), channel_id=1, source_target_pairs={{0,16},{8,24},{16,0},{24,8},{1,17},{9,25},{17,1},{25,9},{2,18},{10... | collective-permute-start | bytes 2359304 | tf_op jit(solution)/shard_map/ppermute | solution.py:371
  122.2 5.7 %collective-permute-start.13 = (bf16[8,2,3,64,128]{4,3,2,1,0:T(8,128)(2,1)}, bf16[8,2,3,64,128]{4,3,2,1,0:T(8,128)(2,1)S(1)}, u32[]{:S(2)}, u32[]{:S(2)}) collective-permute-start(bf16[8,2,3,64,128]{4,3,2,1,0:T(8,128)(2,1)} %get-tuple-element.41), channel_id=1, source_target_pairs={{0,8},{8,0},{16,24},{24,16},{1,9},{9,1},{17,25},{25,17},{2,10},{10... | collective-permute-start | bytes 2359304 | tf_op jit(solution)/shard_map/ppermute | solution.py:371
  123.6 24.7 %all-to-all-start.2 = ((bf16[8,2,3,64,128]{4,3,2,1,0:T(8,128)(2,1)}), bf16[8,2,3,64,128]{4,3,2,1,0:T(8,128)(2,1)S(1)}, u32[]{:S(2)}, u32[]{:S(2)}) async-start(bf16[8,2,3,64,128]{4,3,2,1,0:T(8,128)(2,1)} %add_convert_fusion.2), calls=%async_computation.2 | async-start | bytes 1572864 | tf_op jit(solution)/shard_map/all_to_all | solution.py:419
  127.3 2.5 %collective-permute-start.12 = (bf16[8,2,3,64,128]{4,3,2,1,0:T(8,128)(2,1)S(1)}, bf16[8,2,3,64,128]{4,3,2,1,0:T(8,128)(2,1)S(1)}, u32[]{:S(2)}, u32[]{:S(2)}) collective-permute-start(bf16[8,2,3,64,128]{4,3,2,1,0:T(8,128)(2,1)S(1)} %copy-done.7), channel_id=1, source_target_pairs={{0,8},{8,0},{16,24},{24,16},{1,9},{9,1},{17,25},{25,17},{2,10},{10... | collective-permute-start | bytes 2359304 | tf_op jit(solution)/shard_map/ppermute | solution.py:371
  128.2 19.5 %collective-permute-start.14 = (bf16[8,2,3,64,128]{4,3,2,1,0:T(8,128)(2,1)S(1)}, bf16[8,2,3,64,128]{4,3,2,1,0:T(8,128)(2,1)S(1)}, u32[]{:S(2)}, u32[]{:S(2)}) collective-permute-start(bf16[8,2,3,64,128]{4,3,2,1,0:T(8,128)(2,1)S(1)} %add_convert_fusion.1), channel_id=1, source_target_pairs={{0,16},{8,24},{16,0},{24,8},{1,17},{9,25},{17,1},{25,9},{2,18},{10... | collective-permute-start | bytes 2359304 | tf_op jit(solution)/shard_map/ppermute | solution.py:371
  148.3 25.5 %copy-start.1 = (bf16[8,2,3,64,128]{4,3,2,1,0:T(8,128)(2,1)}, bf16[8,2,3,64,128]{4,3,2,1,0:T(8,128)(2,1)S(1)}, u32[]{:S(2)}) copy-start(bf16[8,2,3,64,128]{4,3,2,1,0:T(8,128)(2,1)S(1)} %all-to-all-done.2.rest_0_) | copy-start | bytes 2359300
  179.4 1.9 collective-permute-start.15
  179.4 8.0 %collective-permute-start.16 = (bf16[4,3,64,128]{3,2,1,0:T(8,128)(2,1)}, bf16[4,3,64,128]{3,2,1,0:T(8,128)(2,1)S(1)}, u32[]{:S(2)}, u32[]{:S(2)}) collective-permute-start(bf16[4,3,64,128]{3,2,1,0:T(8,128)(2,1)} %get-tuple-element.45), channel_id=1, source_target_pairs={{0,16},{8,24},{16,0},{24,8},{1,17},{9,25},{17,1},{25,9},{2,18},{10... | collective-permute-start | bytes 589832 | tf_op jit(solution)/shard_map/ppermute | solution.py:371
  180.0 10.6 %collective-permute-start.17 = (bf16[4,3,64,128]{3,2,1,0:T(8,128)(2,1)}, bf16[4,3,64,128]{3,2,1,0:T(8,128)(2,1)S(1)}, u32[]{:S(2)}, u32[]{:S(2)}) collective-permute-start(bf16[4,3,64,128]{3,2,1,0:T(8,128)(2,1)} %get-tuple-element.46), channel_id=1, source_target_pairs={{0,24},{8,16},{16,8},{24,0},{1,25},{9,17},{17,9},{25,1},{2,26},{10... | collective-permute-start | bytes 589832 | tf_op jit(solution)/shard_map/ppermute | solution.py:371
  (14 other events, 70.3 us)

commit v3 on v2

--- a/solution.py
+++ b/solution.py
@@ -57,28 +57,42 @@
     return pltpu.roll(value, value.shape[-1] // 2, 1)
 
 
-def times(value, angle, low):
+def opened(value, low):
+    half = value.shape[0] // 2
+    a, b = value[:half], value[half:]
+    return jnp.where(low, a, swapped(b)), jnp.where(low, swapped(a), b)
+
+
+def closed(pair, low):
+    re, im = pair
+    return jnp.concatenate([jnp.where(low, re, swapped(im)), jnp.where(low, swapped(re), im)], axis=0)
+
+
+def plus(a, b):
+    return a[0] + b[0], a[1] + b[1]
+
+
+def minus(a, b):
+    return a[0] - b[0], a[1] - b[1]
+
+
+def times(pair, angle):
+    re, im = pair
     turn = round(angle / (math.pi / 2.0), 9) % 4
-    if turn == 0:
-        return value
-    if turn == 2:
-        return -value
-    other = swapped(value)
-    if turn in (1, 3):
-        s = 1.0 if turn == 1 else -1.0
-        return other * jnp.where(low, -s, s)
+    if turn in (0, 1, 2, 3):
+        return ((re, im), (-im, re), (-re, -im), (im, -re))[int(turn)]
     c, s = math.cos(angle), math.sin(angle)
-    return value * c + other * jnp.where(low, -s, s)
-
-
-def transform_list(values, sign, low):
+    return re * c - im * s, re * s + im * c
+
+
+def transform_list(values, sign):
     n = len(values)
     if n == 1:
         return values
-    even = transform_list(values[0::2], sign, low)
-    odd = transform_list(values[1::2], sign, low)
-    odd = [times(v, sign * 2.0 * math.pi * k / n, low) for k, v in enumerate(odd)]
-    return [e + o for e, o in zip(even, odd)] + [e - o for e, o in zip(even, odd)]
+    even = transform_list(values[0::2], sign)
+    odd = transform_list(values[1::2], sign)
+    odd = [times(v, sign * 2.0 * math.pi * k / n) for k, v in enumerate(odd)]
+    return [plus(e, o) for e, o in zip(even, odd)] + [minus(e, o) for e, o in zip(even, odd)]
 
 
 def moments_kernel(alpha_ref, field_ref, material_ref, order_ref, *rest, groups, counts):
@@ -130,26 +144,28 @@
     for s in range(groups):
         source[me ^ s] = pieces[s][...]
     tile = min(16, rows)
-    low = lax.broadcasted_iota(jnp.int32, (tile, lanes), 1) < lanes // 2
+    low = lax.broadcasted_iota(jnp.int32, (tile // 2, lanes), 1) < lanes // 2
 
     def step(n, carry):
         top = pl.multiple_of(n * tile, tile)
 
         def values():
-            return [source[z // planes, z % planes, pl.ds(top, tile), :].astype(f32) for z in range(total)]
+            return [
+                opened(source[z // planes, z % planes, pl.ds(top, tile), :].astype(f32), low) for z in range(total)
+            ]
 
         def keep(k, v):
             chunk, place = places[k % held]
-            outs[chunk][k // held, place, pl.ds(top, tile), :] = v.astype(bf16)
-
-        for k, v in enumerate(transform_list(values(), -1.0, low)):
+            outs[chunk][k // held, place, pl.ds(top, tile), :] = closed(v, low).astype(bf16)
+
+        for k, v in enumerate(transform_list(values(), -1.0)):
             keep(2 * k, v)
-        turned = [times(v, -2.0 * math.pi * z / (2 * total), low) for z, v in enumerate(values())]
-        for k, v in enumerate(transform_list(turned, -1.0, low)):
+        turned = [times(v, -2.0 * math.pi * z / (2 * total)) for z, v in enumerate(values())]
+        for k, v in enumerate(transform_list(turned, -1.0)):
             keep(2 * k + 1, v)
         return carry
 
-    lax.fori_loop(0, rows // tile, step, 0)
+    lax.fori_loop(0, rows // tile, step, 0, unroll=2 if rows > tile else 1)
 
 
 def inverse_z_kernel(*rest, groups, places, chunks):
@@ -161,23 +177,23 @@
     total = members * held // 2
     planes = total // groups
     tile = min(16, rows)
-    low = lax.broadcasted_iota(jnp.int32, (tile, lanes), 1) < lanes // 2
+    low = lax.broadcasted_iota(jnp.int32, (tile // 2, lanes), 1) < lanes // 2
 
     def step(n, carry):
         top = pl.multiple_of(n * tile, tile)
 
         def value(k):
             chunk, place = places[k % held]
-            return pieces[chunk][k // held, place, pl.ds(top, tile), :].astype(f32)
-
-        even = transform_list([value(k) for k in range(0, 2 * total, 2)], 1.0, low)
-        odd = transform_list([value(k) for k in range(1, 2 * total, 2)], 1.0, low)
+            return opened(pieces[chunk][k // held, place, pl.ds(top, tile), :].astype(f32), low)
+
+        even = transform_list([value(k) for k in range(0, 2 * total, 2)], 1.0)
+        odd = transform_list([value(k) for k in range(1, 2 * total, 2)], 1.0)
         for z in range(total):
-            v = even[z] + times(odd[z], 2.0 * math.pi * z / (2 * total), low)
-            target[z // planes, z % planes, pl.ds(top, tile), :] = v.astype(bf16)
+            v = plus(even[z], times(odd[z], 2.0 * math.pi * z / (2 * total)))
+            target[z // planes, z % planes, pl.ds(top, tile), :] = closed(v, low).astype(bf16)
         return carry
 
-    lax.fori_loop(0, rows // tile, step, 0)
+    lax.fori_loop(0, rows // tile, step, 0, unroll=2 if rows > tile else 1)
     for s in range(groups):
         outs[s][...] = target[me ^ s]
 
@@ -228,7 +244,7 @@
             wide[j, p] = jnp.dot(forward[p], spread[j, p], preferred_element_type=f32)
     load.wait()
     many = wide.shape[2] // 2
-    tile = 16
+    tile = 32
 
     def step(n, carry):
         top = pl.multiple_of(n * tile, tile)

time: 195 us -> 192 us (0.985)
  Pallas kernels: 56.8 us -> 54.1 us
    pallas_call x6, Pallas kernels: 56.8 us -> 54.1 us  [call(): pl.pallas_call(kernel, grid=grid, in_specs=specs, out_specs=(out_spec if...]
where the time goes in v3:
time: 192 us
  waiting for transfers between devices  59.6 us (31%)
  Pallas kernels  54.1 us (28%)
  blocking collectives  51.9 us (27%)
  starting transfers between devices  18.3 us (10%)
  local copies, waits for them, and re-layouts  4.02 us (2%)
  other arithmetic  3.46 us (2%)
    pallas_call x6, Pallas kernels, call(): pl.pallas_call(kernel, grid=grid, in_specs=specs, out_specs=(out_spec if...  54.1 us
    ppermute x18, waiting for transfers between devices, send(): return lax.ppermute(value, axis, [(i, i ^ distance) for i in range(size)])  52.9 us
    all_to_all x2, blocking collectives, across(): return lax.all_to_all(value, 'xy', 0, 0, tiled=True)  51.9 us
    ppermute x18, starting transfers between devices, send(): return lax.ppermute(value, axis, [(i, i ^ distance) for i in range(size)])  10.9 us
    all_to_all x2, starting transfers between devices, across(): return lax.all_to_all(value, 'xy', 0, 0, tiled=True)  7.32 us
    all_to_all x2, waiting for transfers between devices, across(): return lax.all_to_all(value, 'xy', 0, 0, tiled=True)  6.68 us
    unnamed x36, local copies, waits for them, and re-layouts  4.02 us
  transfers between devices with their start and end apart: 20, of which 10 were waited for; matrix products, arithmetic and copies ran while one was open for 2% of the time, Pallas kernels for 20%

profile of v3, /device:TPU:0, one launch (start us, length us, event | category | flops | bytes accessed | tf_op | source)
XLA Modules:
  0.0 191.5 jit_solution(15746667542076914261)
XLA Ops:
  0.0 4.5 %moments.1 = (bf16[4,3,64,128]{3,2,1,0:T(8,128)(2,1)}, bf16[4,3,64,128]{3,2,1,0:T(8,128)(2,1)}, bf16[4,3,64,128]{3,2,1,0:T(8,128)(2,1)}, bf16[4,3,64,128]{3,2,1,0:T(8,128)(2,1)}) custom-call(f32[3,3,2,4]{3,2,1,0:T(2,128)} %bitcast.3, bf16[2,3,4,64,256]{4,3,2,1,0:T(8,128)(2,1)} %field_ref.3, s32[4,2,64]{2,1,0:T(2,128)} %bitcast.4, ...), custom_call_target="tpu_custom_call" | custom-call | flops 5000000000 | bytes 1048576 | tf_op jit(solution)/shard_map/moments/pallas_call | solution.py:351
  5.1 2.6 %collective-permute-start.1 = (bf16[4,3,64,128]{3,2,1,0:T(8,128)(2,1)}, bf16[4,3,64,128]{3,2,1,0:T(8,128)(2,1)S(1)}, u32[]{:S(2)}, u32[]{:S(2)}) collective-permute-start(bf16[4,3,64,128]{3,2,1,0:T(8,128)(2,1)} %get-tuple-element.28), channel_id=1, source_target_pairs={{0,16},{8,24},{16,0},{24,8},{1,17},{9,25},{17,1},{25,9},{2,18},{10... | collective-permute-start | bytes 589832 | tf_op jit(solution)/shard_map/ppermute | solution.py:387
  7.7 5.9 %collective-permute-done.1.rest_2_ = bf16[4,3,64,128]{3,2,1,0:T(8,128)(2,1)S(1)} collective-permute-done((bf16[4,3,64,128]{3,2,1,0:T(8,128)(2,1)}, bf16[4,3,64,128]{3,2,1,0:T(8,128)(2,1)S(1)}, u32[]{:S(2)}, u32[]{:S(2)}) %collective-permute-start.1) | collective-permute-done | bytes 196640 | tf_op jit(solution)/shard_map/ppermute | solution.py:387
  13.7 3.7 %collective-permute-done.2.rest_3_ = bf16[4,3,64,128]{3,2,1,0:T(8,128)(2,1)S(1)} collective-permute-done((bf16[4,3,64,128]{3,2,1,0:T(8,128)(2,1)}, bf16[4,3,64,128]{3,2,1,0:T(8,128)(2,1)S(1)}, u32[]{:S(2)}, u32[]{:S(2)}) %collective-permute-start.2) | collective-permute-done | bytes 196640 | tf_op jit(solution)/shard_map/ppermute | solution.py:387
  18.1 4.5 %forward_z.1 = (bf16[8,2,3,64,128]{4,3,2,1,0:T(8,128)(2,1)}, bf16[8,2,3,64,128]{4,3,2,1,0:T(8,128)(2,1)}) custom-call(bf16[4,3,64,128]{3,2,1,0:T(8,128)(2,1)} %get-tuple-element.26.rest_0_, bf16[4,3,64,128]{3,2,1,0:T(8,128)(2,1)} %copy-done.12, bf16[4,3,64,128]{3,2,1,0:T(8,128)(2,1)} %copy-done.14, bf16[4,3,64,128]{3,2,1,0:T(8,128)(2,1)} %copy-done.16), custom_call_target="tpu_custom_call" | custom-call | flops 4000000000 | bytes 1048576 | tf_op jit(solution)/shard_map/forward_z/pallas_call | solution.py:351
  22.6 26.4 %all_to_all.20.rest_0_ = bf16[8,2,3,64,128]{4,3,2,1,0:T(8,128)(2,1)S(1)} all-to-all(bf16[8,2,3,64,128]{4,3,2,1,0:T(8,128)(2,1)} %get-tuple-element.30), channel_id=1, replica_groups=mesh['zg'=4,'xy'=8] {'xy'}, dimensions={0} | all-to-all | bytes 1572864 | tf_op jit(solution)/shard_map/all_to_all | solution.py:435
  49.0 1.5 collective-permute-start.4
  50.5 3.6 %all-to-all-start.1 = ((bf16[8,2,3,64,128]{4,3,2,1,0:T(8,128)(2,1)}), bf16[8,2,3,64,128]{4,3,2,1,0:T(8,128)(2,1)S(1)}, u32[]{:S(2)}, u32[]{:S(2)}) async-start(bf16[8,2,3,64,128]{4,3,2,1,0:T(8,128)(2,1)} %get-tuple-element.32), calls=%async_computation.1 | async-start | bytes 1572864 | tf_op jit(solution)/shard_map/all_to_all | solution.py:435
  54.2 13.5 %collective-permute-done.4.rest_2_ = bf16[8,2,3,64,128]{4,3,2,1,0:T(8,128)(2,1)S(1)} collective-permute-done((bf16[8,2,3,64,128]{4,3,2,1,0:T(8,128)(2,1)S(1)}, bf16[8,2,3,64,128]{4,3,2,1,0:T(8,128)(2,1)S(1)}, u32[]{:S(2)}, u32[]{:S(2)}) %collective-permute-start.4) | collective-permute-done | bytes 786464 | tf_op jit(solution)/shard_map/ppermute | solution.py:387
  67.7 6.5 %all-to-all-done.1.rest_0_ = bf16[8,2,3,64,128]{4,3,2,1,0:T(8,128)(2,1)S(1)} async-done(((bf16[8,2,3,64,128]{4,3,2,1,0:T(8,128)(2,1)}), bf16[8,2,3,64,128]{4,3,2,1,0:T(8,128)(2,1)S(1)}, u32[]{:S(2)}, u32[]{:S(2)}) %all-to-all-start.1) | async-done | bytes 786464 | tf_op jit(solution)/shard_map/all_to_all | solution.py:435
  75.6 18.8 %middle.2 = (bf16[8,2,3,64,128]{4,3,2,1,0:T(8,128)(2,1)}, bf16[8,2,3,64,128]{4,3,2,1,0:T(8,128)(2,1)}, bf16[8,2,3,64,128]{4,3,2,1,0:T(8,128)(2,1)}, bf16[8,2,3,64,128]{4,3,2,1,0:T(8,128)(2,1)}) custom-call(f32[4,6]{1,0:T(4,128)} %bitcast.5, bf16[4,4,128,256]{3,2,1,0:T(8,128)(2,1)} %constant.8.clone.tabley_hbm, ...), custom_call_target="tpu_custom_call" | custom-call | flops 16000000000 | bytes 1048576 | tf_op jit(solution)/shard_map/middle/pallas_call | solution.py:351
  95.6 1.5 collective-permute-done.7
  97.0 1.4 add_convert_fusion.3
  98.5 1.6 collective-permute-start.8
  101.8 18.9 %middle.3 = (bf16[8,2,3,64,128]{4,3,2,1,0:T(8,128)(2,1)}, bf16[8,2,3,64,128]{4,3,2,1,0:T(8,128)(2,1)}, bf16[8,2,3,64,128]{4,3,2,1,0:T(8,128)(2,1)}, bf16[8,2,3,64,128]{4,3,2,1,0:T(8,128)(2,1)}) custom-call(f32[4,6]{1,0:T(4,128)} %bitcast.6, bf16[4,4,128,256]{3,2,1,0:T(8,128)(2,1)} %constant.8.clone.tabley_hbm, ...), custom_call_target="tpu_custom_call" | custom-call | flops 16000000000 | bytes 1048576 | tf_op jit(solution)/shard_map/middle/pallas_call | solution.py:351
  120.8 1.3 add_convert_fusion.2
  122.1 3.7 %all-to-all-start.2 = ((bf16[8,2,3,64,128]{4,3,2,1,0:T(8,128)(2,1)}), bf16[8,2,3,64,128]{4,3,2,1,0:T(8,128)(2,1)S(1)}, u32[]{:S(2)}, u32[]{:S(2)}) async-start(bf16[8,2,3,64,128]{4,3,2,1,0:T(8,128)(2,1)} %add_convert_fusion.2), calls=%async_computation.2 | async-start | bytes 1572864 | tf_op jit(solution)/shard_map/all_to_all | solution.py:435
  128.3 17.9 %collective-permute-done.14 = bf16[8,2,3,64,128]{4,3,2,1,0:T(8,128)(2,1)S(1)} collective-permute-done((bf16[8,2,3,64,128]{4,3,2,1,0:T(8,128)(2,1)S(1)}, bf16[8,2,3,64,128]{4,3,2,1,0:T(8,128)(2,1)S(1)}, u32[]{:S(2)}, u32[]{:S(2)}) %collective-permute-start.14) | collective-permute-done | bytes 786464 | tf_op jit(solution)/shard_map/ppermute | solution.py:387
  146.8 25.5 %all_to_all.21.rest_1_ = bf16[8,2,3,64,128]{4,3,2,1,0:T(8,128)(2,1)} all-to-all(bf16[8,2,3,64,128]{4,3,2,1,0:T(8,128)(2,1)S(1)} %add_convert_fusion), channel_id=1, replica_groups=mesh['zg'=4,'xy'=8] {'xy'}, dimensions={0} | all-to-all | bytes 1572864 | tf_op jit(solution)/shard_map/all_to_all | solution.py:435
  172.3 4.3 %inverse_z.1 = (bf16[4,3,64,128]{3,2,1,0:T(8,128)(2,1)}, bf16[4,3,64,128]{3,2,1,0:T(8,128)(2,1)}, bf16[4,3,64,128]{3,2,1,0:T(8,128)(2,1)}, bf16[4,3,64,128]{3,2,1,0:T(8,128)(2,1)}) custom-call(bf16[8,2,3,64,128]{4,3,2,1,0:T(8,128)(2,1)} %copy-done.1, bf16[8,2,3,64,128]{4,3,2,1,0:T(8,128)(2,1)} %all_to_all.21.rest_1_), custom_call_target="tpu_custom_call" | custom-call | flops 4000000000 | bytes 1048576 | tf_op jit(solution)/shard_map/inverse_z/pallas_call | solution.py:351
  177.2 1.3 collective-permute-start.17
  178.5 6.2 %collective-permute-done.16.rest_2_ = bf16[4,3,64,128]{3,2,1,0:T(8,128)(2,1)S(1)} collective-permute-done((bf16[4,3,64,128]{3,2,1,0:T(8,128)(2,1)}, bf16[4,3,64,128]{3,2,1,0:T(8,128)(2,1)S(1)}, u32[]{:S(2)}, u32[]{:S(2)}) %collective-permute-start.16) | collective-permute-done | bytes 196640 | tf_op jit(solution)/shard_map/ppermute | solution.py:387
  184.7 3.2 %collective-permute-done.17.rest_3_ = bf16[4,3,64,128]{3,2,1,0:T(8,128)(2,1)S(1)} collective-permute-done((bf16[4,3,64,128]{3,2,1,0:T(8,128)(2,1)}, bf16[4,3,64,128]{3,2,1,0:T(8,128)(2,1)S(1)}, u32[]{:S(2)}, u32[]{:S(2)}) %collective-permute-start.17) | collective-permute-done | bytes 196640 | tf_op jit(solution)/shard_map/ppermute | solution.py:387
  188.5 3.0 %result.1 = bf16[2,3,4,64,256]{4,3,2,1,0:T(8,128)(2,1)} custom-call(bf16[2,3,4,64,256]{4,3,2,1,0:T(8,128)(2,1)} %field_ref.3, bf16[64,64]{1,0:T(8,128)(2,1)} %constant.11.clone.order_ref, bf16[4,3,64,128]{3,2,1,0:T(8,128)(2,1)} %get-tuple-element.43.rest_0_, bf16[4,3,64,128]{3,2,1,0:T(8,128)(2,1)} %copy-done.13, bf16[4,3,64,128]{3,2,1,0:T(8,128)(2,1)} %copy-done.15, ...), custom_call_target="tpu_custom_call" | custom-call | flops 3000000000 | bytes 1048576 | tf_op jit(solution)/shard_map/result/pallas_call | solution.py:351
  (64 shorter events, 9.9 us)
Async XLA Ops:
  4.5 3.2 %collective-permute-start = (bf16[4,3,64,128]{3,2,1,0:T(8,128)(2,1)}, bf16[4,3,64,128]{3,2,1,0:T(8,128)(2,1)S(1)}, u32[]{:S(2)}, u32[]{:S(2)}) collective-permute-start(bf16[4,3,64,128]{3,2,1,0:T(8,128)(2,1)} %get-tuple-element.27), channel_id=1, source_target_pairs={{0,8},{8,0},{16,24},{24,16},{1,9},{9,1},{17,25},{25,17},{2,10},{10... | collective-permute-start | bytes 589832 | tf_op jit(solution)/shard_map/ppermute | solution.py:387
  5.1 8.5 %collective-permute-start.1 = (bf16[4,3,64,128]{3,2,1,0:T(8,128)(2,1)}, bf16[4,3,64,128]{3,2,1,0:T(8,128)(2,1)S(1)}, u32[]{:S(2)}, u32[]{:S(2)}) collective-permute-start(bf16[4,3,64,128]{3,2,1,0:T(8,128)(2,1)} %get-tuple-element.28), channel_id=1, source_target_pairs={{0,16},{8,24},{16,0},{24,8},{1,17},{9,25},{17,1},{25,9},{2,18},{10... | collective-permute-start | bytes 589832 | tf_op jit(solution)/shard_map/ppermute | solution.py:387
  7.7 9.7 %collective-permute-start.2 = (bf16[4,3,64,128]{3,2,1,0:T(8,128)(2,1)}, bf16[4,3,64,128]{3,2,1,0:T(8,128)(2,1)S(1)}, u32[]{:S(2)}, u32[]{:S(2)}) collective-permute-start(bf16[4,3,64,128]{3,2,1,0:T(8,128)(2,1)} %get-tuple-element.29), channel_id=1, source_target_pairs={{0,24},{8,16},{16,8},{24,0},{1,25},{9,17},{17,9},{25,1},{2,26},{10... | collective-permute-start | bytes 589832 | tf_op jit(solution)/shard_map/ppermute | solution.py:387
  49.0 25.7 %copy-start.2 = (bf16[8,2,3,64,128]{4,3,2,1,0:T(8,128)(2,1)}, bf16[8,2,3,64,128]{4,3,2,1,0:T(8,128)(2,1)S(1)}, u32[]{:S(2)}) copy-start(bf16[8,2,3,64,128]{4,3,2,1,0:T(8,128)(2,1)S(1)} %all_to_all.20.rest_0_) | copy-start | bytes 2359300
  49.0 18.7 %collective-permute-start.4 = (bf16[8,2,3,64,128]{4,3,2,1,0:T(8,128)(2,1)S(1)}, bf16[8,2,3,64,128]{4,3,2,1,0:T(8,128)(2,1)S(1)}, u32[]{:S(2)}, u32[]{:S(2)}) collective-permute-start(bf16[8,2,3,64,128]{4,3,2,1,0:T(8,128)(2,1)S(1)} %all_to_all.20.rest_0_), channel_id=1, source_target_pairs={{0,16},{8,24},{16,0},{24,8},{1,17},{9,25},{17,1},{25,9},{2,18},{10... | collective-permute-start | bytes 2359304 | tf_op jit(solution)/shard_map/ppermute | solution.py:387
  50.5 23.7 %all-to-all-start.1 = ((bf16[8,2,3,64,128]{4,3,2,1,0:T(8,128)(2,1)}), bf16[8,2,3,64,128]{4,3,2,1,0:T(8,128)(2,1)S(1)}, u32[]{:S(2)}, u32[]{:S(2)}) async-start(bf16[8,2,3,64,128]{4,3,2,1,0:T(8,128)(2,1)} %get-tuple-element.32), calls=%async_computation.1 | async-start | bytes 1572864 | tf_op jit(solution)/shard_map/all_to_all | solution.py:435
  54.2 20.6 %collective-permute-start.3 = (bf16[8,2,3,64,128]{4,3,2,1,0:T(8,128)(2,1)S(1)}, bf16[8,2,3,64,128]{4,3,2,1,0:T(8,128)(2,1)S(1)}, u32[]{:S(2)}, u32[]{:S(2)}) collective-permute-start(bf16[8,2,3,64,128]{4,3,2,1,0:T(8,128)(2,1)S(1)} %all_to_all.20.rest_0_), channel_id=1, source_target_pairs={{0,8},{8,0},{16,24},{24,16},{1,9},{9,1},{17,25},{25,17},{2,10},{10... | collective-permute-start | bytes 2359304 | tf_op jit(solution)/shard_map/ppermute | solution.py:387
  67.7 7.1 %collective-permute-start.5 = (bf16[8,2,3,64,128]{4,3,2,1,0:T(8,128)(2,1)S(1)}, bf16[8,2,3,64,128]{4,3,2,1,0:T(8,128)(2,1)}, u32[]{:S(2)}, u32[]{:S(2)}) collective-permute-start(bf16[8,2,3,64,128]{4,3,2,1,0:T(8,128)(2,1)S(1)} %collective-permute-done.4.rest_2_), channel_id=1, source_target_pairs={{0,8},{8,0},{16,24},{24,16},{1,9},{9,1},{17,25},{25,17},{2,10},{10... | collective-permute-start | bytes 2359304 | tf_op jit(solution)/shard_map/ppermute | solution.py:387
  74.2 20.8 %collective-permute-start.10 = (bf16[8,2,3,64,128]{4,3,2,1,0:T(8,128)(2,1)S(1)}, bf16[8,2,3,64,128]{4,3,2,1,0:T(8,128)(2,1)S(1)}, u32[]{:S(2)}, u32[]{:S(2)}) collective-permute-start(bf16[8,2,3,64,128]{4,3,2,1,0:T(8,128)(2,1)S(1)} %all-to-all-done.1.rest_0_), channel_id=1, source_target_pairs={{0,16},{8,24},{16,0},{24,8},{1,17},{9,25},{17,1},{25,9},{2,18},{10... | collective-permute-start | bytes 2359304 | tf_op jit(solution)/shard_map/ppermute | solution.py:387
  94.5 2.6 %collective-permute-start.7 = (bf16[8,2,3,64,128]{4,3,2,1,0:T(8,128)(2,1)}, bf16[8,2,3,64,128]{4,3,2,1,0:T(8,128)(2,1)S(1)}, u32[]{:S(2)}, u32[]{:S(2)}) collective-permute-start(bf16[8,2,3,64,128]{4,3,2,1,0:T(8,128)(2,1)} %get-tuple-element.37), channel_id=1, source_target_pairs={{0,8},{8,0},{16,24},{24,16},{1,9},{9,1},{17,25},{25,17},{2,10},{10... | collective-permute-start | bytes 2359304 | tf_op jit(solution)/shard_map/ppermute | solution.py:387
  94.6 5.5 %collective-permute-start.9 = (bf16[8,2,3,64,128]{4,3,2,1,0:T(8,128)(2,1)S(1)}, bf16[8,2,3,64,128]{4,3,2,1,0:T(8,128)(2,1)S(1)}, u32[]{:S(2)}, u32[]{:S(2)}) collective-permute-start(bf16[8,2,3,64,128]{4,3,2,1,0:T(8,128)(2,1)S(1)} %all-to-all-done.1.rest_0_), channel_id=1, source_target_pairs={{0,8},{8,0},{16,24},{24,16},{1,9},{9,1},{17,25},{25,17},{2,10},{10... | collective-permute-start | bytes 2359304 | tf_op jit(solution)/shard_map/ppermute | solution.py:387
  95.1 5.0 %collective-permute-start.11 = (bf16[8,2,3,64,128]{4,3,2,1,0:T(8,128)(2,1)S(1)}, bf16[8,2,3,64,128]{4,3,2,1,0:T(8,128)(2,1)S(1)}, u32[]{:S(2)}, u32[]{:S(2)}) collective-permute-start(bf16[8,2,3,64,128]{4,3,2,1,0:T(8,128)(2,1)S(1)} %collective-permute-done.10.rest_2_), channel_id=1, source_target_pairs={{0,8},{8,0},{16,24},{24,16},{1,9},{9,1},{17,25},{25,17},{2,10},{10... | collective-permute-start | bytes 2359304 | tf_op jit(solution)/shard_map/ppermute | solution.py:387
  95.2 25.6 %collective-permute-start.6 = (bf16[8,2,3,64,128]{4,3,2,1,0:T(8,128)(2,1)}, bf16[8,2,3,64,128]{4,3,2,1,0:T(8,128)(2,1)S(1)}, u32[]{:S(2)}, u32[]{:S(2)}) collective-permute-start(bf16[8,2,3,64,128]{4,3,2,1,0:T(8,128)(2,1)} %get-tuple-element.35), channel_id=1, source_target_pairs={{0,8},{8,0},{16,24},{24,16},{1,9},{9,1},{17,25},{25,17},{2,10},{10... | collective-permute-start | bytes 2359304 | tf_op jit(solution)/shard_map/ppermute | solution.py:387
  98.5 22.3 %copy-start.3 = (bf16[8,2,3,64,128]{4,3,2,1,0:T(8,128)(2,1)S(1)}, bf16[8,2,3,64,128]{4,3,2,1,0:T(8,128)(2,1)}, u32[]{:S(2)}) copy-start(bf16[8,2,3,64,128]{4,3,2,1,0:T(8,128)(2,1)} %get-tuple-element.34) | copy-start | bytes 2359300
  98.5 22.3 %collective-permute-start.8 = (bf16[8,2,3,64,128]{4,3,2,1,0:T(8,128)(2,1)S(1)}, bf16[8,2,3,64,128]{4,3,2,1,0:T(8,128)(2,1)S(1)}, u32[]{:S(2)}, u32[]{:S(2)}) collective-permute-start(bf16[8,2,3,64,128]{4,3,2,1,0:T(8,128)(2,1)S(1)} %add_convert_fusion.3), channel_id=1, source_target_pairs={{0,16},{8,24},{16,0},{24,8},{1,17},{9,25},{17,1},{25,9},{2,18},{10... | collective-permute-start | bytes 2359304 | tf_op jit(solution)/shard_map/ppermute | solution.py:387
  120.7 5.7 %collective-permute-start.13 = (bf16[8,2,3,64,128]{4,3,2,1,0:T(8,128)(2,1)}, bf16[8,2,3,64,128]{4,3,2,1,0:T(8,128)(2,1)S(1)}, u32[]{:S(2)}, u32[]{:S(2)}) collective-permute-start(bf16[8,2,3,64,128]{4,3,2,1,0:T(8,128)(2,1)} %get-tuple-element.41), channel_id=1, source_target_pairs={{0,8},{8,0},{16,24},{24,16},{1,9},{9,1},{17,25},{25,17},{2,10},{10... | collective-permute-start | bytes 2359304 | tf_op jit(solution)/shard_map/ppermute | solution.py:387
  122.1 24.7 %all-to-all-start.2 = ((bf16[8,2,3,64,128]{4,3,2,1,0:T(8,128)(2,1)}), bf16[8,2,3,64,128]{4,3,2,1,0:T(8,128)(2,1)S(1)}, u32[]{:S(2)}, u32[]{:S(2)}) async-start(bf16[8,2,3,64,128]{4,3,2,1,0:T(8,128)(2,1)} %add_convert_fusion.2), calls=%async_computation.2 | async-start | bytes 1572864 | tf_op jit(solution)/shard_map/all_to_all | solution.py:435
  125.8 20.4 %copy-start.4 = (bf16[8,2,3,64,128]{4,3,2,1,0:T(8,128)(2,1)S(1)}, bf16[8,2,3,64,128]{4,3,2,1,0:T(8,128)(2,1)}, u32[]{:S(2)}) copy-start(bf16[8,2,3,64,128]{4,3,2,1,0:T(8,128)(2,1)} %get-tuple-element.38) | copy-start | bytes 2359300
  125.8 2.5 %collective-permute-start.12 = (bf16[8,2,3,64,128]{4,3,2,1,0:T(8,128)(2,1)S(1)}, bf16[8,2,3,64,128]{4,3,2,1,0:T(8,128)(2,1)S(1)}, u32[]{:S(2)}, u32[]{:S(2)}) collective-permute-start(bf16[8,2,3,64,128]{4,3,2,1,0:T(8,128)(2,1)S(1)} %copy-done.7), channel_id=1, source_target_pairs={{0,8},{8,0},{16,24},{24,16},{1,9},{9,1},{17,25},{25,17},{2,10},{10... | collective-permute-start | bytes 2359304 | tf_op jit(solution)/shard_map/ppermute | solution.py:387
  126.7 19.5 %collective-permute-start.14 = (bf16[8,2,3,64,128]{4,3,2,1,0:T(8,128)(2,1)S(1)}, bf16[8,2,3,64,128]{4,3,2,1,0:T(8,128)(2,1)S(1)}, u32[]{:S(2)}, u32[]{:S(2)}) collective-permute-start(bf16[8,2,3,64,128]{4,3,2,1,0:T(8,128)(2,1)S(1)} %add_convert_fusion.1), channel_id=1, source_target_pairs={{0,16},{8,24},{16,0},{24,8},{1,17},{9,25},{17,1},{25,9},{2,18},{10... | collective-permute-start | bytes 2359304 | tf_op jit(solution)/shard_map/ppermute | solution.py:387
  146.8 25.5 %copy-start.1 = (bf16[8,2,3,64,128]{4,3,2,1,0:T(8,128)(2,1)}, bf16[8,2,3,64,128]{4,3,2,1,0:T(8,128)(2,1)S(1)}, u32[]{:S(2)}) copy-start(bf16[8,2,3,64,128]{4,3,2,1,0:T(8,128)(2,1)S(1)} %all-to-all-done.2.rest_0_) | copy-start | bytes 2359300
  176.6 1.9 collective-permute-start.15
  176.6 8.0 %collective-permute-start.16 = (bf16[4,3,64,128]{3,2,1,0:T(8,128)(2,1)}, bf16[4,3,64,128]{3,2,1,0:T(8,128)(2,1)S(1)}, u32[]{:S(2)}, u32[]{:S(2)}) collective-permute-start(bf16[4,3,64,128]{3,2,1,0:T(8,128)(2,1)} %get-tuple-element.45), channel_id=1, source_target_pairs={{0,16},{8,24},{16,0},{24,8},{1,17},{9,25},{17,1},{25,9},{2,18},{10... | collective-permute-start | bytes 589832 | tf_op jit(solution)/shard_map/ppermute | solution.py:387
  177.2 10.7 %collective-permute-start.17 = (bf16[4,3,64,128]{3,2,1,0:T(8,128)(2,1)}, bf16[4,3,64,128]{3,2,1,0:T(8,128)(2,1)S(1)}, u32[]{:S(2)}, u32[]{:S(2)}) collective-permute-start(bf16[4,3,64,128]{3,2,1,0:T(8,128)(2,1)} %get-tuple-element.46), channel_id=1, source_target_pairs={{0,24},{8,16},{16,8},{24,0},{1,25},{9,17},{17,9},{25,1},{2,26},{10... | collective-permute-start | bytes 589832 | tf_op jit(solution)/shard_map/ppermute | solution.py:387
  (14 other events, 70.3 us)

commit v4 on v3

--- a/solution.py
+++ b/solution.py
@@ -216,12 +216,16 @@
     copies.append(pltpu.make_async_copy(forward_hbm, forward, sems.at[groups]))
     copies.append(pltpu.make_async_copy(inverse_hbm, inverse, sems.at[groups + 1]))
     load = pltpu.make_async_copy(green_hbm.at[:, :, plane], green, sems.at[groups + 2])
-    load.start()
 
     @pl.when(g == 0)
     def _():
         for c in copies:
             c.start()
+
+    load.start()
+
+    @pl.when(g == 0)
+    def _():
         for c in copies[:groups]:
             c.wait()
 

time: 192 us -> 191 us (level)
  transfers between devices with their start and end apart: 20 -> 20, of which waited for: 10 -> 10; matrix products, arithmetic and copies ran while one was open for 2% -> 2% of each run, Pallas kernels for 20% -> 19%
where the time goes in v4:
time: 191 us; the launch traced here: 190 us
  waiting for transfers between devices  59.6 us (31%)
  Pallas kernels  52.5 us (27%)
  blocking collectives  51.9 us (27%)
  starting transfers between devices  18.3 us (10%)
  local copies, waits for them, and re-layouts  4.02 us (2%)
  other arithmetic  3.46 us (2%)
    ppermute x18, waiting for transfers between devices, send(): return lax.ppermute(value, axis, [(i, i ^ distance) for i in range(size)])  52.9 us
    pallas_call x6, Pallas kernels, call(): pl.pallas_call(kernel, grid=grid, in_specs=specs, out_specs=(out_spec if...  52.5 us
    all_to_all x2, blocking collectives, across(): return lax.all_to_all(value, 'xy', 0, 0, tiled=True)  51.9 us
    ppermute x18, starting transfers between devices, send(): return lax.ppermute(value, axis, [(i, i ^ distance) for i in range(size)])  10.9 us
    all_to_all x2, starting transfers between devices, across(): return lax.all_to_all(value, 'xy', 0, 0, tiled=True)  7.32 us
    all_to_all x2, waiting for transfers between devices, across(): return lax.all_to_all(value, 'xy', 0, 0, tiled=True)  6.68 us
    unnamed x36, local copies, waits for them, and re-layouts  4.02 us
  transfers between devices with their start and end apart: 20, of which 10 were waited for; matrix products, arithmetic and copies ran while one was open for 2% of the time, Pallas kernels for 19%

profile of v4, /device:TPU:0, one launch (start us, length us, event | category | flops | bytes accessed | tf_op | source)
XLA Modules:
  0.0 189.9 jit_solution(18187920339908634972)
XLA Ops:
  0.0 4.5 %moments.1 = (bf16[4,3,64,128]{3,2,1,0:T(8,128)(2,1)}, bf16[4,3,64,128]{3,2,1,0:T(8,128)(2,1)}, bf16[4,3,64,128]{3,2,1,0:T(8,128)(2,1)}, bf16[4,3,64,128]{3,2,1,0:T(8,128)(2,1)}) custom-call(f32[3,3,2,4]{3,2,1,0:T(2,128)} %bitcast.3, bf16[2,3,4,64,256]{4,3,2,1,0:T(8,128)(2,1)} %field_ref.3, s32[4,2,64]{2,1,0:T(2,128)} %bitcast.4, ...), custom_call_target="tpu_custom_call" | custom-call | flops 5000000000 | bytes 1048576 | tf_op jit(solution)/shard_map/moments/pallas_call | solution.py:355
  5.1 2.6 %collective-permute-start.1 = (bf16[4,3,64,128]{3,2,1,0:T(8,128)(2,1)}, bf16[4,3,64,128]{3,2,1,0:T(8,128)(2,1)S(1)}, u32[]{:S(2)}, u32[]{:S(2)}) collective-permute-start(bf16[4,3,64,128]{3,2,1,0:T(8,128)(2,1)} %get-tuple-element.28), channel_id=1, source_target_pairs={{0,16},{8,24},{16,0},{24,8},{1,17},{9,25},{17,1},{25,9},{2,18},{10... | collective-permute-start | bytes 589832 | tf_op jit(solution)/shard_map/ppermute | solution.py:391
  7.7 5.9 %collective-permute-done.1.rest_2_ = bf16[4,3,64,128]{3,2,1,0:T(8,128)(2,1)S(1)} collective-permute-done((bf16[4,3,64,128]{3,2,1,0:T(8,128)(2,1)}, bf16[4,3,64,128]{3,2,1,0:T(8,128)(2,1)S(1)}, u32[]{:S(2)}, u32[]{:S(2)}) %collective-permute-start.1) | collective-permute-done | bytes 196640 | tf_op jit(solution)/shard_map/ppermute | solution.py:391
  13.7 3.7 %collective-permute-done.2.rest_3_ = bf16[4,3,64,128]{3,2,1,0:T(8,128)(2,1)S(1)} collective-permute-done((bf16[4,3,64,128]{3,2,1,0:T(8,128)(2,1)}, bf16[4,3,64,128]{3,2,1,0:T(8,128)(2,1)S(1)}, u32[]{:S(2)}, u32[]{:S(2)}) %collective-permute-start.2) | collective-permute-done | bytes 196640 | tf_op jit(solution)/shard_map/ppermute | solution.py:391
  18.1 4.5 %forward_z.1 = (bf16[8,2,3,64,128]{4,3,2,1,0:T(8,128)(2,1)}, bf16[8,2,3,64,128]{4,3,2,1,0:T(8,128)(2,1)}) custom-call(bf16[4,3,64,128]{3,2,1,0:T(8,128)(2,1)} %get-tuple-element.26.rest_0_, bf16[4,3,64,128]{3,2,1,0:T(8,128)(2,1)} %copy-done.12, bf16[4,3,64,128]{3,2,1,0:T(8,128)(2,1)} %copy-done.14, bf16[4,3,64,128]{3,2,1,0:T(8,128)(2,1)} %copy-done.16), custom_call_target="tpu_custom_call" | custom-call | flops 4000000000 | bytes 1048576 | tf_op jit(solution)/shard_map/forward_z/pallas_call | solution.py:355
  22.6 26.4 %all_to_all.20.rest_0_ = bf16[8,2,3,64,128]{4,3,2,1,0:T(8,128)(2,1)S(1)} all-to-all(bf16[8,2,3,64,128]{4,3,2,1,0:T(8,128)(2,1)} %get-tuple-element.30), channel_id=1, replica_groups=mesh['zg'=4,'xy'=8] {'xy'}, dimensions={0} | all-to-all | bytes 1572864 | tf_op jit(solution)/shard_map/all_to_all | solution.py:439
  49.0 1.5 collective-permute-start.4
  50.5 3.6 %all-to-all-start.1 = ((bf16[8,2,3,64,128]{4,3,2,1,0:T(8,128)(2,1)}), bf16[8,2,3,64,128]{4,3,2,1,0:T(8,128)(2,1)S(1)}, u32[]{:S(2)}, u32[]{:S(2)}) async-start(bf16[8,2,3,64,128]{4,3,2,1,0:T(8,128)(2,1)} %get-tuple-element.32), calls=%async_computation.1 | async-start | bytes 1572864 | tf_op jit(solution)/shard_map/all_to_all | solution.py:439
  54.2 13.5 %collective-permute-done.4.rest_2_ = bf16[8,2,3,64,128]{4,3,2,1,0:T(8,128)(2,1)S(1)} collective-permute-done((bf16[8,2,3,64,128]{4,3,2,1,0:T(8,128)(2,1)S(1)}, bf16[8,2,3,64,128]{4,3,2,1,0:T(8,128)(2,1)S(1)}, u32[]{:S(2)}, u32[]{:S(2)}) %collective-permute-start.4) | collective-permute-done | bytes 786464 | tf_op jit(solution)/shard_map/ppermute | solution.py:391
  67.7 6.5 %all-to-all-done.1.rest_0_ = bf16[8,2,3,64,128]{4,3,2,1,0:T(8,128)(2,1)S(1)} async-done(((bf16[8,2,3,64,128]{4,3,2,1,0:T(8,128)(2,1)}), bf16[8,2,3,64,128]{4,3,2,1,0:T(8,128)(2,1)S(1)}, u32[]{:S(2)}, u32[]{:S(2)}) %all-to-all-start.1) | async-done | bytes 786464 | tf_op jit(solution)/shard_map/all_to_all | solution.py:439
  75.6 18.0 %middle.2 = (bf16[8,2,3,64,128]{4,3,2,1,0:T(8,128)(2,1)}, bf16[8,2,3,64,128]{4,3,2,1,0:T(8,128)(2,1)}, bf16[8,2,3,64,128]{4,3,2,1,0:T(8,128)(2,1)}, bf16[8,2,3,64,128]{4,3,2,1,0:T(8,128)(2,1)}) custom-call(f32[4,6]{1,0:T(4,128)} %bitcast.5, bf16[4,4,128,256]{3,2,1,0:T(8,128)(2,1)} %constant.8.clone.tabley_hbm, ...), custom_call_target="tpu_custom_call" | custom-call | flops 16000000000 | bytes 1048576 | tf_op jit(solution)/shard_map/middle/pallas_call | solution.py:355
  94.8 1.5 collective-permute-done.7
  96.2 1.4 add_convert_fusion.3
  97.7 1.6 collective-permute-start.8
  101.0 18.1 %middle.3 = (bf16[8,2,3,64,128]{4,3,2,1,0:T(8,128)(2,1)}, bf16[8,2,3,64,128]{4,3,2,1,0:T(8,128)(2,1)}, bf16[8,2,3,64,128]{4,3,2,1,0:T(8,128)(2,1)}, bf16[8,2,3,64,128]{4,3,2,1,0:T(8,128)(2,1)}) custom-call(f32[4,6]{1,0:T(4,128)} %bitcast.6, bf16[4,4,128,256]{3,2,1,0:T(8,128)(2,1)} %constant.8.clone.tabley_hbm, ...), custom_call_target="tpu_custom_call" | custom-call | flops 16000000000 | bytes 1048576 | tf_op jit(solution)/shard_map/middle/pallas_call | solution.py:355
  119.2 1.3 add_convert_fusion.2
  120.5 3.7 %all-to-all-start.2 = ((bf16[8,2,3,64,128]{4,3,2,1,0:T(8,128)(2,1)}), bf16[8,2,3,64,128]{4,3,2,1,0:T(8,128)(2,1)S(1)}, u32[]{:S(2)}, u32[]{:S(2)}) async-start(bf16[8,2,3,64,128]{4,3,2,1,0:T(8,128)(2,1)} %add_convert_fusion.2), calls=%async_computation.2 | async-start | bytes 1572864 | tf_op jit(solution)/shard_map/all_to_all | solution.py:439
  126.7 17.9 %collective-permute-done.14 = bf16[8,2,3,64,128]{4,3,2,1,0:T(8,128)(2,1)S(1)} collective-permute-done((bf16[8,2,3,64,128]{4,3,2,1,0:T(8,128)(2,1)S(1)}, bf16[8,2,3,64,128]{4,3,2,1,0:T(8,128)(2,1)S(1)}, u32[]{:S(2)}, u32[]{:S(2)}) %collective-permute-start.14) | collective-permute-done | bytes 786464 | tf_op jit(solution)/shard_map/ppermute | solution.py:391
  145.2 25.5 %all_to_all.21.rest_1_ = bf16[8,2,3,64,128]{4,3,2,1,0:T(8,128)(2,1)} all-to-all(bf16[8,2,3,64,128]{4,3,2,1,0:T(8,128)(2,1)S(1)} %add_convert_fusion), channel_id=1, replica_groups=mesh['zg'=4,'xy'=8] {'xy'}, dimensions={0} | all-to-all | bytes 1572864 | tf_op jit(solution)/shard_map/all_to_all | solution.py:439
  170.7 4.3 %inverse_z.1 = (bf16[4,3,64,128]{3,2,1,0:T(8,128)(2,1)}, bf16[4,3,64,128]{3,2,1,0:T(8,128)(2,1)}, bf16[4,3,64,128]{3,2,1,0:T(8,128)(2,1)}, bf16[4,3,64,128]{3,2,1,0:T(8,128)(2,1)}) custom-call(bf16[8,2,3,64,128]{4,3,2,1,0:T(8,128)(2,1)} %copy-done.1, bf16[8,2,3,64,128]{4,3,2,1,0:T(8,128)(2,1)} %all_to_all.21.rest_1_), custom_call_target="tpu_custom_call" | custom-call | flops 4000000000 | bytes 1048576 | tf_op jit(solution)/shard_map/inverse_z/pallas_call | solution.py:355
  175.6 1.3 collective-permute-start.17
  176.9 6.2 %collective-permute-done.16.rest_2_ = bf16[4,3,64,128]{3,2,1,0:T(8,128)(2,1)S(1)} collective-permute-done((bf16[4,3,64,128]{3,2,1,0:T(8,128)(2,1)}, bf16[4,3,64,128]{3,2,1,0:T(8,128)(2,1)S(1)}, u32[]{:S(2)}, u32[]{:S(2)}) %collective-permute-start.16) | collective-permute-done | bytes 196640 | tf_op jit(solution)/shard_map/ppermute | solution.py:391
  183.1 3.2 %collective-permute-done.17.rest_3_ = bf16[4,3,64,128]{3,2,1,0:T(8,128)(2,1)S(1)} collective-permute-done((bf16[4,3,64,128]{3,2,1,0:T(8,128)(2,1)}, bf16[4,3,64,128]{3,2,1,0:T(8,128)(2,1)S(1)}, u32[]{:S(2)}, u32[]{:S(2)}) %collective-permute-start.17) | collective-permute-done | bytes 196640 | tf_op jit(solution)/shard_map/ppermute | solution.py:391
  186.9 3.0 %result.1 = bf16[2,3,4,64,256]{4,3,2,1,0:T(8,128)(2,1)} custom-call(bf16[2,3,4,64,256]{4,3,2,1,0:T(8,128)(2,1)} %field_ref.3, bf16[64,64]{1,0:T(8,128)(2,1)} %constant.11.clone.order_ref, bf16[4,3,64,128]{3,2,1,0:T(8,128)(2,1)} %get-tuple-element.43.rest_0_, bf16[4,3,64,128]{3,2,1,0:T(8,128)(2,1)} %copy-done.13, bf16[4,3,64,128]{3,2,1,0:T(8,128)(2,1)} %copy-done.15, ...), custom_call_target="tpu_custom_call" | custom-call | flops 3000000000 | bytes 1048576 | tf_op jit(solution)/shard_map/result/pallas_call | solution.py:355
  (64 shorter events, 9.9 us)
Async XLA Ops:
  4.5 3.2 %collective-permute-start = (bf16[4,3,64,128]{3,2,1,0:T(8,128)(2,1)}, bf16[4,3,64,128]{3,2,1,0:T(8,128)(2,1)S(1)}, u32[]{:S(2)}, u32[]{:S(2)}) collective-permute-start(bf16[4,3,64,128]{3,2,1,0:T(8,128)(2,1)} %get-tuple-element.27), channel_id=1, source_target_pairs={{0,8},{8,0},{16,24},{24,16},{1,9},{9,1},{17,25},{25,17},{2,10},{10... | collective-permute-start | bytes 589832 | tf_op jit(solution)/shard_map/ppermute | solution.py:391
  5.1 8.5 %collective-permute-start.1 = (bf16[4,3,64,128]{3,2,1,0:T(8,128)(2,1)}, bf16[4,3,64,128]{3,2,1,0:T(8,128)(2,1)S(1)}, u32[]{:S(2)}, u32[]{:S(2)}) collective-permute-start(bf16[4,3,64,128]{3,2,1,0:T(8,128)(2,1)} %get-tuple-element.28), channel_id=1, source_target_pairs={{0,16},{8,24},{16,0},{24,8},{1,17},{9,25},{17,1},{25,9},{2,18},{10... | collective-permute-start | bytes 589832 | tf_op jit(solution)/shard_map/ppermute | solution.py:391
  7.7 9.7 %collective-permute-start.2 = (bf16[4,3,64,128]{3,2,1,0:T(8,128)(2,1)}, bf16[4,3,64,128]{3,2,1,0:T(8,128)(2,1)S(1)}, u32[]{:S(2)}, u32[]{:S(2)}) collective-permute-start(bf16[4,3,64,128]{3,2,1,0:T(8,128)(2,1)} %get-tuple-element.29), channel_id=1, source_target_pairs={{0,24},{8,16},{16,8},{24,0},{1,25},{9,17},{17,9},{25,1},{2,26},{10... | collective-permute-start | bytes 589832 | tf_op jit(solution)/shard_map/ppermute | solution.py:391
  49.0 25.7 %copy-start.2 = (bf16[8,2,3,64,128]{4,3,2,1,0:T(8,128)(2,1)}, bf16[8,2,3,64,128]{4,3,2,1,0:T(8,128)(2,1)S(1)}, u32[]{:S(2)}) copy-start(bf16[8,2,3,64,128]{4,3,2,1,0:T(8,128)(2,1)S(1)} %all_to_all.20.rest_0_) | copy-start | bytes 2359300
  49.0 18.7 %collective-permute-start.4 = (bf16[8,2,3,64,128]{4,3,2,1,0:T(8,128)(2,1)S(1)}, bf16[8,2,3,64,128]{4,3,2,1,0:T(8,128)(2,1)S(1)}, u32[]{:S(2)}, u32[]{:S(2)}) collective-permute-start(bf16[8,2,3,64,128]{4,3,2,1,0:T(8,128)(2,1)S(1)} %all_to_all.20.rest_0_), channel_id=1, source_target_pairs={{0,16},{8,24},{16,0},{24,8},{1,17},{9,25},{17,1},{25,9},{2,18},{10... | collective-permute-start | bytes 2359304 | tf_op jit(solution)/shard_map/ppermute | solution.py:391
  50.5 23.7 %all-to-all-start.1 = ((bf16[8,2,3,64,128]{4,3,2,1,0:T(8,128)(2,1)}), bf16[8,2,3,64,128]{4,3,2,1,0:T(8,128)(2,1)S(1)}, u32[]{:S(2)}, u32[]{:S(2)}) async-start(bf16[8,2,3,64,128]{4,3,2,1,0:T(8,128)(2,1)} %get-tuple-element.32), calls=%async_computation.1 | async-start | bytes 1572864 | tf_op jit(solution)/shard_map/all_to_all | solution.py:439
  54.2 20.6 %collective-permute-start.3 = (bf16[8,2,3,64,128]{4,3,2,1,0:T(8,128)(2,1)S(1)}, bf16[8,2,3,64,128]{4,3,2,1,0:T(8,128)(2,1)S(1)}, u32[]{:S(2)}, u32[]{:S(2)}) collective-permute-start(bf16[8,2,3,64,128]{4,3,2,1,0:T(8,128)(2,1)S(1)} %all_to_all.20.rest_0_), channel_id=1, source_target_pairs={{0,8},{8,0},{16,24},{24,16},{1,9},{9,1},{17,25},{25,17},{2,10},{10... | collective-permute-start | bytes 2359304 | tf_op jit(solution)/shard_map/ppermute | solution.py:391
  67.7 7.1 %collective-permute-start.5 = (bf16[8,2,3,64,128]{4,3,2,1,0:T(8,128)(2,1)S(1)}, bf16[8,2,3,64,128]{4,3,2,1,0:T(8,128)(2,1)}, u32[]{:S(2)}, u32[]{:S(2)}) collective-permute-start(bf16[8,2,3,64,128]{4,3,2,1,0:T(8,128)(2,1)S(1)} %collective-permute-done.4.rest_2_), channel_id=1, source_target_pairs={{0,8},{8,0},{16,24},{24,16},{1,9},{9,1},{17,25},{25,17},{2,10},{10... | collective-permute-start | bytes 2359304 | tf_op jit(solution)/shard_map/ppermute | solution.py:391
  74.2 20.0 %collective-permute-start.10 = (bf16[8,2,3,64,128]{4,3,2,1,0:T(8,128)(2,1)S(1)}, bf16[8,2,3,64,128]{4,3,2,1,0:T(8,128)(2,1)S(1)}, u32[]{:S(2)}, u32[]{:S(2)}) collective-permute-start(bf16[8,2,3,64,128]{4,3,2,1,0:T(8,128)(2,1)S(1)} %all-to-all-done.1.rest_0_), channel_id=1, source_target_pairs={{0,16},{8,24},{16,0},{24,8},{1,17},{9,25},{17,1},{25,9},{2,18},{10... | collective-permute-start | bytes 2359304 | tf_op jit(solution)/shard_map/ppermute | solution.py:391
  93.7 2.6 %collective-permute-start.7 = (bf16[8,2,3,64,128]{4,3,2,1,0:T(8,128)(2,1)}, bf16[8,2,3,64,128]{4,3,2,1,0:T(8,128)(2,1)S(1)}, u32[]{:S(2)}, u32[]{:S(2)}) collective-permute-start(bf16[8,2,3,64,128]{4,3,2,1,0:T(8,128)(2,1)} %get-tuple-element.37), channel_id=1, source_target_pairs={{0,8},{8,0},{16,24},{24,16},{1,9},{9,1},{17,25},{25,17},{2,10},{10... | collective-permute-start | bytes 2359304 | tf_op jit(solution)/shard_map/ppermute | solution.py:391
  93.8 5.5 %collective-permute-start.9 = (bf16[8,2,3,64,128]{4,3,2,1,0:T(8,128)(2,1)S(1)}, bf16[8,2,3,64,128]{4,3,2,1,0:T(8,128)(2,1)S(1)}, u32[]{:S(2)}, u32[]{:S(2)}) collective-permute-start(bf16[8,2,3,64,128]{4,3,2,1,0:T(8,128)(2,1)S(1)} %all-to-all-done.1.rest_0_), channel_id=1, source_target_pairs={{0,8},{8,0},{16,24},{24,16},{1,9},{9,1},{17,25},{25,17},{2,10},{10... | collective-permute-start | bytes 2359304 | tf_op jit(solution)/shard_map/ppermute | solution.py:391
  94.3 5.0 %collective-permute-start.11 = (bf16[8,2,3,64,128]{4,3,2,1,0:T(8,128)(2,1)S(1)}, bf16[8,2,3,64,128]{4,3,2,1,0:T(8,128)(2,1)S(1)}, u32[]{:S(2)}, u32[]{:S(2)}) collective-permute-start(bf16[8,2,3,64,128]{4,3,2,1,0:T(8,128)(2,1)S(1)} %collective-permute-done.10.rest_2_), channel_id=1, source_target_pairs={{0,8},{8,0},{16,24},{24,16},{1,9},{9,1},{17,25},{25,17},{2,10},{10... | collective-permute-start | bytes 2359304 | tf_op jit(solution)/shard_map/ppermute | solution.py:391
  94.3 24.8 %collective-permute-start.6 = (bf16[8,2,3,64,128]{4,3,2,1,0:T(8,128)(2,1)}, bf16[8,2,3,64,128]{4,3,2,1,0:T(8,128)(2,1)S(1)}, u32[]{:S(2)}, u32[]{:S(2)}) collective-permute-start(bf16[8,2,3,64,128]{4,3,2,1,0:T(8,128)(2,1)} %get-tuple-element.35), channel_id=1, source_target_pairs={{0,8},{8,0},{16,24},{24,16},{1,9},{9,1},{17,25},{25,17},{2,10},{10... | collective-permute-start | bytes 2359304 | tf_op jit(solution)/shard_map/ppermute | solution.py:391
  97.7 21.5 %copy-start.3 = (bf16[8,2,3,64,128]{4,3,2,1,0:T(8,128)(2,1)S(1)}, bf16[8,2,3,64,128]{4,3,2,1,0:T(8,128)(2,1)}, u32[]{:S(2)}) copy-start(bf16[8,2,3,64,128]{4,3,2,1,0:T(8,128)(2,1)} %get-tuple-element.34) | copy-start | bytes 2359300
  97.7 21.5 %collective-permute-start.8 = (bf16[8,2,3,64,128]{4,3,2,1,0:T(8,128)(2,1)S(1)}, bf16[8,2,3,64,128]{4,3,2,1,0:T(8,128)(2,1)S(1)}, u32[]{:S(2)}, u32[]{:S(2)}) collective-permute-start(bf16[8,2,3,64,128]{4,3,2,1,0:T(8,128)(2,1)S(1)} %add_convert_fusion.3), channel_id=1, source_target_pairs={{0,16},{8,24},{16,0},{24,8},{1,17},{9,25},{17,1},{25,9},{2,18},{10... | collective-permute-start | bytes 2359304 | tf_op jit(solution)/shard_map/ppermute | solution.py:391
  119.1 5.7 %collective-permute-start.13 = (bf16[8,2,3,64,128]{4,3,2,1,0:T(8,128)(2,1)}, bf16[8,2,3,64,128]{4,3,2,1,0:T(8,128)(2,1)S(1)}, u32[]{:S(2)}, u32[]{:S(2)}) collective-permute-start(bf16[8,2,3,64,128]{4,3,2,1,0:T(8,128)(2,1)} %get-tuple-element.41), channel_id=1, source_target_pairs={{0,8},{8,0},{16,24},{24,16},{1,9},{9,1},{17,25},{25,17},{2,10},{10... | collective-permute-start | bytes 2359304 | tf_op jit(solution)/shard_map/ppermute | solution.py:391
  120.5 24.7 %all-to-all-start.2 = ((bf16[8,2,3,64,128]{4,3,2,1,0:T(8,128)(2,1)}), bf16[8,2,3,64,128]{4,3,2,1,0:T(8,128)(2,1)S(1)}, u32[]{:S(2)}, u32[]{:S(2)}) async-start(bf16[8,2,3,64,128]{4,3,2,1,0:T(8,128)(2,1)} %add_convert_fusion.2), calls=%async_computation.2 | async-start | bytes 1572864 | tf_op jit(solution)/shard_map/all_to_all | solution.py:439
  124.2 20.4 %copy-start.4 = (bf16[8,2,3,64,128]{4,3,2,1,0:T(8,128)(2,1)S(1)}, bf16[8,2,3,64,128]{4,3,2,1,0:T(8,128)(2,1)}, u32[]{:S(2)}) copy-start(bf16[8,2,3,64,128]{4,3,2,1,0:T(8,128)(2,1)} %get-tuple-element.38) | copy-start | bytes 2359300
  124.2 2.5 %collective-permute-start.12 = (bf16[8,2,3,64,128]{4,3,2,1,0:T(8,128)(2,1)S(1)}, bf16[8,2,3,64,128]{4,3,2,1,0:T(8,128)(2,1)S(1)}, u32[]{:S(2)}, u32[]{:S(2)}) collective-permute-start(bf16[8,2,3,64,128]{4,3,2,1,0:T(8,128)(2,1)S(1)} %copy-done.7), channel_id=1, source_target_pairs={{0,8},{8,0},{16,24},{24,16},{1,9},{9,1},{17,25},{25,17},{2,10},{10... | collective-permute-start | bytes 2359304 | tf_op jit(solution)/shard_map/ppermute | solution.py:391
  125.1 19.5 %collective-permute-start.14 = (bf16[8,2,3,64,128]{4,3,2,1,0:T(8,128)(2,1)S(1)}, bf16[8,2,3,64,128]{4,3,2,1,0:T(8,128)(2,1)S(1)}, u32[]{:S(2)}, u32[]{:S(2)}) collective-permute-start(bf16[8,2,3,64,128]{4,3,2,1,0:T(8,128)(2,1)S(1)} %add_convert_fusion.1), channel_id=1, source_target_pairs={{0,16},{8,24},{16,0},{24,8},{1,17},{9,25},{17,1},{25,9},{2,18},{10... | collective-permute-start | bytes 2359304 | tf_op jit(solution)/shard_map/ppermute | solution.py:391
  145.2 25.5 %copy-start.1 = (bf16[8,2,3,64,128]{4,3,2,1,0:T(8,128)(2,1)}, bf16[8,2,3,64,128]{4,3,2,1,0:T(8,128)(2,1)S(1)}, u32[]{:S(2)}) copy-start(bf16[8,2,3,64,128]{4,3,2,1,0:T(8,128)(2,1)S(1)} %all-to-all-done.2.rest_0_) | copy-start | bytes 2359300
  175.0 1.9 collective-permute-start.15
  175.0 8.0 %collective-permute-start.16 = (bf16[4,3,64,128]{3,2,1,0:T(8,128)(2,1)}, bf16[4,3,64,128]{3,2,1,0:T(8,128)(2,1)S(1)}, u32[]{:S(2)}, u32[]{:S(2)}) collective-permute-start(bf16[4,3,64,128]{3,2,1,0:T(8,128)(2,1)} %get-tuple-element.45), channel_id=1, source_target_pairs={{0,16},{8,24},{16,0},{24,8},{1,17},{9,25},{17,1},{25,9},{2,18},{10... | collective-permute-start | bytes 589832 | tf_op jit(solution)/shard_map/ppermute | solution.py:391
  175.6 10.6 %collective-permute-start.17 = (bf16[4,3,64,128]{3,2,1,0:T(8,128)(2,1)}, bf16[4,3,64,128]{3,2,1,0:T(8,128)(2,1)S(1)}, u32[]{:S(2)}, u32[]{:S(2)}) collective-permute-start(bf16[4,3,64,128]{3,2,1,0:T(8,128)(2,1)} %get-tuple-element.46), channel_id=1, source_target_pairs={{0,24},{8,16},{16,8},{24,0},{1,25},{9,17},{17,9},{25,1},{2,26},{10... | collective-permute-start | bytes 589832 | tf_op jit(solution)/shard_map/ppermute | solution.py:391
  (14 other events, 69.4 us)
